TPU v7x, 32 devices: a whole 2x2x4 slice. The times are simulated.
32 devices in a mesh: gx: 4 (over z), gy: 4 (over x, core), gz: 2 (over y).
Axes of the slice: x: 2, y: 2, z: 4, core: 2. Of those that a mesh axis runs over, the one named last changes fastest.
Arguments:
- hidden_in: bfloat16 [2048, 4096], P(('gx', 'gy'), 'gz'), may hold values from -40 to 40
- norm_gain: float32 [4096], P('gz'), may hold values from 0.25 to 1.75
- normed_grad: bfloat16 [2048, 4096], P(('gx', 'gy'), 'gz'), may hold values from -64 to 64
- key_grad: bfloat16 [2048, 512], P(('gx', 'gy')), may hold values from -6 to 6
- weight_blocks: bfloat16 [16, 2, 520, 128], P(('gx', 'gy'), 'gz'), may hold values from -0.09375 to 0.09375
- block_count: int32 [2, 16], P('gz'), may hold values from 1 to 520, as said below
Outputs:
- hidden_grad: bfloat16 [2048, 4096], P(('gx', 'gy'), 'gz')
- weight_grad: float32 [16, 2, 520, 128], P(('gx', 'gy'), 'gz')
Inputs may be any that keep to these rules, and one draw needn't show every extreme that they name: `block_count`: each row sums to 8192; in each row the owners i * 4 to i * 4 + 3 hold together exactly the blocks i * 2048 to min((i + 1) * 2048, 8192) - 1, and one of them holds exactly 520 blocks.
All inputs are finite; a program needn't handle non-finite values.
Results may differ from a plain program's by a relative error of at most 0.0029.
Values may be sent and summed in bfloat16 or wider, within the bound.
No kernel may reach another device: no remote copies, remote signals or barrier semaphores. Data moves between devices by JAX's collectives and lax.ppermute only.
A program may use at most 64 MiB of HBM per device.

v0:
```python
import jax
import jax.numpy as jnp
from jax import lax
from jax.sharding import PartitionSpec as P

EPS = 1e-06


def block_layout(counts, blocks, owners, most):
    ends = jnp.cumsum(counts)
    starts = ends - counts
    block_ids = jnp.arange(blocks, dtype=jnp.int32)
    owner = jnp.searchsorted(ends, block_ids, side="right")
    gather_index = owner * most + block_ids - starts[owner]
    slot_owner = jnp.arange(owners * most, dtype=jnp.int32) // most
    slot_within = jnp.arange(owners * most, dtype=jnp.int32) % most
    valid = slot_within < counts[slot_owner]
    source = jnp.clip(starts[slot_owner] + slot_within, 0, blocks - 1)
    return (gather_index, source, valid)


def select_rows(index, keep, rows):
    columns = jnp.arange(rows.shape[0], dtype=jnp.int32)
    onehot = (index[:, None] == columns[None, :]) & keep[:, None]
    if rows.dtype == jnp.bfloat16:
        picked = jnp.dot(onehot.astype(jnp.bfloat16), rows, preferred_element_type=jnp.float32)
        return picked.astype(jnp.bfloat16)
    return jnp.dot(
        onehot.astype(jnp.float32),
        rows,
        precision=lax.Precision.HIGHEST,
        preferred_element_type=jnp.float32,
    )


def select_groups(index, keep, rows):

    def one_group(items):
        return select_rows(items[0], items[1], items[2])

    return lax.map(one_group, (index, keep, rows))


def shards(hidden_in, norm_gain, normed_grad, key_grad, weight_blocks, block_count):
    outer_size = lax.axis_size("gx")
    inner_size = lax.axis_size("gy")
    owners = outer_size * inner_size
    most = weight_blocks.shape[2]
    group_slots_count = inner_size * most
    group_rows = hidden_in.shape[1]
    width = key_grad.shape[1]
    blocks = group_rows * width // 128
    group_blocks = (blocks + outer_size - 1) // outer_size
    model_width = group_rows * lax.axis_size("gz")
    gather_index, source, valid = block_layout(block_count[0], blocks, owners, most)
    outer_index = lax.axis_index("gx")
    padded_index = jnp.pad(gather_index, (0, outer_size * group_blocks - blocks), mode="edge")
    group_offsets = jnp.arange(outer_size, dtype=jnp.int32)[:, None]
    local_index = jnp.clip(
        padded_index.reshape(outer_size, group_blocks) - group_offsets * group_slots_count,
        0,
        group_slots_count - 1,
    )
    local_source = jnp.clip(
        source.reshape(outer_size, group_slots_count) - group_offsets * group_blocks,
        0,
        group_blocks - 1,
    )
    local_valid = valid.reshape(outer_size, group_slots_count)
    all_rows = jnp.ones((outer_size, group_blocks), dtype=bool)
    local_blocks = weight_blocks.reshape(most, 128)
    gathered = lax.all_gather(local_blocks, ("gx", "gy"), axis=0, tiled=True)
    dense = select_groups(
        local_index, all_rows, gathered.reshape(outer_size, group_slots_count, 128)
    )
    weight = dense.reshape(outer_size * group_blocks, 128)[:blocks].reshape(group_rows, width)
    hfloat = hidden_in.astype(jnp.float32)
    squares = lax.psum(jnp.sum(hfloat * hfloat, axis=1), "gz")
    rstd = lax.rsqrt(squares / model_width + EPS)
    normed = (hfloat * rstd[:, None] * norm_gain).astype(jnp.bfloat16)
    dnorm = normed_grad.astype(jnp.float32) + lax.dot_general(
        key_grad, weight, (((1,), (1,)), ((), ())), preferred_element_type=jnp.float32
    )
    proj = lax.psum(jnp.sum(norm_gain * dnorm * hfloat, axis=1), "gz")
    grad = norm_gain * dnorm * rstd[:, None] - hfloat * (rstd**3 * proj / model_width)[:, None]
    hidden_grad = grad.astype(jnp.bfloat16)
    dweight = lax.dot_general(
        normed, key_grad, (((0,), (0,)), ((), ())), preferred_element_type=jnp.float32
    )
    flat = dweight.reshape(blocks, 128)
    flat_padded = jnp.pad(flat, ((0, outer_size * group_blocks - blocks), (0, 0)))
    group_sum = lax.psum_scatter(flat_padded, "gx", scatter_dimension=0, tiled=True)
    slot_source = lax.dynamic_index_in_dim(local_source, outer_index, 0, keepdims=False)
    slot_valid = lax.dynamic_index_in_dim(local_valid, outer_index, 0, keepdims=False)
    slotted = select_rows(slot_source, slot_valid, group_sum)
    owned = lax.psum_scatter(slotted, "gy", scatter_dimension=0, tiled=True)
    return (hidden_grad, owned.reshape(1, 1, most, 128))


def solution(mesh):
    placed = (
        P(("gx", "gy"), "gz"),
        P("gz"),
        P(("gx", "gy"), "gz"),
        P(("gx", "gy"), None),
        P(("gx", "gy"), "gz", None, None),
        P("gz", None),
    )
    return jax.shard_map(
        shards,
        mesh=mesh,
        in_specs=placed,
        out_specs=(P(("gx", "gy"), "gz"), P(("gx", "gy"), "gz", None, None)),
        check_vma=False,
    )
```

profile of v0, /device:TPU:0, one launch (start us, length us, event | category | flops | bytes accessed | tf_op | source)
XLA Modules:
  0.0 235.7 jit_solution(7891955440732720645)
XLA Ops:
  11.6 53.5 %while.35 = (s32[]{:T(128)}, u32[8192]{0:T(1024)S(1)}, u32[8192]{0:T(1024)S(1)}, s32[16]{0:T(128)S(1)}, s32[]{:T(128)}, /*index=5*/s32[]{:T(128)}) while((s32[]{:T(128)}, u32[8192]{0:T(1024)S(1)}, u32[8192]{0:T(1024)S(1)}, s32[16]{0:T(128)S(1)}, s32[]{:T(128)}, /*index=5*/s32[]{:T(128)}) %tuple.103), condition=%wide.region_2.3_spmd.clone, body=%wide.region_1.2_spmd.clone.sunk | while | flops 311299 | bytes 131351 | solution.py:13
  12.3 10.0 %fusion.53 = (u32[8192]{0:T(1024)S(1)}, u32[8192]{0:T(1024)S(1)}) fusion(u32[8192]{0:T(1024)S(1)} %get-tuple-element.281, u32[8192]{0:T(1024)S(1)} %get-tuple-element.280, s32[]{:T(128)} %bitcast.94, s32[]{:T(128)} %bitcast.95, s32[]{:T(128)} %bitcast.96, s32[]{:T(128)} %bitcast.97, s32[]{:T(128)} %bitcast.98, s32[]{:T(128)} %bitcast.99, ...), kind=kLoop, calls=%fused_computation.12.clone.1 | loop fusion | flops 311296 | bytes 131137 | tf_op jit(solution)/shard_map/jit(searchsorted)/jit(_searchsorted_scan_impl)/vmap(jit(_searchsorted_scan_impl))/while/body/eval_jaxpr/select_n | solution.py:13
  23.0 10.0 %fusion.53 = (u32[8192]{0:T(1024)S(1)}, u32[8192]{0:T(1024)S(1)}) fusion(u32[8192]{0:T(1024)S(1)} %get-tuple-element.281, u32[8192]{0:T(1024)S(1)} %get-tuple-element.280, s32[]{:T(128)} %bitcast.94, s32[]{:T(128)} %bitcast.95, s32[]{:T(128)} %bitcast.96, s32[]{:T(128)} %bitcast.97, s32[]{:T(128)} %bitcast.98, s32[]{:T(128)} %bitcast.99, ...), kind=kLoop, calls=%fused_computation.12.clone.1 | loop fusion | flops 311296 | bytes 131137 | tf_op jit(solution)/shard_map/jit(searchsorted)/jit(_searchsorted_scan_impl)/vmap(jit(_searchsorted_scan_impl))/while/body/eval_jaxpr/select_n | solution.py:13
  33.7 10.0 %fusion.53 = (u32[8192]{0:T(1024)S(1)}, u32[8192]{0:T(1024)S(1)}) fusion(u32[8192]{0:T(1024)S(1)} %get-tuple-element.281, u32[8192]{0:T(1024)S(1)} %get-tuple-element.280, s32[]{:T(128)} %bitcast.94, s32[]{:T(128)} %bitcast.95, s32[]{:T(128)} %bitcast.96, s32[]{:T(128)} %bitcast.97, s32[]{:T(128)} %bitcast.98, s32[]{:T(128)} %bitcast.99, ...), kind=kLoop, calls=%fused_computation.12.clone.1 | loop fusion | flops 311296 | bytes 131137 | tf_op jit(solution)/shard_map/jit(searchsorted)/jit(_searchsorted_scan_impl)/vmap(jit(_searchsorted_scan_impl))/while/body/eval_jaxpr/select_n | solution.py:13
  44.4 10.0 %fusion.53 = (u32[8192]{0:T(1024)S(1)}, u32[8192]{0:T(1024)S(1)}) fusion(u32[8192]{0:T(1024)S(1)} %get-tuple-element.281, u32[8192]{0:T(1024)S(1)} %get-tuple-element.280, s32[]{:T(128)} %bitcast.94, s32[]{:T(128)} %bitcast.95, s32[]{:T(128)} %bitcast.96, s32[]{:T(128)} %bitcast.97, s32[]{:T(128)} %bitcast.98, s32[]{:T(128)} %bitcast.99, ...), kind=kLoop, calls=%fused_computation.12.clone.1 | loop fusion | flops 311296 | bytes 131137 | tf_op jit(solution)/shard_map/jit(searchsorted)/jit(_searchsorted_scan_impl)/vmap(jit(_searchsorted_scan_impl))/while/body/eval_jaxpr/select_n | solution.py:13
  55.1 10.0 %fusion.53 = (u32[8192]{0:T(1024)S(1)}, u32[8192]{0:T(1024)S(1)}) fusion(u32[8192]{0:T(1024)S(1)} %get-tuple-element.281, u32[8192]{0:T(1024)S(1)} %get-tuple-element.280, s32[]{:T(128)} %bitcast.94, s32[]{:T(128)} %bitcast.95, s32[]{:T(128)} %bitcast.96, s32[]{:T(128)} %bitcast.97, s32[]{:T(128)} %bitcast.98, s32[]{:T(128)} %bitcast.99, ...), kind=kLoop, calls=%fused_computation.12.clone.1 | loop fusion | flops 311296 | bytes 131137 | tf_op jit(solution)/shard_map/jit(searchsorted)/jit(_searchsorted_scan_impl)/vmap(jit(_searchsorted_scan_impl))/while/body/eval_jaxpr/select_n | solution.py:13
  65.1 10.2 %select_subtract_fusion = s32[8192]{0:T(1024)S(1)} fusion(u32[8192]{0:T(1024)S(1)} %get-tuple-element.89, s32[]{:T(128)} %bitcast.5, s32[]{:T(128)} %bitcast.6, s32[]{:T(128)} %bitcast.7, s32[]{:T(128)} %bitcast.8, s32[]{:T(128)} %bitcast.9, s32[]{:T(128)} %bitcast.10, s32[]{:T(128)} %bitcast.11, s32[]{:T(128)} %bitcast.12, s32[]{:T(128)} %bitcast.13, ...), kind=kLoop, calls=%fused_computation.74 | loop fusion | flops 303104 | bytes 65600 | tf_op jit(solution)/shard_map/sub | solution.py:14
  75.7 20.5 %while.34 = (s32[]{:T(128)}, bf16[4,2048,128]{2,1,0:T(8,128)(2,1)}, s32[4,2048]{1,0:T(4,128)S(1)}, bf16[4,2080,128]{2,1,0:T(8,128)(2,1)}, s32[]{:T(128)}) while((s32[]{:T(128)}, bf16[4,2048,128]{2,1,0:T(8,128)(2,1)}, s32[4,2048]{1,0:T(4,128)S(1)}, bf16[4,2080,128]{2,1,0:T(8,128)(2,1)}, s32[]{:T(128)}) %tuple.115), condition=%wide.region_4.5_spmd, body=%wide.region_3.4_spmd.sunk | while | flops 1095041024 | bytes 1082441 | solution.py:41
  75.8 5.1 %fusion.51 = bf16[4,2048,128]{2,1,0:T(8,128)(2,1)} fusion(bf16[4,2048,128]{2,1,0:T(8,128)(2,1)} %get-tuple-element.297, s32[]{:T(128)S(6)} %copy.32, s32[2048]{0:T(1024)S(1)} %bitcast.110, bf16[4,2080,128]{2,1,0:T(8,128)(2,1)} %get-tuple-element.304), kind=kOutput, calls=%fused_computation.6.clone.1 | convolution fusion | flops 1095041024 | bytes 1065984 | tf_op jit(solution)/shard_map/while/body/eval_jaxpr/dot_general | solution.py:26
  80.9 5.1 %fusion.51 = bf16[4,2048,128]{2,1,0:T(8,128)(2,1)} fusion(bf16[4,2048,128]{2,1,0:T(8,128)(2,1)} %get-tuple-element.297, s32[]{:T(128)S(6)} %copy.32, s32[2048]{0:T(1024)S(1)} %bitcast.110, bf16[4,2080,128]{2,1,0:T(8,128)(2,1)} %get-tuple-element.304), kind=kOutput, calls=%fused_computation.6.clone.1 | convolution fusion | flops 1095041024 | bytes 1065984 | tf_op jit(solution)/shard_map/while/body/eval_jaxpr/dot_general | solution.py:26
  86.0 5.1 %fusion.51 = bf16[4,2048,128]{2,1,0:T(8,128)(2,1)} fusion(bf16[4,2048,128]{2,1,0:T(8,128)(2,1)} %get-tuple-element.297, s32[]{:T(128)S(6)} %copy.32, s32[2048]{0:T(1024)S(1)} %bitcast.110, bf16[4,2080,128]{2,1,0:T(8,128)(2,1)} %get-tuple-element.304), kind=kOutput, calls=%fused_computation.6.clone.1 | convolution fusion | flops 1095041024 | bytes 1065984 | tf_op jit(solution)/shard_map/while/body/eval_jaxpr/dot_general | solution.py:26
  91.1 5.1 %fusion.51 = bf16[4,2048,128]{2,1,0:T(8,128)(2,1)} fusion(bf16[4,2048,128]{2,1,0:T(8,128)(2,1)} %get-tuple-element.297, s32[]{:T(128)S(6)} %copy.32, s32[2048]{0:T(1024)S(1)} %bitcast.110, bf16[4,2080,128]{2,1,0:T(8,128)(2,1)} %get-tuple-element.304), kind=kOutput, calls=%fused_computation.6.clone.1 | convolution fusion | flops 1095041024 | bytes 1065984 | tf_op jit(solution)/shard_map/while/body/eval_jaxpr/dot_general | solution.py:26
  96.2 3.1 %reshape_reshape.3 = bf16[2048,512]{1,0:T(8,128)(2,1)S(1)} reshape(bf16[4,2048,128]{2,1,0:T(8,128)(2,1)} %get-tuple-element.90) | data formatting | bytes 4194304 | tf_op jit(solution)/shard_map/reshape;reshape | solution.py:76
  99.3 1.8 fusion.19
  101.1 5.9 %all-reduce.1 = (f32[128]{0:T(128)S(1)}, f32[128]{0:T(128)S(1)}) all-reduce(f32[128]{0:T(128)S(1)} %get-tuple-element.115, f32[128]{0:T(128)S(1)} %get-tuple-element.114), channel_id=1, replica_groups=mesh['gx'=4,'gy'=4,'gz'=2] {'gz'}, use_global_device_ids=true, to_apply=%region_8.9 | all-reduce | flops 256 | bytes 2048 | tf_op jit(solution)/shard_map/psum | solution.py:84
  107.0 2.7 %fusion.25 = f32[2048,512]{1,0:T(8,128)} fusion(bf16[128,512]{1,0:T(8,128)(2,1)S(1)} %copy-done, bf16[128,2048]{0,1:T(8,128)(2,1)S(1)} %copy.18, f32[128]{0:T(128)S(1)} %get-tuple-element.168, f32[2048]{0:T(1024)S(1)} %copy-done.4), kind=kOutput, calls=%fused_computation.34 | convolution fusion | flops 269484032 | bytes 4858368 | tf_op jit(solution)/shard_map/dot_general | solution.py:87
  109.7 4.7 %reshape.119 = f32[8192,128]{1,0:T(8,128)} reshape(f32[2048,512]{1,0:T(8,128)} %fusion.25) | data formatting | bytes 8388608 | tf_op jit(solution)/shard_map/reshape | solution.py:90
  116.4 4.7 %fusion.33 = s32[8320]{0:T(1024)S(1)} fusion(s32[]{:T(128)} %bitcast.14, s32[]{:T(128)} %bitcast.15, s32[]{:T(128)} %bitcast.16, s32[]{:T(128)} %bitcast.17, s32[]{:T(128)} %bitcast.18, s32[]{:T(128)} %bitcast.20, s32[]{:T(128)} %bitcast.19), kind=kLoop, calls=%fused_computation.73 | loop fusion | flops 191360 | bytes 33308 | tf_op jit(solution)/shard_map/gather | solution.py:18
  121.1 5.7 %select_select_fusion.2 = s32[8320]{0:T(1024)S(1)} fusion(pred[8320]{0:T(1024)(128)(4,1)S(1)} %compare_reduce_fusion, pred[8320]{0:T(1024)(128)(4,1)S(1)} %compare_reduce_fusion.1, pred[8320]{0:T(1024)(128)(4,1)S(1)} %compare_reduce_fusion.2, pred[8320]{0:T(1024)(128)(4,1)S(1)} %compare_reduce_fusion.3, pred[8320]{0:T(1024)(128)(4,1)S(1)} %compare_reduce_fusion.4, ...), kind=kLoop, calls=%fused_computation.66 | loop fusion | flops 74880 | bytes 141476 | tf_op jit(solution)/shard_map/gather | solution.py:18
  127.6 4.6 %fusion.32 = s32[8320]{0:T(1024)S(1)} fusion(s32[]{:T(128)} %bitcast.32, s32[]{:T(128)} %bitcast.33, s32[]{:T(128)} %bitcast.34, s32[]{:T(128)} %bitcast.35, s32[]{:T(128)} %bitcast.36, s32[]{:T(128)} %bitcast.38, s32[]{:T(128)} %bitcast.37), kind=kLoop, calls=%fused_computation.72 | loop fusion | flops 191360 | bytes 33308 | tf_op jit(solution)/shard_map/gather | solution.py:17
  132.3 5.7 %select_select_fusion.1 = s32[8320]{0:T(1024)S(1)} fusion(pred[8320]{0:T(1024)(128)(4,1)S(1)} %compare_reduce_fusion, pred[8320]{0:T(1024)(128)(4,1)S(1)} %compare_reduce_fusion.1, pred[8320]{0:T(1024)(128)(4,1)S(1)} %compare_reduce_fusion.2, pred[8320]{0:T(1024)(128)(4,1)S(1)} %compare_reduce_fusion.3, pred[8320]{0:T(1024)(128)(4,1)S(1)} %compare_reduce_fusion.4, ...), kind=kLoop, calls=%fused_computation.65 | loop fusion | flops 74880 | bytes 141476 | tf_op jit(solution)/shard_map/gather | solution.py:17
  139.5 53.7 %reduce-scatter.5.cloned.1.call-done = f32[2048,128]{1,0:T(8,128)} async-done(((f32[8192,128]{1,0:T(8,128)}), f32[2048,128]{1,0:T(8,128)}) %reduce-scatter.5.cloned.1.call-update) | async-done | bytes 1048592 | tf_op jit(solution)/shard_map/reduce_scatter | solution.py:92
  193.2 10.4 %fusion.13 = f32[2080,128]{1,0:T(8,128)} fusion(f32[2048,128]{1,0:T(8,128)} %reduce-scatter.5.cloned.1.call-done, s32[2080]{0:T(1024)S(1)} %clamp_reduce_fusion, pred[2080]{0:T(1024)(128)(4,1)S(1)} %compare_reduce_fusion.9), kind=kOutput, calls=%fused_computation.18 | convolution fusion | flops 6551633920 | bytes 2123936 | tf_op jit(solution)/shard_map/dot_general | solution.py:28
  204.8 24.4 %reduce-scatter.7.cloned.1.call-done = f32[520,128]{1,0:T(8,128)} async-done(((f32[2080,128]{1,0:T(8,128)}), f32[520,128]{1,0:T(8,128)}) %reduce-scatter.7.cloned.1.call-update) | async-done | bytes 266256
  (59 shorter events, 13.8 us)
Async XLA Ops:
  7.2 92.2 %copy-start = (bf16[128,512]{1,0:T(8,128)(2,1)S(1)}, bf16[128,512]{1,0:T(8,128)(2,1)}, u32[]{:S(2)}) copy-start(bf16[128,512]{1,0:T(8,128)(2,1)} %param.13) | copy-start | bytes 393220
  7.2 68.2 %copy-start.2 = (bf16[128,2048]{1,0:T(8,128)(2,1)S(1)}, bf16[128,2048]{1,0:T(8,128)(2,1)}, u32[]{:S(2)}) copy-start(bf16[128,2048]{1,0:T(8,128)(2,1)} %param.12) | copy-start | bytes 1572868
  7.2 68.5 %all-gather.3.cloned.1.call-start = ((), (), s32[]{:S(2)}) async-start(), calls=%async_computation.3 | async-start | bytes 2263040 | tf_op jit(solution)/shard_map/all_gather | solution.py:72
  7.9 185.3 %reduce-scatter.5.cloned.1.call-start = ((), (), s32[]{:S(2)}) async-start(), calls=%async_computation.2 | async-start | bytes 5242880 | tf_op jit(solution)/shard_map/reduce_scatter | solution.py:92
  96.2 3.1 %copy-start.4 = (f32[2048]{0:T(1024)S(1)}, f32[2048]{0:T(1024)}, u32[]{:S(2)}) copy-start(f32[2048]{0:T(1024)} %param.11) | copy-start | bytes 24580
  114.4 12.4 %copy-start.3 = (s32[1,16]{1,0:T(1,128)S(1)}, s32[1,16]{1,0:T(1,128)}, u32[]{:S(2)}) copy-start(s32[1,16]{1,0:T(1,128)} %param.15) | copy-start | bytes 196
  114.5 114.7 %reduce-scatter.7.cloned.1.call-start = ((), (), s32[]{:S(2)}) async-start(), calls=%async_computation.4 | async-start | bytes 1331200
  139.5 64.1 %copy-start.1 = (f32[128,2048]{0,1:T(8,128)S(1)}, f32[128,2048]{0,1:T(8,128)}, u32[]{:S(2)}) copy-start(f32[128,2048]{0,1:T(8,128)} %get-tuple-element.186) | copy-start | bytes 3145732
Sparse Core Ops, SparseCore 0:
  10.2 44.2 all-gather.2
  114.6 78.5 reduce-scatter.4
  203.7 25.4 reduce-scatter.6
where the time goes:
time: 237 us; the launch traced here: 236 us
  other arithmetic  84.5 us (36%)
  waiting for transfers between devices  78.8 us (33%)
  matrix products  35.3 us (15%)
  local copies, waits for them, and re-layouts  17 us (7%)
  between operations  14 us (6%)
  blocking collectives  5.87 us (2%)
    reduce_scatter x1, waiting for transfers between devices, shards(): lax.psum_scatter(flat_padded, 'gx', scatter_dimension=0, tiled=True)  53.7 us
    select_n x5, other arithmetic, block_layout(): owner = jnp.searchsorted(ends, block_ids, side='right')  49.8 us
    unnamed x4, waiting for transfers between devices  25.1 us
    dot_general x4, matrix products, select_rows(): jnp.dot(onehot.astype(jnp.bfloat16), rows, preferred_element_type=jnp.flo...  20.4 us
    gather x11, other arithmetic, block_layout(): source = jnp.clip(starts[slot_owner] + slot_within, 0, blocks - 1)  12.3 us
    dot_general x1, matrix products, select_rows(): jnp.dot(onehot.astype(jnp.float32), rows, precision=lax.Precision.HIGHEST...  10.4 us
    gather x2, other arithmetic, block_layout(): valid = slot_within < counts[slot_owner]  10.3 us
    sub x1, other arithmetic, block_layout(): gather_index = owner * most + block_ids - starts[owner]  10.2 us
  transfers between devices with their start and end apart: 3, of which 2 were waited for; matrix products, arithmetic and copies ran while one was open for 40% of the time, Pallas kernels for 0%

commit v1 on v0

v1 whole, which is shorter than its diff:
```python
import jax
import jax.numpy as jnp
from jax import lax
from jax.experimental import pallas as pl
from jax.experimental.pallas import tpu as pltpu
from jax.sharding import PartitionSpec as P

EPS = 1e-06
LANES = 128


def ceil_to(n, m):
    return (n + m - 1) // m * m


def power_of_two(n):
    return n & (n - 1) == 0


def relative(n, r):
    if power_of_two(n):
        return [(i, i ^ r) for i in range(n)]
    return [(i, (i + r) % n) for i in range(n)]


def relative_index(n, me, r):
    if power_of_two(n):
        return me ^ r
    return lax.rem(me + (n - r), n)


def gather_relatives(x, axis, n):
    known = {0: x}
    if power_of_two(n):
        basis = n - 1
        while basis:
            for r in list(known):
                known[r ^ basis] = lax.ppermute(known[r], axis, relative(n, basis))
            basis //= 2
    else:
        for r in range(1, n):
            known[r] = lax.ppermute(x, axis, relative(n, r))
    return known


def axis_sum(x, axis, n):
    if power_of_two(n):
        bit = 1
        while bit < n:
            x = x + lax.ppermute(x, axis, relative(n, bit))
            bit *= 2
        return x
    return lax.psum(x, axis)


def input_grad_kernel(owner_of, most, counts, place, key, grad, hidden, gain, *refs):
    pieces, (scaled, proj, dense, starts) = refs[:-4], refs[-4:]
    owners = counts.shape[0]

    def mark(o, at):
        starts[o] = at
        return at + counts[o]

    lax.fori_loop(0, owners, mark, jnp.int32(0))
    slot = lax.broadcasted_iota(jnp.int32, (most, LANES), 0)
    index = 0
    for piece in pieces:
        for i in range(piece.shape[0]):
            owner = owner_of(place[0], place[1], index)
            rows = pl.ds(starts[owner], most)
            new = piece[i].astype(jnp.float32)
            dense[rows, :] = jnp.where(slot < counts[owner], new, dense[rows, :])
            index += 1
    tokens, features = hidden.shape
    parts = key.shape[1] // LANES
    step = 256 if features % 256 == 0 else features
    total = jnp.zeros((tokens, LANES), jnp.float32)
    for at in range(0, features, step):
        weight = jnp.concatenate(
            [dense[pl.ds(at * parts + c, step, stride=parts), :] for c in range(parts)], axis=1
        ).astype(jnp.bfloat16)
        cols = slice(at, at + step)
        product = lax.dot_general(
            key[...], weight, (((1,), (1,)), ((), ())), preferred_element_type=jnp.float32
        )
        gained = gain[:, cols] * (grad[:, cols].astype(jnp.float32) + product)
        scaled[:, cols] = gained
        terms = gained * hidden[:, cols].astype(jnp.float32)
        for c in range(0, step, LANES):
            total = total + terms[:, c : c + LANES]
    proj[...] = jnp.sum(total, axis=1, keepdims=True)


def weight_grad_kernel(inner, group_blocks, most, counts, place, *refs):
    norms, keys = refs[: (len(refs) - 3) // 2], refs[(len(refs) - 3) // 2 : -3]
    sent, kept, flat = refs[-3:]
    rows = norms[0].shape[1]
    parts = keys[0].shape[1] // LANES
    step = 256 if rows % 256 == 0 else rows
    for at in range(0, rows, step):
        total = None
        for norm, key in zip(norms, keys):
            part = lax.dot_general(
                norm[:, at : at + step],
                key[...],
                (((0,), (0,)), ((), ())),
                preferred_element_type=jnp.float32,
            )
            total = part if total is None else total + part
        for c in range(parts):
            flat[pl.ds(at * parts + c, step, stride=parts), :] = total[:, c * LANES : (c + 1) * LANES]
    outer_index, inner_index = place[0], place[1]
    lead = lax.rem(outer_index * group_blocks, parts)
    for k in range(inner):
        owner = inner_index ^ k

        def add(j, at):
            return at + jnp.where(j < owner, counts[outer_index * inner + j], 0)

        start = lax.fori_loop(0, inner, add, lead)
        target = sent if k % 2 else kept
        target[k // 2] = flat[pl.ds(start, most), :]


def shards(hidden_in, norm_gain, normed_grad, key_grad, weight_blocks, block_count):
    outer, inner, halves = lax.axis_size("gx"), lax.axis_size("gy"), lax.axis_size("gz")
    owners = outer * inner
    most = weight_blocks.shape[2]
    tokens, features = hidden_in.shape
    width = key_grad.shape[1]
    parts = width // LANES
    blocks = features * parts
    group_blocks = (blocks + outer - 1) // outer
    model_width = features * halves
    gx, gy = lax.axis_index("gx"), lax.axis_index("gy")
    counts = block_count[0]
    place = jnp.stack([gx, gy]).astype(jnp.int32)

    found = gather_relatives(weight_blocks.reshape(most, LANES), "gx", outer)
    order = list(found)
    column = jnp.stack([found[r] for r in order])
    spread = {0: column}
    bit = inner // 2
    while bit:
        for r in list(spread):
            spread[r ^ bit] = lax.ppermute(spread[r], "gy", relative(inner, bit))
        bit //= 2
    names = [(r, s) for s in spread for r in order]

    def owner_of(i, j, index):
        r, s = names[index]
        return relative_index(outer, i, r) * inner + (j ^ s)

    hfloat = hidden_in.astype(jnp.float32)
    squares = axis_sum(jnp.sum(hfloat * hfloat, axis=1), "gz", halves)
    rstd = lax.rsqrt(squares / model_width + EPS)
    normed = (hfloat * rstd[:, None] * norm_gain).astype(jnp.bfloat16)

    rows = max(
        ((i + 1) * group_blocks + parts - 1) // parts - i * group_blocks // parts
        for i in range(outer)
    )
    reach = (outer - 1) * group_blocks // parts + rows
    padded = jnp.pad(normed, ((0, 0), (0, max(0, reach - features))))

    def window(member):
        return lax.dynamic_slice(padded, (0, member * group_blocks // parts), (tokens, rows))

    keys = gather_relatives(key_grad, "gx", outer)
    norms = {0: window(gx)}
    for r in range(1, outer):
        target = gx ^ r if power_of_two(outer) else lax.rem(gx + r, outer)
        norms[r] = lax.ppermute(window(target), "gx", relative(outer, r))

    smem = pl.BlockSpec(memory_space=pltpu.SMEM)
    vmem = pl.BlockSpec(memory_space=pltpu.VMEM)
    pieces = [spread[s] for s in spread]
    scaled, proj = pl.pallas_call(
        lambda *refs: input_grad_kernel(owner_of, most, *refs),
        name="input_grad",
        out_shape=(
            jax.ShapeDtypeStruct((tokens, features), jnp.float32),
            jax.ShapeDtypeStruct((tokens, 1), jnp.float32),
        ),
        in_specs=[smem, smem] + [vmem] * (4 + len(pieces)),
        out_specs=(vmem, vmem),
        scratch_shapes=[
            pltpu.VMEM((ceil_to(blocks + most, 8), LANES), jnp.float32),
            pltpu.SMEM((owners,), jnp.int32),
        ],
    )(counts, place, key_grad, normed_grad, hidden_in, norm_gain[None, :], *pieces)
    proj = axis_sum(proj[:, 0], "gz", halves)
    grad = scaled * rstd[:, None] - hfloat * (rstd**3 * proj / model_width)[:, None]
    hidden_grad = grad.astype(jnp.bfloat16)

    half = jax.ShapeDtypeStruct((inner // 2, most, LANES), jnp.float32)
    sent, kept = pl.pallas_call(
        lambda *refs: weight_grad_kernel(inner, group_blocks, most, *refs),
        name="weight_grad",
        out_shape=(half, half),
        in_specs=[smem, smem] + [vmem] * (2 * outer),
        out_specs=(vmem, vmem),
        scratch_shapes=[pltpu.VMEM((ceil_to(rows * parts + most, 8), LANES), jnp.float32)],
    )(counts, place, *[norms[r] for r in range(outer)], *[keys[r] for r in range(outer)])
    bit = 1
    while True:
        got = lax.ppermute(sent, "gy", relative(inner, bit))
        bit *= 2
        if bit == inner:
            break
        sent, kept = kept[1::2] + got[1::2], kept[0::2] + got[0::2]
    owned = (kept + got)[0]
    count = lax.dynamic_index_in_dim(counts, gx * inner + gy, 0, keepdims=False)
    slots = lax.broadcasted_iota(jnp.int32, (most, LANES), 0)
    owned = jnp.where(slots < count, owned, jnp.float32(0.0))
    return (hidden_grad, owned.reshape(1, 1, most, LANES))


def solution(mesh):
    placed = (
        P(("gx", "gy"), "gz"),
        P("gz"),
        P(("gx", "gy"), "gz"),
        P(("gx", "gy"), None),
        P(("gx", "gy"), "gz", None, None),
        P("gz", None),
    )
    return jax.shard_map(
        shards,
        mesh=mesh,
        in_specs=placed,
        out_specs=(P(("gx", "gy"), "gz"), P(("gx", "gy"), "gz", None, None)),
        check_vma=False,
    )
```

time: 237 us -> 77.6 us (0.33)
  other arithmetic: 84.5 us -> 7.6 us
  waiting for transfers between devices: 78.8 us -> 36.2 us
  matrix products: 35.3 us -> 0 us
  starting transfers between devices: 0.12 us -> 21 us
  between operations: 14 us -> 0.76 us
  local copies, waits for them, and re-layouts: 17 us -> 3.81 us
  Pallas kernels: 0 us -> 7.98 us
  blocking collectives: 5.87 us -> 0 us
    reduce_scatter x1 -> x0, waiting for transfers between devices: 53.7 us -> none  [shards(): lax.psum_scatter(flat_padded, 'gx', scatter_dimension=0, tiled=True)]
    select_n x6 -> x1, other arithmetic: 49.8 us -> 0.84 us  [shards(): owned = jnp.where(slots < count, owned, jnp.float32(0.0))]
    ppermute x0 -> x16, waiting for transfers between devices: none -> 36.2 us  [the longest x3 10.7 us: shards(): spread[r ^ bit] = lax.ppermute(spread[r], 'gy', relative(inner, bit))]
    dot_general x7 -> x0, matrix products: 35.3 us -> none  [the longest x4 20.4 us: select_rows(): jnp.dot(onehot.astype(jnp.bfloat16), rows, preferred_element_type=jnp.flo...]
    unnamed x4 -> x0, waiting for transfers between devices: 25.1 us -> none
    gather x13 -> x0, other arithmetic: 22.6 us -> none  [the longest x11 12.3 us: block_layout(): source = jnp.clip(starts[slot_owner] + slot_within, 0, blocks - 1)]
    ppermute x0 -> x16, starting transfers between devices: none -> 21 us  [the longest x6 11.2 us: gather_relatives(): known[r ^ basis] = lax.ppermute(known[r], axis, relative(n, basis))]
    sub x2 -> x0, other arithmetic: 10.8 us -> none  [the longest x1 10.2 us: block_layout(): gather_index = owner * most + block_ids - starts[owner]]
  transfers between devices with their start and end apart: 3 -> 16, of which waited for: 2 -> 10; matrix products, arithmetic and copies ran while one was open for 40% -> 8% of each run, Pallas kernels for 0% -> 6%
where the time goes in v1:
time: 77.6 us; the launch traced here: 77.3 us
  waiting for transfers between devices  36.2 us (47%)
  starting transfers between devices  21 us (27%)
  Pallas kernels  7.98 us (10%)
  other arithmetic  7.6 us (10%)
  local copies, waits for them, and re-layouts  3.81 us (5%)
    ppermute x6, starting transfers between devices, gather_relatives(): known[r ^ basis] = lax.ppermute(known[r], axis, relative(n, basis))  11.2 us
    ppermute x3, waiting for transfers between devices, shards(): spread[r ^ bit] = lax.ppermute(spread[r], 'gy', relative(inner, bit))  10.7 us
    ppermute x3, waiting for transfers between devices, shards(): norms[r] = lax.ppermute(window(target), 'gx', relative(outer, r))  9.33 us
    ppermute x6, waiting for transfers between devices, gather_relatives(): known[r ^ basis] = lax.ppermute(known[r], axis, relative(n, basis))  7.97 us
    ppermute x2, waiting for transfers between devices, shards(): got = lax.ppermute(sent, 'gy', relative(inner, bit))  7.18 us
    pallas_call x1, Pallas kernels, shards(): pl.pallas_call(lambda *refs: input_grad_kernel(owner_of, most, *refs), na...  4.82 us
    ppermute x3, starting transfers between devices, shards(): norms[r] = lax.ppermute(window(target), 'gx', relative(outer, r))  4.39 us
    pallas_call x1, Pallas kernels, shards(): pl.pallas_call(lambda *refs: weight_grad_kernel(inner, group_blocks, most...  3.17 us
  transfers between devices with their start and end apart: 16, of which 10 were waited for; matrix products, arithmetic and copies ran while one was open for 8% of the time, Pallas kernels for 6%

profile of v1, /device:TPU:0, one launch (start us, length us, event | category | flops | bytes accessed | tf_op | source)
XLA Modules:
  0.0 77.3 jit_solution(18187363443991219476)
XLA Ops:
  0.6 5.1 %collective-permute-start = (bf16[520,128]{1,0:T(8,128)(2,1)}, bf16[520,128]{1,0:T(8,128)(2,1)S(1)}, u32[]{:S(2)}, u32[]{:S(2)}) collective-permute-start(bf16[520,128]{1,0:T(8,128)(2,1)} %bitcast.14), channel_id=1, source_target_pairs={{0,24},{8,16},{16,8},{24,0},{1,25},{9,17},{17,9},{25,1},{2,26},{10... | collective-permute-start | bytes 399368 | tf_op jit(solution)/shard_map/ppermute | solution.py:38
  5.8 4.6 %collective-permute-done = bf16[520,128]{1,0:T(8,128)(2,1)S(1)} collective-permute-done((bf16[520,128]{1,0:T(8,128)(2,1)}, bf16[520,128]{1,0:T(8,128)(2,1)S(1)}, u32[]{:S(2)}, u32[]{:S(2)}) %collective-permute-start) | collective-permute-done | bytes 133152 | tf_op jit(solution)/shard_map/ppermute | solution.py:38
  10.4 1.7 %collective-permute-start.2 = (bf16[520,128]{1,0:T(8,128)(2,1)S(1)}, bf16[520,128]{1,0:T(8,128)(2,1)S(1)}, u32[]{:S(2)}, u32[]{:S(2)}) collective-permute-start(bf16[520,128]{1,0:T(8,128)(2,1)S(1)} %collective-permute-done), channel_id=1, source_target_pairs={{0,8},{8,0},{16,24},{24,16},{1,9},{9,1},{17,25},{25,17},{2,10},{10... | collective-permute-start | bytes 399368 | tf_op jit(solution)/shard_map/ppermute | solution.py:38
  12.8 2.6 %collective-permute-done.2 = bf16[520,128]{1,0:T(8,128)(2,1)S(1)} collective-permute-done((bf16[520,128]{1,0:T(8,128)(2,1)S(1)}, bf16[520,128]{1,0:T(8,128)(2,1)S(1)}, u32[]{:S(2)}, u32[]{:S(2)}) %collective-permute-start.2) | collective-permute-done | bytes 133152 | tf_op jit(solution)/shard_map/ppermute | solution.py:38
  15.4 1.0 %pad_maximum_fusion.refs_6_ = bf16[4,520,128]{2,1,0:T(8,128)(2,1)S(1)} fusion(bf16[1,520,128]{2,1,0:T(8,128)(2,1)S(1)} %bitcast.19, bf16[1,520,128]{2,1,0:T(8,128)(2,1)S(1)} %bitcast.18, bf16[1,520,128]{2,1,0:T(8,128)(2,1)S(1)} %bitcast.17, bf16[1,520,128]{2,1,0:T(8,128)(2,1)} %bitcast.16), kind=kLoop, calls=%fused_computation.8 | loop fusion | flops 798720 | bytes 1064960 | tf_op jit(solution)/shard_map/stack | solution.py:141
  16.5 1.7 %collective-permute-start.3 = (bf16[4,520,128]{2,1,0:T(8,128)(2,1)S(1)}, bf16[4,520,128]{2,1,0:T(8,128)(2,1)S(1)}, u32[]{:S(2)}, u32[]{:S(2)}) collective-permute-start(bf16[4,520,128]{2,1,0:T(8,128)(2,1)S(1)} %pad_maximum_fusion.refs_6_), channel_id=1, source_target_pairs={{0,4},{2,6},{4,0},{6,2},{1,5},{3,7},{5,1},{7,3},{8,12},{10,14},{12... | collective-permute-start | bytes 1597448 | tf_op jit(solution)/shard_map/ppermute | solution.py:146
  18.2 10.6 %collective-permute-done.3.refs_7_ = bf16[4,520,128]{2,1,0:T(8,128)(2,1)S(1)} collective-permute-done((bf16[4,520,128]{2,1,0:T(8,128)(2,1)S(1)}, bf16[4,520,128]{2,1,0:T(8,128)(2,1)S(1)}, u32[]{:S(2)}, u32[]{:S(2)}) %collective-permute-start.3) | collective-permute-done | bytes 532512 | tf_op jit(solution)/shard_map/ppermute | solution.py:146
  28.9 2.3 %collective-permute-start.12 = (bf16[128,512]{1,0:T(8,128)(2,1)S(1)}, bf16[128,512]{1,0:T(8,128)(2,1)S(1)}, u32[]{:S(2)}, u32[]{:S(2)}) collective-permute-start(bf16[128,512]{1,0:T(8,128)(2,1)S(1)} %copy-done.7), channel_id=1, source_target_pairs={{0,24},{8,16},{16,8},{24,0},{1,25},{9,17},{17,9},{25,1},{2,26},{10... | collective-permute-start | bytes 393224 | tf_op jit(solution)/shard_map/ppermute | solution.py:38
  31.4 1.6 %collective-permute-start.6 = (f32[128]{0:T(128)S(1)}, f32[128]{0:T(128)S(1)}, u32[]{:S(2)}, u32[]{:S(2)}) collective-permute-start(f32[128]{0:T(128)S(1)} %fusion), channel_id=1, source_target_pairs={{0,1},{1,0},{2,3},{3,2},{4,5},{5,4},{6,7},{7,6},{8,9},{9,8},{10,11... | collective-permute-start | bytes 1544 | tf_op jit(solution)/shard_map/ppermute | solution.py:50
  34.5 4.8 %input_grad.1 = (f32[128,2048]{1,0:T(8,128)}, f32[128,1]{1,0:T(8,128)}) custom-call(s32[16]{0:T(128)} %bitcast.21, s32[2]{0:T(128)} %pad_add_fusion.refs_1_, bf16[128,512]{1,0:T(8,128)(2,1)} %refs_6_.1, bf16[128,2048]{1,0:T(8,128)(2,1)} %refs_3_.1, bf16[128,2048]{1,0:T(8,128)(2,1)} %refs_4_.1, f32[1,2048]{1,0:T(1,128)} %bitcast.20, ...), custom_call_target="tpu_custom_call" | custom-call | tf_op jit(solution)/shard_map/input_grad/pallas_call | solution.py:178
  39.3 0.9 %reduce = f32[128]{0:T(128)S(1)} reduce(f32[128,1]{1,0:T(8,128)} %get-tuple-element.7, f32[]{:T(128)} %constant.69), dimensions={1}, to_apply=%get-tuple-element.7.reduce_sub_computation | reduce | bytes 1028 | tf_op jit(solution)/shard_map/input_grad/pallas_call | solution.py:178
  40.8 2.0 %collective-permute-start.13 = (bf16[128,512]{1,0:T(8,128)(2,1)S(1)}, bf16[128,512]{1,0:T(8,128)(2,1)S(1)}, u32[]{:S(2)}, u32[]{:S(2)}) collective-permute-start(bf16[128,512]{1,0:T(8,128)(2,1)S(1)} %collective-permute-done.12.refs_9_), channel_id=1, source_target_pairs={{0,8},{8,0},{16,24},{24,16},{1,9},{9,1},{17,25},{25,17},{2,10},{10... | collective-permute-start | bytes 393224 | tf_op jit(solution)/shard_map/ppermute | solution.py:38
  42.9 1.0 %collective-permute-done.7 = f32[128]{0:T(128)S(1)} collective-permute-done((f32[128]{0:T(128)S(1)}, f32[128]{0:T(128)S(1)}, u32[]{:S(2)}, u32[]{:S(2)}) %collective-permute-start.7) | collective-permute-done | bytes 544 | tf_op jit(solution)/shard_map/ppermute | solution.py:50
  43.9 2.4 %fusion.4 = (bf16[128,2048]{1,0:T(8,128)(2,1)S(1)}, bf16[128,2048]{1,0:T(8,128)(2,1)}) fusion(bf16[128,2048]{1,0:T(8,128)(2,1)S(1)} %copy-done.1, f32[2048]{0:T(1024)S(1)} %copy-done.14, f32[128]{0:T(128)S(1)} %get-tuple-element.11, f32[128]{0:T(128)S(1)} %get-tuple-element.10, f32[128,2048]{1,0:T(8,128)} %get-tuple-element.6), kind=kLoop, calls=%fused_computation.7 | loop fusion | flops 2097152 | bytes 2630656 | tf_op jit(solution)/shard_map/convert_element_type | solution.py:157
  46.3 0.9 %constant_dynamic-slice_fusion = (bf16[128,512]{1,0:T(8,128)(2,1)S(1)}, bf16[128,512]{1,0:T(8,128)(2,1)S(1)}, bf16[128,512]{1,0:T(8,128)(2,1)S(1)}, bf16[128,512]{1,0:T(8,128)(2,1)}) fusion(bf16[128,2048]{1,0:T(8,128)(2,1)S(1)} %get-tuple-element.12, s32[]{:T(128)S(6)} %select_n.49, s32[]{:T(128)S(6)} %select_n.47, s32[]{:T(128)S(6)} %select_n.45, ...), kind=kLoop, calls=%fused_computation.15 | loop fusion | bytes 1048592 | tf_op jit(solution)/shard_map/dynamic_slice | solution.py:167
  47.3 2.4 %collective-permute-start.10 = (bf16[128,512]{1,0:T(8,128)(2,1)S(1)}, bf16[128,512]{1,0:T(8,128)(2,1)S(1)}, u32[]{:S(2)}, u32[]{:S(2)}) collective-permute-start(bf16[128,512]{1,0:T(8,128)(2,1)S(1)} %get-tuple-element.14), channel_id=1, source_target_pairs={{0,24},{8,16},{16,8},{24,0},{1,25},{9,17},{17,9},{25,1},{2,26},{10... | collective-permute-start | bytes 393224 | tf_op jit(solution)/shard_map/ppermute | solution.py:173
  50.0 1.7 %collective-permute-start.9 = (bf16[128,512]{1,0:T(8,128)(2,1)S(1)}, bf16[128,512]{1,0:T(8,128)(2,1)S(1)}, u32[]{:S(2)}, u32[]{:S(2)}) collective-permute-start(bf16[128,512]{1,0:T(8,128)(2,1)S(1)} %get-tuple-element.15), channel_id=1, source_target_pairs={{0,16},{8,24},{16,0},{24,8},{1,17},{9,25},{17,1},{25,9},{2,18},{10... | collective-permute-start | bytes 393224 | tf_op jit(solution)/shard_map/ppermute | solution.py:173
  51.7 3.9 %collective-permute-done.10.refs_5_ = bf16[128,512]{1,0:T(8,128)(2,1)S(1)} collective-permute-done((bf16[128,512]{1,0:T(8,128)(2,1)S(1)}, bf16[128,512]{1,0:T(8,128)(2,1)S(1)}, u32[]{:S(2)}, u32[]{:S(2)}) %collective-permute-start.10) | collective-permute-done | bytes 131104 | tf_op jit(solution)/shard_map/ppermute | solution.py:173
  56.5 4.6 %collective-permute-done.9.refs_4_ = bf16[128,512]{1,0:T(8,128)(2,1)S(1)} collective-permute-done((bf16[128,512]{1,0:T(8,128)(2,1)S(1)}, bf16[128,512]{1,0:T(8,128)(2,1)S(1)}, u32[]{:S(2)}, u32[]{:S(2)}) %collective-permute-start.9) | collective-permute-done | bytes 131104 | tf_op jit(solution)/shard_map/ppermute | solution.py:173
  61.7 3.2 %weight_grad.1 = (f32[2,520,128]{2,1,0:T(8,128)}, f32[2,520,128]{2,1,0:T(8,128)}) custom-call(s32[16]{0:T(128)} %bitcast.22, s32[2]{0:T(128)} %pad_add_fusion.refs_1_, bf16[128,512]{1,0:T(8,128)(2,1)} %get-tuple-element.17.refs_2_, bf16[128,512]{1,0:T(8,128)(2,1)} %copy-done.12, bf16[128,512]{1,0:T(8,128)(2,1)} %copy-done.13, bf16[128,512]{1,0:T(8,128)(2,1)} %copy-done.11, ...), custom_call_target="tpu_custom_call" | custom-call | tf_op jit(solution)/shard_map/weight_grad/pallas_call | solution.py:197
  64.8 2.1 %collective-permute-done.14 = f32[2,520,128]{2,1,0:T(8,128)S(1)} collective-permute-done((f32[2,520,128]{2,1,0:T(8,128)}, f32[2,520,128]{2,1,0:T(8,128)S(1)}, u32[]{:S(2)}, u32[]{:S(2)}) %collective-permute-start.14) | collective-permute-done | bytes 532512 | tf_op jit(solution)/shard_map/ppermute | solution.py:207
  67.0 1.0 %slice_add_fusion = f32[1,520,128]{2,1,0:T(8,128)S(1)} fusion(f32[2,520,128]{2,1,0:T(8,128)S(1)} %collective-permute-done.14, f32[2,520,128]{2,1,0:T(8,128)} %get-tuple-element.8), kind=kLoop, calls=%fused_computation.9 | loop fusion | flops 66560 | bytes 798720 | tf_op jit(solution)/shard_map/add | solution.py:211
  68.0 1.6 %collective-permute-start.15 = (f32[1,520,128]{2,1,0:T(8,128)S(1)}, f32[1,520,128]{2,1,0:T(8,128)S(1)}, u32[]{:S(2)}, u32[]{:S(2)}) collective-permute-start(f32[1,520,128]{2,1,0:T(8,128)S(1)} %slice_add_fusion), channel_id=1, source_target_pairs={{0,4},{2,6},{4,0},{6,2},{1,5},{3,7},{5,1},{7,3},{8,12},{10,14},{12... | collective-permute-start | bytes 798728 | tf_op jit(solution)/shard_map/ppermute | solution.py:207
  71.4 5.1 %collective-permute-done.15 = f32[1,520,128]{2,1,0:T(8,128)S(1)} collective-permute-done((f32[1,520,128]{2,1,0:T(8,128)S(1)}, f32[1,520,128]{2,1,0:T(8,128)S(1)}, u32[]{:S(2)}, u32[]{:S(2)}) %collective-permute-start.15) | collective-permute-done | bytes 266272 | tf_op jit(solution)/shard_map/ppermute | solution.py:207
  (53 shorter events, 7.7 us)
Async XLA Ops:
  0.6 9.8 %collective-permute-start = (bf16[520,128]{1,0:T(8,128)(2,1)}, bf16[520,128]{1,0:T(8,128)(2,1)S(1)}, u32[]{:S(2)}, u32[]{:S(2)}) collective-permute-start(bf16[520,128]{1,0:T(8,128)(2,1)} %bitcast.14), channel_id=1, source_target_pairs={{0,24},{8,16},{16,8},{24,0},{1,25},{9,17},{17,9},{25,1},{2,26},{10... | collective-permute-start | bytes 399368 | tf_op jit(solution)/shard_map/ppermute | solution.py:38
  5.8 7.1 %collective-permute-start.1 = (bf16[520,128]{1,0:T(8,128)(2,1)}, bf16[520,128]{1,0:T(8,128)(2,1)S(1)}, u32[]{:S(2)}, u32[]{:S(2)}) collective-permute-start(bf16[520,128]{1,0:T(8,128)(2,1)} %bitcast.15), channel_id=1, source_target_pairs={{0,8},{8,0},{16,24},{24,16},{1,9},{9,1},{17,25},{25,17},{2,10},{10... | collective-permute-start | bytes 399368 | tf_op jit(solution)/shard_map/ppermute | solution.py:38
  10.4 5.0 %collective-permute-start.2 = (bf16[520,128]{1,0:T(8,128)(2,1)S(1)}, bf16[520,128]{1,0:T(8,128)(2,1)S(1)}, u32[]{:S(2)}, u32[]{:S(2)}) collective-permute-start(bf16[520,128]{1,0:T(8,128)(2,1)S(1)} %collective-permute-done), channel_id=1, source_target_pairs={{0,8},{8,0},{16,24},{24,16},{1,9},{9,1},{17,25},{25,17},{2,10},{10... | collective-permute-start | bytes 399368 | tf_op jit(solution)/shard_map/ppermute | solution.py:38
  15.4 13.4 %copy-start.7 = (bf16[128,512]{1,0:T(8,128)(2,1)S(1)}, bf16[128,512]{1,0:T(8,128)(2,1)}, u32[]{:S(2)}) copy-start(bf16[128,512]{1,0:T(8,128)(2,1)} %refs_6_.1) | copy-start | bytes 393220
  15.4 15.8 %copy-start = (bf16[128,2048]{1,0:T(8,128)(2,1)S(1)}, bf16[128,2048]{1,0:T(8,128)(2,1)}, u32[]{:S(2)}) copy-start(bf16[128,2048]{1,0:T(8,128)(2,1)} %refs_4_.1) | copy-start | bytes 1572868
  16.5 17.1 %copy-start.2 = (bf16[4,520,128]{2,1,0:T(8,128)(2,1)}, bf16[4,520,128]{2,1,0:T(8,128)(2,1)S(1)}, u32[]{:S(2)}) copy-start(bf16[4,520,128]{2,1,0:T(8,128)(2,1)S(1)} %pad_maximum_fusion.refs_6_) | copy-start | bytes 1597444
  16.5 12.4 %collective-permute-start.3 = (bf16[4,520,128]{2,1,0:T(8,128)(2,1)S(1)}, bf16[4,520,128]{2,1,0:T(8,128)(2,1)S(1)}, u32[]{:S(2)}, u32[]{:S(2)}) collective-permute-start(bf16[4,520,128]{2,1,0:T(8,128)(2,1)S(1)} %pad_maximum_fusion.refs_6_), channel_id=1, source_target_pairs={{0,4},{2,6},{4,0},{6,2},{1,5},{3,7},{5,1},{7,3},{8,12},{10,14},{12... | collective-permute-start | bytes 1597448 | tf_op jit(solution)/shard_map/ppermute | solution.py:146
  18.2 15.3 %collective-permute-start.4 = (bf16[4,520,128]{2,1,0:T(8,128)(2,1)S(1)}, bf16[4,520,128]{2,1,0:T(8,128)(2,1)S(1)}, u32[]{:S(2)}, u32[]{:S(2)}) collective-permute-start(bf16[4,520,128]{2,1,0:T(8,128)(2,1)S(1)} %pad_maximum_fusion.refs_6_), channel_id=1, source_target_pairs={{0,2},{2,0},{4,6},{6,4},{1,3},{3,1},{5,7},{7,5},{8,10},{10,8},{12,... | collective-permute-start | bytes 1597448 | tf_op jit(solution)/shard_map/ppermute | solution.py:146
  28.9 4.7 %collective-permute-start.5 = (bf16[4,520,128]{2,1,0:T(8,128)(2,1)S(1)}, bf16[4,520,128]{2,1,0:T(8,128)(2,1)S(1)}, u32[]{:S(2)}, u32[]{:S(2)}) collective-permute-start(bf16[4,520,128]{2,1,0:T(8,128)(2,1)S(1)} %collective-permute-done.3.refs_7_), channel_id=1, source_target_pairs={{0,2},{2,0},{4,6},{6,4},{1,3},{3,1},{5,7},{7,5},{8,10},{10,8},{12,... | collective-permute-start | bytes 1597448 | tf_op jit(solution)/shard_map/ppermute | solution.py:146
  28.9 12.0 %collective-permute-start.12 = (bf16[128,512]{1,0:T(8,128)(2,1)S(1)}, bf16[128,512]{1,0:T(8,128)(2,1)S(1)}, u32[]{:S(2)}, u32[]{:S(2)}) collective-permute-start(bf16[128,512]{1,0:T(8,128)(2,1)S(1)} %copy-done.7), channel_id=1, source_target_pairs={{0,24},{8,16},{16,8},{24,0},{1,25},{9,17},{17,9},{25,1},{2,26},{10... | collective-permute-start | bytes 393224 | tf_op jit(solution)/shard_map/ppermute | solution.py:38
  31.2 20.5 %collective-permute-start.11 = (bf16[128,512]{1,0:T(8,128)(2,1)S(1)}, bf16[128,512]{1,0:T(8,128)(2,1)S(1)}, u32[]{:S(2)}, u32[]{:S(2)}) collective-permute-start(bf16[128,512]{1,0:T(8,128)(2,1)S(1)} %copy-done.7), channel_id=1, source_target_pairs={{0,8},{8,0},{16,24},{24,16},{1,9},{9,1},{17,25},{25,17},{2,10},{10... | collective-permute-start | bytes 393224 | tf_op jit(solution)/shard_map/ppermute | solution.py:38
  31.4 11.5 %collective-permute-start.6 = (f32[128]{0:T(128)S(1)}, f32[128]{0:T(128)S(1)}, u32[]{:S(2)}, u32[]{:S(2)}) collective-permute-start(f32[128]{0:T(128)S(1)} %fusion), channel_id=1, source_target_pairs={{0,1},{1,0},{2,3},{3,2},{4,5},{5,4},{6,7},{7,6},{8,9},{9,8},{10,11... | collective-permute-start | bytes 1544 | tf_op jit(solution)/shard_map/ppermute | solution.py:50
  34.5 9.4 %copy-start.1 = (bf16[128,2048]{1,0:T(8,128)(2,1)S(1)}, bf16[128,2048]{1,0:T(8,128)(2,1)}, u32[]{:S(2)}) copy-start(bf16[128,2048]{1,0:T(8,128)(2,1)} %refs_4_.1) | copy-start | bytes 1572868
  40.3 3.6 %collective-permute-start.7 = (f32[128]{0:T(128)S(1)}, f32[128]{0:T(128)S(1)}, u32[]{:S(2)}, u32[]{:S(2)}) collective-permute-start(f32[128]{0:T(128)S(1)} %reduce), channel_id=1, source_target_pairs={{0,1},{1,0},{2,3},{3,2},{4,5},{5,4},{6,7},{7,6},{8,9},{9,8},{10,11... | collective-permute-start | bytes 1544 | tf_op jit(solution)/shard_map/ppermute | solution.py:50
  40.8 10.8 %collective-permute-start.13 = (bf16[128,512]{1,0:T(8,128)(2,1)S(1)}, bf16[128,512]{1,0:T(8,128)(2,1)S(1)}, u32[]{:S(2)}, u32[]{:S(2)}) collective-permute-start(bf16[128,512]{1,0:T(8,128)(2,1)S(1)} %collective-permute-done.12.refs_9_), channel_id=1, source_target_pairs={{0,8},{8,0},{16,24},{24,16},{1,9},{9,1},{17,25},{25,17},{2,10},{10... | collective-permute-start | bytes 393224 | tf_op jit(solution)/shard_map/ppermute | solution.py:38
  47.3 8.3 %collective-permute-start.10 = (bf16[128,512]{1,0:T(8,128)(2,1)S(1)}, bf16[128,512]{1,0:T(8,128)(2,1)S(1)}, u32[]{:S(2)}, u32[]{:S(2)}) collective-permute-start(bf16[128,512]{1,0:T(8,128)(2,1)S(1)} %get-tuple-element.14), channel_id=1, source_target_pairs={{0,24},{8,16},{16,8},{24,0},{1,25},{9,17},{17,9},{25,1},{2,26},{10... | collective-permute-start | bytes 393224 | tf_op jit(solution)/shard_map/ppermute | solution.py:173
  49.6 6.8 %collective-permute-start.8 = (bf16[128,512]{1,0:T(8,128)(2,1)S(1)}, bf16[128,512]{1,0:T(8,128)(2,1)S(1)}, u32[]{:S(2)}, u32[]{:S(2)}) collective-permute-start(bf16[128,512]{1,0:T(8,128)(2,1)S(1)} %get-tuple-element.16), channel_id=1, source_target_pairs={{0,8},{8,0},{16,24},{24,16},{1,9},{9,1},{17,25},{25,17},{2,10},{10... | collective-permute-start | bytes 393224 | tf_op jit(solution)/shard_map/ppermute | solution.py:173
  50.0 11.0 %collective-permute-start.9 = (bf16[128,512]{1,0:T(8,128)(2,1)S(1)}, bf16[128,512]{1,0:T(8,128)(2,1)S(1)}, u32[]{:S(2)}, u32[]{:S(2)}) collective-permute-start(bf16[128,512]{1,0:T(8,128)(2,1)S(1)} %get-tuple-element.15), channel_id=1, source_target_pairs={{0,16},{8,24},{16,0},{24,8},{1,17},{9,25},{17,1},{25,9},{2,18},{10... | collective-permute-start | bytes 393224 | tf_op jit(solution)/shard_map/ppermute | solution.py:173
  51.7 9.4 %copy-start.9 = (bf16[128,512]{1,0:T(8,128)(2,1)}, bf16[128,512]{1,0:T(8,128)(2,1)S(1)}, u32[]{:S(2)}) copy-start(bf16[128,512]{1,0:T(8,128)(2,1)S(1)} %collective-permute-done.11.refs_7_) | copy-start | bytes 393220
  51.7 9.4 %copy-start.10 = (bf16[128,512]{1,0:T(8,128)(2,1)}, bf16[128,512]{1,0:T(8,128)(2,1)S(1)}, u32[]{:S(2)}) copy-start(bf16[128,512]{1,0:T(8,128)(2,1)S(1)} %collective-permute-done.13.refs_8_) | copy-start | bytes 393220
  55.5 5.5 %copy-start.11 = (bf16[128,512]{1,0:T(8,128)(2,1)}, bf16[128,512]{1,0:T(8,128)(2,1)S(1)}, u32[]{:S(2)}) copy-start(bf16[128,512]{1,0:T(8,128)(2,1)S(1)} %collective-permute-done.10.refs_5_) | copy-start | bytes 393220
  64.8 11.6 %copy-start.3 = (f32[2,520,128]{2,1,0:T(8,128)S(1)}, f32[2,520,128]{2,1,0:T(8,128)}, u32[]{:S(2)}) copy-start(f32[2,520,128]{2,1,0:T(8,128)} %get-tuple-element.8) | copy-start | bytes 1597444
  64.8 2.1 %collective-permute-start.14 = (f32[2,520,128]{2,1,0:T(8,128)}, f32[2,520,128]{2,1,0:T(8,128)S(1)}, u32[]{:S(2)}, u32[]{:S(2)}) collective-permute-start(f32[2,520,128]{2,1,0:T(8,128)} %get-tuple-element.9), channel_id=1, source_target_pairs={{0,2},{2,0},{4,6},{6,4},{1,3},{3,1},{5,7},{7,5},{8,10},{10,8},{12,... | collective-permute-start | bytes 1597448 | tf_op jit(solution)/shard_map/ppermute | solution.py:207
  68.0 8.5 %collective-permute-start.15 = (f32[1,520,128]{2,1,0:T(8,128)S(1)}, f32[1,520,128]{2,1,0:T(8,128)S(1)}, u32[]{:S(2)}, u32[]{:S(2)}) collective-permute-start(f32[1,520,128]{2,1,0:T(8,128)S(1)} %slice_add_fusion), channel_id=1, source_target_pairs={{0,4},{2,6},{4,0},{6,2},{1,5},{3,7},{5,1},{7,3},{8,12},{10,14},{12... | collective-permute-start | bytes 798728 | tf_op jit(solution)/shard_map/ppermute | solution.py:207
  (8 other events, 20.9 us)

commit v2 on v1

--- a/solution.py
+++ b/solution.py
@@ -1,3 +1,5 @@
+import functools
+
 import jax
 import jax.numpy as jnp
 from jax import lax
@@ -43,14 +45,59 @@
     return known
 
 
-def axis_sum(x, axis, n):
-    if power_of_two(n):
-        bit = 1
-        while bit < n:
-            x = x + lax.ppermute(x, axis, relative(n, bit))
-            bit *= 2
-        return x
-    return lax.psum(x, axis)
+def axis_terms(x, axis, n):
+    if not power_of_two(n):
+        return lax.psum(x, axis), jnp.zeros_like(x)
+    bit = 1
+    while True:
+        got = lax.ppermute(x, axis, relative(n, bit)) if n > 1 else jnp.zeros_like(x)
+        bit *= 2
+        if bit >= n:
+            return x, got
+        x = x + got
+
+
+def column(row, lanes):
+    return jnp.transpose(jnp.broadcast_to(row, (lanes, row.shape[1])))
+
+
+def norm_kernel(members, model_width, starts, rows, place, square, other, hidden, gain, *outs):
+    tokens, features = hidden.shape
+    total = square[...] + other[...]
+    rstd = column(lax.rsqrt(total / model_width + EPS), LANES)
+
+    def scale(cols):
+        return (hidden[:, cols].astype(jnp.float32) * rstd[:, :1]) * gain[:, cols]
+
+    aligned = rows % LANES == 0 and all(s == i * rows for i, s in enumerate(starts))
+    for r, out in enumerate(outs):
+        member = members(place[0], r)
+        if aligned:
+            for at in range(0, rows, LANES):
+                cols = pl.ds(pl.multiple_of(member * rows + at, LANES), LANES)
+                part = (hidden[:, cols].astype(jnp.float32) * rstd) * gain[:, cols]
+                out[:, at : at + LANES] = part.astype(jnp.bfloat16)
+        else:
+            for i, start in enumerate(starts):
+
+                @pl.when(member == i)
+                def _(out=out, start=start):
+                    end = min(features, start + rows)
+                    part = scale(slice(start, end))
+                    if end - start < rows:
+                        fill = jnp.zeros((tokens, rows - (end - start)), jnp.float32)
+                        part = jnp.concatenate([part, fill], axis=1)
+                    out[...] = part.astype(jnp.bfloat16)
+
+
+def finish_kernel(model_width, square, other, proj, proj_other, scaled, hidden, out):
+    rstd = lax.rsqrt((square[...] + other[...]) / model_width + EPS)
+    shift = rstd**3 * (proj[...] + proj_other[...]) / model_width
+    rstd, shift = column(rstd, LANES), column(shift, LANES)
+    for at in range(0, hidden.shape[1], LANES):
+        cols = slice(at, at + LANES)
+        grad = scaled[:, cols] * rstd - hidden[:, cols].astype(jnp.float32) * shift
+        out[:, cols] = grad.astype(jnp.bfloat16)
 
 
 def input_grad_kernel(owner_of, most, counts, place, key, grad, hidden, gain, *refs):
@@ -88,7 +135,7 @@
         terms = gained * hidden[:, cols].astype(jnp.float32)
         for c in range(0, step, LANES):
             total = total + terms[:, c : c + LANES]
-    proj[...] = jnp.sum(total, axis=1, keepdims=True)
+    proj[...] = jnp.sum(jnp.transpose(total), axis=0, keepdims=True)
 
 
 def weight_grad_kernel(inner, group_blocks, most, counts, place, *refs):
@@ -136,72 +183,92 @@
     counts = block_count[0]
     place = jnp.stack([gx, gy]).astype(jnp.int32)
 
+    smem = pl.BlockSpec(memory_space=pltpu.SMEM)
+    vmem = pl.BlockSpec(memory_space=pltpu.VMEM)
+
+    def call(kernel, out_shape, scalars, arrays, scratch=(), megabytes=16):
+        single = not isinstance(out_shape, tuple)
+        return pl.pallas_call(
+            kernel,
+            out_shape=out_shape,
+            in_specs=[smem] * len(scalars) + [vmem] * len(arrays),
+            out_specs=vmem if single else (vmem,) * len(out_shape),
+            scratch_shapes=list(scratch),
+            compiler_params=pltpu.CompilerParams(vmem_limit_bytes=megabytes << 20),
+        )(*scalars, *arrays)
+
     found = gather_relatives(weight_blocks.reshape(most, LANES), "gx", outer)
     order = list(found)
-    column = jnp.stack([found[r] for r in order])
-    spread = {0: column}
-    bit = inner // 2
-    while bit:
-        for r in list(spread):
-            spread[r ^ bit] = lax.ppermute(spread[r], "gy", relative(inner, bit))
-        bit //= 2
-    names = [(r, s) for s in spread for r in order]
+    lots = [order[: len(order) // 2], order[len(order) // 2 :]]
+    pieces, names = [], []
+    for lot in lots:
+        spread = {0: jnp.stack([found[r] for r in lot])}
+        bit = inner // 2
+        while bit:
+            for r in list(spread):
+                spread[r ^ bit] = lax.ppermute(spread[r], "gy", relative(inner, bit))
+            bit //= 2
+        pieces += list(spread.values())
+        names += [(r, s) for s in spread for r in lot]
 
     def owner_of(i, j, index):
         r, s = names[index]
         return relative_index(outer, i, r) * inner + (j ^ s)
 
     hfloat = hidden_in.astype(jnp.float32)
-    squares = axis_sum(jnp.sum(hfloat * hfloat, axis=1), "gz", halves)
-    rstd = lax.rsqrt(squares / model_width + EPS)
-    normed = (hfloat * rstd[:, None] * norm_gain).astype(jnp.bfloat16)
-
+    square = jnp.sum(hfloat * hfloat, axis=1)
+    squares = [t[None, :] for t in axis_terms(square, "gz", halves)]
+    gain = norm_gain[None, :]
+
+    starts = [i * group_blocks // parts for i in range(outer)]
     rows = max(
-        ((i + 1) * group_blocks + parts - 1) // parts - i * group_blocks // parts
-        for i in range(outer)
-    )
-    reach = (outer - 1) * group_blocks // parts + rows
-    padded = jnp.pad(normed, ((0, 0), (0, max(0, reach - features))))
-
-    def window(member):
-        return lax.dynamic_slice(padded, (0, member * group_blocks // parts), (tokens, rows))
-
+        ((i + 1) * group_blocks + parts - 1) // parts - starts[i] for i in range(outer)
+    )
+
+    def target(i, r):
+        return i ^ r if power_of_two(outer) else lax.rem(i + r, outer)
+
+    window = jax.ShapeDtypeStruct((tokens, rows), jnp.bfloat16)
+    windows = call(
+        functools.partial(norm_kernel, target, model_width, starts, rows),
+        (window,) * outer,
+        [place],
+        [*squares, hidden_in, gain],
+    )
     keys = gather_relatives(key_grad, "gx", outer)
-    norms = {0: window(gx)}
+    norms = [windows[0]]
     for r in range(1, outer):
-        target = gx ^ r if power_of_two(outer) else lax.rem(gx + r, outer)
-        norms[r] = lax.ppermute(window(target), "gx", relative(outer, r))
-
-    smem = pl.BlockSpec(memory_space=pltpu.SMEM)
-    vmem = pl.BlockSpec(memory_space=pltpu.VMEM)
-    pieces = [spread[s] for s in spread]
-    scaled, proj = pl.pallas_call(
-        lambda *refs: input_grad_kernel(owner_of, most, *refs),
-        name="input_grad",
-        out_shape=(
+        norms.append(lax.ppermute(windows[r], "gx", relative(outer, r)))
+
+    scaled, proj = call(
+        functools.partial(input_grad_kernel, owner_of, most),
+        (
             jax.ShapeDtypeStruct((tokens, features), jnp.float32),
-            jax.ShapeDtypeStruct((tokens, 1), jnp.float32),
+            jax.ShapeDtypeStruct((1, tokens), jnp.float32),
         ),
-        in_specs=[smem, smem] + [vmem] * (4 + len(pieces)),
-        out_specs=(vmem, vmem),
-        scratch_shapes=[
+        [counts, place],
+        [key_grad, normed_grad, hidden_in, gain, *pieces],
+        [
             pltpu.VMEM((ceil_to(blocks + most, 8), LANES), jnp.float32),
             pltpu.SMEM((owners,), jnp.int32),
         ],
-    )(counts, place, key_grad, normed_grad, hidden_in, norm_gain[None, :], *pieces)
-    proj = axis_sum(proj[:, 0], "gz", halves)
-    grad = scaled * rstd[:, None] - hfloat * (rstd**3 * proj / model_width)[:, None]
-    hidden_grad = grad.astype(jnp.bfloat16)
+    )
+    projs = axis_terms(proj, "gz", halves)
+    hidden_grad = call(
+        functools.partial(finish_kernel, model_width),
+        jax.ShapeDtypeStruct((tokens, features), jnp.bfloat16),
+        [],
+        [*squares, *projs, scaled, hidden_in],
+    )
 
     half = jax.ShapeDtypeStruct((inner // 2, most, LANES), jnp.float32)
-    sent, kept = pl.pallas_call(
-        lambda *refs: weight_grad_kernel(inner, group_blocks, most, *refs),
-        name="weight_grad",
-        out_shape=(half, half),
-        in_specs=[smem, smem] + [vmem] * (2 * outer),
-        out_specs=(vmem, vmem),
-        scratch_shapes=[pltpu.VMEM((ceil_to(rows * parts + most, 8), LANES), jnp.float32)],
-    )(counts, place, *[norms[r] for r in range(outer)], *[keys[r] for r in range(outer)])
+    sent, kept = call(
+        functools.partial(weight_grad_kernel, inner, group_blocks, most),
+        (half, half),
+        [counts, place],
+        [*norms, *[keys[r] for r in range(outer)]],
+        [pltpu.VMEM((ceil_to(rows * parts + most, 8), LANES), jnp.float32)],
+    )
     bit = 1
     while True:
         got = lax.ppermute(sent, "gy", relative(inner, bit))

time: 77.6 us -> 61.3 us (0.79)
  waiting for transfers between devices: 36.2 us -> 24.6 us
  other arithmetic: 7.6 us -> 4.54 us
  starting transfers between devices: 21 us -> 22.8 us
  local copies, waits for them, and re-layouts: 3.81 us -> 2.07 us
  Pallas kernels: 7.98 us -> 6.28 us
    ppermute x2, waiting for transfers between devices: 7.18 us -> 0.01 us  [shards(): got = lax.ppermute(sent, 'gy', relative(inner, bit))]
    ppermute x3 -> x6, waiting for transfers between devices: 10.7 us -> 6.16 us  [shards(): spread[r ^ bit] = lax.ppermute(spread[r], 'gy', relative(inner, bit))]
    convert_element_type x1 -> x0, other arithmetic: 2.39 us -> none  [shards(): normed = (hfloat * rstd[:, None] * norm_gain).astype(jnp.bfloat16)]
    ppermute x3 -> x6, starting transfers between devices: 1.74 us -> 3.63 us  [shards(): spread[r ^ bit] = lax.ppermute(spread[r], 'gy', relative(inner, bit))]
    pallas_call x2 -> x4, Pallas kernels: 7.98 us -> 6.28 us  [call(): pl.pallas_call(kernel, out_shape=out_shape, in_specs=[smem] * len(scalars...]
    ppermute x6, starting transfers between devices: 11.2 us -> 10 us  [gather_relatives(): known[r ^ basis] = lax.ppermute(known[r], axis, relative(n, basis))]
    ppermute x5, starting transfers between devices: 6.53 us -> 7.6 us  [the longest x3 4.45 us: shards(): norms.append(lax.ppermute(windows[r], 'gx', relative(outer, r)))]
    reduce_sum x1, other arithmetic: 0.19 us -> 1.23 us  [shards(): square = jnp.sum(hfloat * hfloat, axis=1)]
  transfers between devices with their start and end apart: 16 -> 19, of which waited for: 10 -> 8; matrix products, arithmetic and copies ran while one was open for 8% -> 5% of each run, Pallas kernels for 6% -> 10%
where the time goes in v2:
time: 61.3 us; the launch traced here: 61 us
  waiting for transfers between devices  24.6 us (40%)
  starting transfers between devices  22.8 us (37%)
  Pallas kernels  6.28 us (10%)
  other arithmetic  4.54 us (7%)
  local copies, waits for them, and re-layouts  2.07 us (3%)
  between operations  0.75 us (1%)
    ppermute x6, starting transfers between devices, gather_relatives(): known[r ^ basis] = lax.ppermute(known[r], axis, relative(n, basis))  10 us
    ppermute x3, waiting for transfers between devices, shards(): norms.append(lax.ppermute(windows[r], 'gx', relative(outer, r)))  7.73 us
    ppermute x6, waiting for transfers between devices, gather_relatives(): known[r ^ basis] = lax.ppermute(known[r], axis, relative(n, basis))  7.3 us
    pallas_call x4, Pallas kernels, call(): pl.pallas_call(kernel, out_shape=out_shape, in_specs=[smem] * len(scalars...  6.28 us
    ppermute x6, waiting for transfers between devices, shards(): spread[r ^ bit] = lax.ppermute(spread[r], 'gy', relative(inner, bit))  6.16 us
    ppermute x3, starting transfers between devices, shards(): norms.append(lax.ppermute(windows[r], 'gx', relative(outer, r)))  4.45 us
    ppermute x6, starting transfers between devices, shards(): spread[r ^ bit] = lax.ppermute(spread[r], 'gy', relative(inner, bit))  3.63 us
    ppermute x2, waiting for transfers between devices, axis_terms(): lax.ppermute(x, axis, relative(n, bit))  3.37 us
  transfers between devices with their start and end apart: 19, of which 8 were waited for; matrix products, arithmetic and copies ran while one was open for 5% of the time, Pallas kernels for 10%

profile of v2, /device:TPU:0, one launch (start us, length us, event | category | flops | bytes accessed | tf_op | source)
XLA Modules:
  0.0 61.0 jit_solution(9179374044539400932)
XLA Ops:
  0.6 3.1 %collective-permute-start.14 = (bf16[128,512]{1,0:T(8,128)(2,1)}, bf16[128,512]{1,0:T(8,128)(2,1)S(1)}, u32[]{:S(2)}, u32[]{:S(2)}) collective-permute-start(bf16[128,512]{1,0:T(8,128)(2,1)} %refs_4_.1), channel_id=1, source_target_pairs={{0,8},{8,0},{16,24},{24,16},{1,9},{9,1},{17,25},{25,17},{2,10},{10... | collective-permute-start | bytes 393224 | tf_op jit(solution)/shard_map/ppermute | solution.py:40
  3.8 2.5 %collective-permute-start.15 = (bf16[128,512]{1,0:T(8,128)(2,1)}, bf16[128,512]{1,0:T(8,128)(2,1)S(1)}, u32[]{:S(2)}, u32[]{:S(2)}) collective-permute-start(bf16[128,512]{1,0:T(8,128)(2,1)} %refs_4_.1), channel_id=1, source_target_pairs={{0,24},{8,16},{16,8},{24,0},{1,25},{9,17},{17,9},{25,1},{2,26},{10... | collective-permute-start | bytes 393224 | tf_op jit(solution)/shard_map/ppermute | solution.py:40
  6.2 1.2 %multiply_reduce_fusion = f32[128]{0:T(128)S(1)} fusion(bf16[128,2048]{1,0:T(8,128)(2,1)} %hidden.5), kind=kLoop, calls=%fused_computation | loop fusion | flops 786304 | bytes 524800 | tf_op jit(solution)/shard_map/reduce_sum | solution.py:219
  7.5 1.6 %collective-permute-start = (f32[128]{0:T(128)S(1)}, f32[128]{0:T(128)S(1)}, u32[]{:S(2)}, u32[]{:S(2)}) collective-permute-start(f32[128]{0:T(128)S(1)} %multiply_reduce_fusion), channel_id=1, source_target_pairs={{0,1},{1,0},{2,3},{3,2},{4,5},{5,4},{6,7},{7,6},{8,9},{9,8},{10,11... | collective-permute-start | bytes 1544 | tf_op jit(solution)/shard_map/ppermute | solution.py:53
  9.1 2.0 %collective-permute-done = f32[128]{0:T(128)S(1)} collective-permute-done((f32[128]{0:T(128)S(1)}, f32[128]{0:T(128)S(1)}, u32[]{:S(2)}, u32[]{:S(2)}) %collective-permute-start) | collective-permute-done | bytes 544 | tf_op jit(solution)/shard_map/ppermute | solution.py:53
  12.7 1.2 %collective-permute-start.12 = (bf16[128,512]{1,0:T(8,128)(2,1)S(1)}, bf16[128,512]{1,0:T(8,128)(2,1)S(1)}, u32[]{:S(2)}, u32[]{:S(2)}) collective-permute-start(bf16[128,512]{1,0:T(8,128)(2,1)S(1)} %get-tuple-element.14), channel_id=1, source_target_pairs={{0,16},{8,24},{16,0},{24,8},{1,17},{9,25},{17,1},{25,9},{2,18},{10... | collective-permute-start | bytes 393224 | tf_op jit(solution)/shard_map/ppermute | solution.py:241
  13.9 2.5 %collective-permute-start.13 = (bf16[128,512]{1,0:T(8,128)(2,1)S(1)}, bf16[128,512]{1,0:T(8,128)(2,1)S(1)}, u32[]{:S(2)}, u32[]{:S(2)}) collective-permute-start(bf16[128,512]{1,0:T(8,128)(2,1)S(1)} %get-tuple-element.15), channel_id=1, source_target_pairs={{0,24},{8,16},{16,8},{24,0},{1,25},{9,17},{17,9},{25,1},{2,26},{10... | collective-permute-start | bytes 393224 | tf_op jit(solution)/shard_map/ppermute | solution.py:241
  16.4 1.4 %collective-permute-start.1 = (bf16[520,128]{1,0:T(8,128)(2,1)S(1)}, bf16[520,128]{1,0:T(8,128)(2,1)S(1)}, u32[]{:S(2)}, u32[]{:S(2)}) collective-permute-start(bf16[520,128]{1,0:T(8,128)(2,1)S(1)} %bitcast.24), channel_id=1, source_target_pairs={{0,24},{8,16},{16,8},{24,0},{1,25},{9,17},{17,9},{25,1},{2,26},{10... | collective-permute-start | bytes 399368 | tf_op jit(solution)/shard_map/ppermute | solution.py:40
  17.8 2.5 %collective-permute-done.11.refs_1_ = bf16[128,512]{1,0:T(8,128)(2,1)S(1)} collective-permute-done((bf16[128,512]{1,0:T(8,128)(2,1)S(1)}, bf16[128,512]{1,0:T(8,128)(2,1)S(1)}, u32[]{:S(2)}, u32[]{:S(2)}) %collective-permute-start.11) | collective-permute-done | bytes 131104 | tf_op jit(solution)/shard_map/ppermute | solution.py:241
  20.4 5.2 %collective-permute-done.12.refs_2_ = bf16[128,512]{1,0:T(8,128)(2,1)S(1)} collective-permute-done((bf16[128,512]{1,0:T(8,128)(2,1)S(1)}, bf16[128,512]{1,0:T(8,128)(2,1)S(1)}, u32[]{:S(2)}, u32[]{:S(2)}) %collective-permute-start.12) | collective-permute-done | bytes 131104 | tf_op jit(solution)/shard_map/ppermute | solution.py:241
  25.5 2.0 %collective-permute-done.16.refs_6_ = bf16[128,512]{1,0:T(8,128)(2,1)S(1)} collective-permute-done((bf16[128,512]{1,0:T(8,128)(2,1)S(1)}, bf16[128,512]{1,0:T(8,128)(2,1)S(1)}, u32[]{:S(2)}, u32[]{:S(2)}) %collective-permute-start.16) | collective-permute-done | bytes 131104 | tf_op jit(solution)/shard_map/ppermute | solution.py:40
  28.2 1.4 %shard_map.80 = (f32[2,520,128]{2,1,0:T(8,128)S(1)}, f32[2,520,128]{2,1,0:T(8,128)S(1)}) custom-call(s32[16]{0:T(128)S(1)} %bitcast.20, s32[2]{0:T(128)S(1)} %pad_add_fusion.place, bf16[128,512]{1,0:T(8,128)(2,1)S(1)} %get-tuple-element.12.refs_0_, bf16[128,512]{1,0:T(8,128)(2,1)S(1)} %collective-permute-done.11.refs_1_, ...), custom_call_target="tpu_custom_call" | custom-call | tf_op jit(solution)/shard_map/pallas_call | solution.py:191
  29.7 2.9 %collective-permute-start.5 = (bf16[520,128]{1,0:T(8,128)(2,1)S(1)}, bf16[520,128]{1,0:T(8,128)(2,1)S(1)}, u32[]{:S(2)}, u32[]{:S(2)}) collective-permute-start(bf16[520,128]{1,0:T(8,128)(2,1)S(1)} %bitcast.25), channel_id=1, source_target_pairs={{0,8},{8,0},{16,24},{24,16},{1,9},{9,1},{17,25},{25,17},{2,10},{10... | collective-permute-start | bytes 399368 | tf_op jit(solution)/shard_map/ppermute | solution.py:40
  32.7 1.6 %collective-permute-start.2 = (bf16[2,520,128]{2,1,0:T(8,128)(2,1)S(1)}, bf16[2,520,128]{2,1,0:T(8,128)(2,1)S(1)}, u32[]{:S(2)}, u32[]{:S(2)}) collective-permute-start(bf16[2,520,128]{2,1,0:T(8,128)(2,1)S(1)} %pad_maximum_fusion.refs_0_), channel_id=1, source_target_pairs={{0,4},{2,6},{4,0},{6,2},{1,5},{3,7},{5,1},{7,3},{8,12},{10,14},{12... | collective-permute-start | bytes 798728 | tf_op jit(solution)/shard_map/ppermute | solution.py:209
  34.3 2.7 %collective-permute-done.5 = bf16[520,128]{1,0:T(8,128)(2,1)S(1)} collective-permute-done((bf16[520,128]{1,0:T(8,128)(2,1)S(1)}, bf16[520,128]{1,0:T(8,128)(2,1)S(1)}, u32[]{:S(2)}, u32[]{:S(2)}) %collective-permute-start.5) | collective-permute-done | bytes 133152 | tf_op jit(solution)/shard_map/ppermute | solution.py:40
  37.0 2.6 %collective-permute-done.6 = bf16[520,128]{1,0:T(8,128)(2,1)S(1)} collective-permute-done((bf16[520,128]{1,0:T(8,128)(2,1)S(1)}, bf16[520,128]{1,0:T(8,128)(2,1)S(1)}, u32[]{:S(2)}, u32[]{:S(2)}) %collective-permute-start.6) | collective-permute-done | bytes 133152 | tf_op jit(solution)/shard_map/ppermute | solution.py:40
  39.6 1.6 %collective-permute-start.7 = (bf16[2,520,128]{2,1,0:T(8,128)(2,1)S(1)}, bf16[2,520,128]{2,1,0:T(8,128)(2,1)S(1)}, u32[]{:S(2)}, u32[]{:S(2)}) collective-permute-start(bf16[2,520,128]{2,1,0:T(8,128)(2,1)S(1)} %pad_maximum_fusion.1.refs_4_), channel_id=1, source_target_pairs={{0,4},{2,6},{4,0},{6,2},{1,5},{3,7},{5,1},{7,3},{8,12},{10,14},{12... | collective-permute-start | bytes 798728 | tf_op jit(solution)/shard_map/ppermute | solution.py:209
  41.7 6.1 %collective-permute-done.7.refs_5_ = bf16[2,520,128]{2,1,0:T(8,128)(2,1)S(1)} collective-permute-done((bf16[2,520,128]{2,1,0:T(8,128)(2,1)S(1)}, bf16[2,520,128]{2,1,0:T(8,128)(2,1)S(1)}, u32[]{:S(2)}, u32[]{:S(2)}) %collective-permute-start.7) | collective-permute-done | bytes 266272 | tf_op jit(solution)/shard_map/ppermute | solution.py:209
  49.4 1.5 %collective-permute-start.18 = (f32[1,520,128]{2,1,0:T(8,128)}, f32[1,520,128]{2,1,0:T(8,128)}, u32[]{:S(2)}, u32[]{:S(2)}) collective-permute-start(f32[1,520,128]{2,1,0:T(8,128)} %slice_add_fusion), channel_id=1, source_target_pairs={{0,4},{2,6},{4,0},{6,2},{1,5},{3,7},{5,1},{7,3},{8,12},{10,14},{12... | collective-permute-start | bytes 798728 | tf_op jit(solution)/shard_map/ppermute | solution.py:274
  51.5 3.0 %shard_map.77 = (f32[128,2048]{1,0:T(8,128)S(1)}, f32[1,128]{1,0:T(1,128)S(1)}) custom-call(s32[16]{0:T(128)S(1)} %bitcast.21, s32[2]{0:T(128)S(1)} %pad_add_fusion.place, bf16[128,512]{1,0:T(8,128)(2,1)S(1)} %copy-done.1, bf16[128,2048]{1,0:T(8,128)(2,1)S(1)} %copy-done.2, bf16[128,2048]{1,0:T(8,128)(2,1)S(1)} %copy-done, f32[1,2048]{1,0:T(1,128)S(1)} %bitcast.17, ...), custom_call_target="tpu_custom_call" | custom-call | tf_op jit(solution)/shard_map/pallas_call | solution.py:191
  54.5 1.6 %collective-permute-start.10 = (f32[1,128]{1,0:T(1,128)S(1)}, f32[1,128]{1,0:T(1,128)S(1)}, u32[]{:S(2)}, u32[]{:S(2)}) collective-permute-start(f32[1,128]{1,0:T(1,128)S(1)} %get-tuple-element.10.proj), channel_id=1, source_target_pairs={{0,1},{1,0},{2,3},{3,2},{4,5},{5,4},{6,7},{7,6},{8,9},{9,8},{10,11... | collective-permute-start | bytes 1544 | tf_op jit(solution)/shard_map/ppermute | solution.py:53
  56.7 1.4 %collective-permute-done.10.proj_other = f32[1,128]{1,0:T(1,128)S(1)} collective-permute-done((f32[1,128]{1,0:T(1,128)S(1)}, f32[1,128]{1,0:T(1,128)S(1)}, u32[]{:S(2)}, u32[]{:S(2)}) %collective-permute-start.10) | collective-permute-done | bytes 544 | tf_op jit(solution)/shard_map/ppermute | solution.py:53
  58.1 1.0 %shard_map.78 = bf16[128,2048]{1,0:T(8,128)(2,1)} custom-call(f32[1,128]{1,0:T(1,128)S(1)} %bitcast.19, f32[1,128]{1,0:T(1,128)S(1)} %bitcast.23, f32[1,128]{1,0:T(1,128)S(1)} %get-tuple-element.10.proj, f32[1,128]{1,0:T(1,128)S(1)} %collective-permute-done.10.proj_other, f32[128,2048]{1,0:T(8,128)S(1)} %get-tuple-element.11.scaled, ...), custom_call_target="tpu_custom_call" | custom-call | tf_op jit(solution)/shard_map/pallas_call | solution.py:191
  59.2 1.8 %fusion.2 = f32[1,1,520,128]{3,2,1,0:T(8,128)} fusion(f32[1,520,128]{2,1,0:T(8,128)} %collective-permute-done.18, f32[2,520,128]{2,1,0:T(8,128)S(1)} %copy-done.6, f32[2,520,128]{2,1,0:T(8,128)S(1)} %get-tuple-element.16, pred[520]{0:T(1024)(128)(4,1)S(1)} %iota_compare_fusion), kind=kLoop, calls=%fused_computation.5 | loop fusion | flops 199680 | bytes 1065480 | tf_op jit(solution)/shard_map/jit(_where)/select_n | solution.py:282
  (42 shorter events, 5.8 us)
Async XLA Ops:
  0.6 10.5 %copy-start = (bf16[128,2048]{1,0:T(8,128)(2,1)S(1)}, bf16[128,2048]{1,0:T(8,128)(2,1)}, u32[]{:S(2)}) copy-start(bf16[128,2048]{1,0:T(8,128)(2,1)} %hidden.5) | copy-start | bytes 1572868
  0.6 15.7 %collective-permute-start.14 = (bf16[128,512]{1,0:T(8,128)(2,1)}, bf16[128,512]{1,0:T(8,128)(2,1)S(1)}, u32[]{:S(2)}, u32[]{:S(2)}) collective-permute-start(bf16[128,512]{1,0:T(8,128)(2,1)} %refs_4_.1), channel_id=1, source_target_pairs={{0,8},{8,0},{16,24},{24,16},{1,9},{9,1},{17,25},{25,17},{2,10},{10... | collective-permute-start | bytes 393224 | tf_op jit(solution)/shard_map/ppermute | solution.py:40
  3.8 12.6 %collective-permute-start.15 = (bf16[128,512]{1,0:T(8,128)(2,1)}, bf16[128,512]{1,0:T(8,128)(2,1)S(1)}, u32[]{:S(2)}, u32[]{:S(2)}) collective-permute-start(bf16[128,512]{1,0:T(8,128)(2,1)} %refs_4_.1), channel_id=1, source_target_pairs={{0,24},{8,16},{16,8},{24,0},{1,25},{9,17},{17,9},{25,1},{2,26},{10... | collective-permute-start | bytes 393224 | tf_op jit(solution)/shard_map/ppermute | solution.py:40
  7.5 3.6 %collective-permute-start = (f32[128]{0:T(128)S(1)}, f32[128]{0:T(128)S(1)}, u32[]{:S(2)}, u32[]{:S(2)}) collective-permute-start(f32[128]{0:T(128)S(1)} %multiply_reduce_fusion), channel_id=1, source_target_pairs={{0,1},{1,0},{2,3},{3,2},{4,5},{5,4},{6,7},{7,6},{8,9},{9,8},{10,11... | collective-permute-start | bytes 1544 | tf_op jit(solution)/shard_map/ppermute | solution.py:53
  9.0 2.1 %copy-start.3 = (f32[2048]{0:T(1024)S(1)}, f32[2048]{0:T(1024)}, u32[]{:S(2)}) copy-start(f32[2048]{0:T(1024)} %param.7) | copy-start | bytes 24580
  11.1 5.3 %copy-start.7 = (bf16[1,1,520,128]{3,2,1,0:T(8,128)(2,1)S(1)}, bf16[1,1,520,128]{3,2,1,0:T(8,128)(2,1)}, u32[]{:S(2)}) copy-start(bf16[1,1,520,128]{3,2,1,0:T(8,128)(2,1)} %param.10) | copy-start | bytes 399364
  11.1 16.4 %copy-start.1 = (bf16[128,512]{1,0:T(8,128)(2,1)S(1)}, bf16[128,512]{1,0:T(8,128)(2,1)}, u32[]{:S(2)}) copy-start(bf16[128,512]{1,0:T(8,128)(2,1)} %refs_4_.1) | copy-start | bytes 393220
  11.9 8.4 %collective-permute-start.11 = (bf16[128,512]{1,0:T(8,128)(2,1)S(1)}, bf16[128,512]{1,0:T(8,128)(2,1)S(1)}, u32[]{:S(2)}, u32[]{:S(2)}) collective-permute-start(bf16[128,512]{1,0:T(8,128)(2,1)S(1)} %get-tuple-element.13), channel_id=1, source_target_pairs={{0,8},{8,0},{16,24},{24,16},{1,9},{9,1},{17,25},{25,17},{2,10},{10... | collective-permute-start | bytes 393224 | tf_op jit(solution)/shard_map/ppermute | solution.py:241
  12.7 12.9 %collective-permute-start.12 = (bf16[128,512]{1,0:T(8,128)(2,1)S(1)}, bf16[128,512]{1,0:T(8,128)(2,1)S(1)}, u32[]{:S(2)}, u32[]{:S(2)}) collective-permute-start(bf16[128,512]{1,0:T(8,128)(2,1)S(1)} %get-tuple-element.14), channel_id=1, source_target_pairs={{0,16},{8,24},{16,0},{24,8},{1,17},{9,25},{17,1},{25,9},{2,18},{10... | collective-permute-start | bytes 393224 | tf_op jit(solution)/shard_map/ppermute | solution.py:241
  13.9 11.6 %collective-permute-start.13 = (bf16[128,512]{1,0:T(8,128)(2,1)S(1)}, bf16[128,512]{1,0:T(8,128)(2,1)S(1)}, u32[]{:S(2)}, u32[]{:S(2)}) collective-permute-start(bf16[128,512]{1,0:T(8,128)(2,1)S(1)} %get-tuple-element.15), channel_id=1, source_target_pairs={{0,24},{8,16},{16,8},{24,0},{1,25},{9,17},{17,9},{25,1},{2,26},{10... | collective-permute-start | bytes 393224 | tf_op jit(solution)/shard_map/ppermute | solution.py:241
  16.4 11.1 %collective-permute-start.16 = (bf16[128,512]{1,0:T(8,128)(2,1)S(1)}, bf16[128,512]{1,0:T(8,128)(2,1)S(1)}, u32[]{:S(2)}, u32[]{:S(2)}) collective-permute-start(bf16[128,512]{1,0:T(8,128)(2,1)S(1)} %collective-permute-done.15.refs_7_), channel_id=1, source_target_pairs={{0,8},{8,0},{16,24},{24,16},{1,9},{9,1},{17,25},{25,17},{2,10},{10... | collective-permute-start | bytes 393224 | tf_op jit(solution)/shard_map/ppermute | solution.py:40
  16.4 16.2 %collective-permute-start.1 = (bf16[520,128]{1,0:T(8,128)(2,1)S(1)}, bf16[520,128]{1,0:T(8,128)(2,1)S(1)}, u32[]{:S(2)}, u32[]{:S(2)}) collective-permute-start(bf16[520,128]{1,0:T(8,128)(2,1)S(1)} %bitcast.24), channel_id=1, source_target_pairs={{0,24},{8,16},{16,8},{24,0},{1,25},{9,17},{17,9},{25,1},{2,26},{10... | collective-permute-start | bytes 399368 | tf_op jit(solution)/shard_map/ppermute | solution.py:40
  29.6 18.3 %collective-permute-start.17 = (f32[2,520,128]{2,1,0:T(8,128)S(1)}, f32[2,520,128]{2,1,0:T(8,128)S(1)}, u32[]{:S(2)}, u32[]{:S(2)}) collective-permute-start(f32[2,520,128]{2,1,0:T(8,128)S(1)} %get-tuple-element.17), channel_id=1, source_target_pairs={{0,2},{2,0},{4,6},{6,4},{1,3},{3,1},{5,7},{7,5},{8,10},{10,8},{12,... | collective-permute-start | bytes 1597448 | tf_op jit(solution)/shard_map/ppermute | solution.py:274
  29.7 7.3 %collective-permute-start.5 = (bf16[520,128]{1,0:T(8,128)(2,1)S(1)}, bf16[520,128]{1,0:T(8,128)(2,1)S(1)}, u32[]{:S(2)}, u32[]{:S(2)}) collective-permute-start(bf16[520,128]{1,0:T(8,128)(2,1)S(1)} %bitcast.25), channel_id=1, source_target_pairs={{0,8},{8,0},{16,24},{24,16},{1,9},{9,1},{17,25},{25,17},{2,10},{10... | collective-permute-start | bytes 399368 | tf_op jit(solution)/shard_map/ppermute | solution.py:40
  32.6 7.0 %collective-permute-start.6 = (bf16[520,128]{1,0:T(8,128)(2,1)S(1)}, bf16[520,128]{1,0:T(8,128)(2,1)S(1)}, u32[]{:S(2)}, u32[]{:S(2)}) collective-permute-start(bf16[520,128]{1,0:T(8,128)(2,1)S(1)} %collective-permute-done.1), channel_id=1, source_target_pairs={{0,8},{8,0},{16,24},{24,16},{1,9},{9,1},{17,25},{25,17},{2,10},{10... | collective-permute-start | bytes 399368 | tf_op jit(solution)/shard_map/ppermute | solution.py:40
  32.7 9.0 %collective-permute-start.2 = (bf16[2,520,128]{2,1,0:T(8,128)(2,1)S(1)}, bf16[2,520,128]{2,1,0:T(8,128)(2,1)S(1)}, u32[]{:S(2)}, u32[]{:S(2)}) collective-permute-start(bf16[2,520,128]{2,1,0:T(8,128)(2,1)S(1)} %pad_maximum_fusion.refs_0_), channel_id=1, source_target_pairs={{0,4},{2,6},{4,0},{6,2},{1,5},{3,7},{5,1},{7,3},{8,12},{10,14},{12... | collective-permute-start | bytes 798728 | tf_op jit(solution)/shard_map/ppermute | solution.py:209
  39.6 11.9 %copy-start.2 = (bf16[128,2048]{1,0:T(8,128)(2,1)S(1)}, bf16[128,2048]{1,0:T(8,128)(2,1)}, u32[]{:S(2)}) copy-start(bf16[128,2048]{1,0:T(8,128)(2,1)} %grad.1) | copy-start | bytes 1572868
  39.6 8.2 %collective-permute-start.7 = (bf16[2,520,128]{2,1,0:T(8,128)(2,1)S(1)}, bf16[2,520,128]{2,1,0:T(8,128)(2,1)S(1)}, u32[]{:S(2)}, u32[]{:S(2)}) collective-permute-start(bf16[2,520,128]{2,1,0:T(8,128)(2,1)S(1)} %pad_maximum_fusion.1.refs_4_), channel_id=1, source_target_pairs={{0,4},{2,6},{4,0},{6,2},{1,5},{3,7},{5,1},{7,3},{8,12},{10,14},{12... | collective-permute-start | bytes 798728 | tf_op jit(solution)/shard_map/ppermute | solution.py:209
  41.2 10.3 %collective-permute-start.3 = (bf16[2,520,128]{2,1,0:T(8,128)(2,1)S(1)}, bf16[2,520,128]{2,1,0:T(8,128)(2,1)S(1)}, u32[]{:S(2)}, u32[]{:S(2)}) collective-permute-start(bf16[2,520,128]{2,1,0:T(8,128)(2,1)S(1)} %pad_maximum_fusion.refs_0_), channel_id=1, source_target_pairs={{0,2},{2,0},{4,6},{6,4},{1,3},{3,1},{5,7},{7,5},{8,10},{10,8},{12,... | collective-permute-start | bytes 798728 | tf_op jit(solution)/shard_map/ppermute | solution.py:209
  41.2 10.3 %collective-permute-start.8 = (bf16[2,520,128]{2,1,0:T(8,128)(2,1)S(1)}, bf16[2,520,128]{2,1,0:T(8,128)(2,1)S(1)}, u32[]{:S(2)}, u32[]{:S(2)}) collective-permute-start(bf16[2,520,128]{2,1,0:T(8,128)(2,1)S(1)} %pad_maximum_fusion.1.refs_4_), channel_id=1, source_target_pairs={{0,2},{2,0},{4,6},{6,4},{1,3},{3,1},{5,7},{7,5},{8,10},{10,8},{12,... | collective-permute-start | bytes 798728 | tf_op jit(solution)/shard_map/ppermute | solution.py:209
  41.7 9.8 %collective-permute-start.4 = (bf16[2,520,128]{2,1,0:T(8,128)(2,1)S(1)}, bf16[2,520,128]{2,1,0:T(8,128)(2,1)}, u32[]{:S(2)}, u32[]{:S(2)}) collective-permute-start(bf16[2,520,128]{2,1,0:T(8,128)(2,1)S(1)} %collective-permute-done.2.refs_1_), channel_id=1, source_target_pairs={{0,2},{2,0},{4,6},{6,4},{1,3},{3,1},{5,7},{7,5},{8,10},{10,8},{12,... | collective-permute-start | bytes 798728 | tf_op jit(solution)/shard_map/ppermute | solution.py:209
  47.9 3.6 %collective-permute-start.9 = (bf16[2,520,128]{2,1,0:T(8,128)(2,1)S(1)}, bf16[2,520,128]{2,1,0:T(8,128)(2,1)}, u32[]{:S(2)}, u32[]{:S(2)}) collective-permute-start(bf16[2,520,128]{2,1,0:T(8,128)(2,1)S(1)} %collective-permute-done.7.refs_5_), channel_id=1, source_target_pairs={{0,2},{2,0},{4,6},{6,4},{1,3},{3,1},{5,7},{7,5},{8,10},{10,8},{12,... | collective-permute-start | bytes 798728 | tf_op jit(solution)/shard_map/ppermute | solution.py:209
  49.4 9.8 %collective-permute-start.18 = (f32[1,520,128]{2,1,0:T(8,128)}, f32[1,520,128]{2,1,0:T(8,128)}, u32[]{:S(2)}, u32[]{:S(2)}) collective-permute-start(f32[1,520,128]{2,1,0:T(8,128)} %slice_add_fusion), channel_id=1, source_target_pairs={{0,4},{2,6},{4,0},{6,2},{1,5},{3,7},{5,1},{7,3},{8,12},{10,14},{12... | collective-permute-start | bytes 798728 | tf_op jit(solution)/shard_map/ppermute | solution.py:274
  54.5 3.6 %collective-permute-start.10 = (f32[1,128]{1,0:T(1,128)S(1)}, f32[1,128]{1,0:T(1,128)S(1)}, u32[]{:S(2)}, u32[]{:S(2)}) collective-permute-start(f32[1,128]{1,0:T(1,128)S(1)} %get-tuple-element.10.proj), channel_id=1, source_target_pairs={{0,1},{1,0},{2,3},{3,2},{4,5},{5,4},{6,7},{7,6},{8,9},{9,8},{10,11... | collective-permute-start | bytes 1544 | tf_op jit(solution)/shard_map/ppermute | solution.py:53
  (3 other events, 2.5 us)

commit v3 on v2

--- a/solution.py
+++ b/solution.py
@@ -9,6 +9,7 @@
 
 EPS = 1e-06
 LANES = 128
+PLACE = 3
 
 
 def ceil_to(n, m):
@@ -61,7 +62,29 @@
     return jnp.transpose(jnp.broadcast_to(row, (lanes, row.shape[1])))
 
 
-def norm_kernel(members, model_width, starts, rows, place, square, other, hidden, gain, *outs):
+def load_kernel(share, blocks, key, hidden, parcel, square, loaded, sems):
+    parts = key.shape[1] // LANES
+    at = 0
+    if share < key.shape[0]:
+        at = pl.multiple_of(lax.axis_index("gz") * share, share)
+    pairs = [(hidden, loaded), (blocks, parcel.at[pl.ds(parts * share, blocks.shape[0]), :])]
+    for c in range(parts):
+        part = key.at[pl.ds(at, share), c * LANES : (c + 1) * LANES]
+        pairs.append((part, parcel.at[c * share : (c + 1) * share, :]))
+    copies = [pltpu.make_async_copy(a, b, sems.at[i]) for i, (a, b) in enumerate(pairs)]
+    for copy in copies:
+        copy.start()
+    copies[0].wait()
+    total = jnp.zeros((hidden.shape[0], LANES), jnp.float32)
+    for c in range(0, hidden.shape[1], LANES):
+        value = loaded[:, c : c + LANES].astype(jnp.float32)
+        total = total + value * value
+    square[...] = jnp.sum(jnp.transpose(total), axis=0, keepdims=True)
+    for copy in copies[1:]:
+        copy.wait()
+
+
+def norm_kernel(members, model_width, starts, rows, meta, square, other, hidden, gain, *outs):
     tokens, features = hidden.shape
     total = square[...] + other[...]
     rstd = column(lax.rsqrt(total / model_width + EPS), LANES)
@@ -71,7 +94,7 @@
 
     aligned = rows % LANES == 0 and all(s == i * rows for i, s in enumerate(starts))
     for r, out in enumerate(outs):
-        member = members(place[0], r)
+        member = members(meta[0], r)
         if aligned:
             for at in range(0, rows, LANES):
                 cols = pl.ds(pl.multiple_of(member * rows + at, LANES), LANES)
@@ -100,23 +123,23 @@
         out[:, cols] = grad.astype(jnp.bfloat16)
 
 
-def input_grad_kernel(owner_of, most, counts, place, key, grad, hidden, gain, *refs):
+def input_grad_kernel(owner_of, most, meta, key, grad, hidden, gain, *refs):
     pieces, (scaled, proj, dense, starts) = refs[:-4], refs[-4:]
-    owners = counts.shape[0]
+    owners = meta.shape[0] - PLACE
 
     def mark(o, at):
         starts[o] = at
-        return at + counts[o]
+        return at + meta[PLACE + o]
 
     lax.fori_loop(0, owners, mark, jnp.int32(0))
     slot = lax.broadcasted_iota(jnp.int32, (most, LANES), 0)
     index = 0
     for piece in pieces:
         for i in range(piece.shape[0]):
-            owner = owner_of(place[0], place[1], index)
+            owner = owner_of(meta[0], meta[1], index)
             rows = pl.ds(starts[owner], most)
             new = piece[i].astype(jnp.float32)
-            dense[rows, :] = jnp.where(slot < counts[owner], new, dense[rows, :])
+            dense[rows, :] = jnp.where(slot < meta[PLACE + owner], new, dense[rows, :])
             index += 1
     tokens, features = hidden.shape
     parts = key.shape[1] // LANES
@@ -138,35 +161,46 @@
     proj[...] = jnp.sum(jnp.transpose(total), axis=0, keepdims=True)
 
 
-def weight_grad_kernel(inner, group_blocks, most, counts, place, *refs):
-    norms, keys = refs[: (len(refs) - 3) // 2], refs[(len(refs) - 3) // 2 : -3]
-    sent, kept, flat = refs[-3:]
+def weight_grad_kernel(sources, inner, group_blocks, most, meta, own, *refs):
+    sent, kept, flat, whole = refs[-4:]
+    pieces, norms = refs[: len(sources)], refs[len(sources) : -4]
+    tokens, width = own.shape
     rows = norms[0].shape[1]
-    parts = keys[0].shape[1] // LANES
+    parts = width // LANES
+    whole[:tokens, :] = own[...]
+    for (member, lot, share), piece in zip(sources, pieces):
+        offset = member(meta[2]) * share
+        for i, r in enumerate(lot):
+            for c in range(parts):
+                target = pl.ds(pl.multiple_of(r * tokens + offset, share), share)
+                whole[target, c * LANES : (c + 1) * LANES] = piece[i, c * share : (c + 1) * share, :]
     step = 256 if rows % 256 == 0 else rows
     for at in range(0, rows, step):
         total = None
-        for norm, key in zip(norms, keys):
+        for r, norm in enumerate(norms):
             part = lax.dot_general(
                 norm[:, at : at + step],
-                key[...],
+                whole[r * tokens : (r + 1) * tokens, :],
                 (((0,), (0,)), ((), ())),
                 preferred_element_type=jnp.float32,
             )
             total = part if total is None else total + part
         for c in range(parts):
             flat[pl.ds(at * parts + c, step, stride=parts), :] = total[:, c * LANES : (c + 1) * LANES]
-    outer_index, inner_index = place[0], place[1]
+    outer_index, inner_index = meta[0], meta[1]
+    slot = lax.broadcasted_iota(jnp.int32, (most, LANES), 0)
     lead = lax.rem(outer_index * group_blocks, parts)
     for k in range(inner):
         owner = inner_index ^ k
 
         def add(j, at):
-            return at + jnp.where(j < owner, counts[outer_index * inner + j], 0)
+            return at + jnp.where(j < owner, meta[PLACE + outer_index * inner + j], 0)
 
         start = lax.fori_loop(0, inner, add, lead)
         target = sent if k % 2 else kept
-        target[k // 2] = flat[pl.ds(start, most), :]
+        target[k // 2] = jnp.where(
+            slot < meta[PLACE + outer_index * inner + owner], flat[pl.ds(start, most), :], 0.0
+        )
 
 
 def shards(hidden_in, norm_gain, normed_grad, key_grad, weight_blocks, block_count):
@@ -179,14 +213,14 @@
     blocks = features * parts
     group_blocks = (blocks + outer - 1) // outer
     model_width = features * halves
-    gx, gy = lax.axis_index("gx"), lax.axis_index("gy")
-    counts = block_count[0]
-    place = jnp.stack([gx, gy]).astype(jnp.int32)
+    gx, gy, gz = (lax.axis_index(name) for name in ("gx", "gy", "gz"))
+    place = jnp.stack([gx, gy, gz]).astype(jnp.int32)
+    meta = jnp.concatenate([place, block_count[0]])
 
     smem = pl.BlockSpec(memory_space=pltpu.SMEM)
     vmem = pl.BlockSpec(memory_space=pltpu.VMEM)
 
-    def call(kernel, out_shape, scalars, arrays, scratch=(), megabytes=16):
+    def call(kernel, out_shape, scalars, arrays, scratch=(), megabytes=4):
         single = not isinstance(out_shape, tuple)
         return pl.pallas_call(
             kernel,
@@ -197,12 +231,36 @@
             compiler_params=pltpu.CompilerParams(vmem_limit_bytes=megabytes << 20),
         )(*scalars, *arrays)
 
-    found = gather_relatives(weight_blocks.reshape(most, LANES), "gx", outer)
+    share = tokens // halves
+    split = halves > 1 and tokens % halves == 0 and share % 16 == 0
+    share = share if split else tokens
+    head = share * parts
+    hbm = pl.BlockSpec(memory_space=pltpu.HBM)
+    parcel, square = pl.pallas_call(
+        functools.partial(load_kernel, share),
+        name="load",
+        out_shape=(
+            jax.ShapeDtypeStruct((head + most, LANES), jnp.bfloat16),
+            jax.ShapeDtypeStruct((1, tokens), jnp.float32),
+        ),
+        in_specs=[hbm] * 3,
+        out_specs=(vmem, vmem),
+        scratch_shapes=[
+            pltpu.VMEM((tokens, features), jnp.bfloat16),
+            pltpu.SemaphoreType.DMA((parts + 2,)),
+        ],
+        compiler_params=pltpu.CompilerParams(vmem_limit_bytes=60 << 20),
+    )(weight_blocks.reshape(most, LANES), key_grad, hidden_in)
+    hidden, gain = hidden_in, norm_gain[None, :]
+    found = gather_relatives(parcel, "gx", outer)
     order = list(found)
-    lots = [order[: len(order) // 2], order[len(order) // 2 :]]
+    lots = [lot for lot in (order[:1], order[1:-1], order[-1:]) if lot]
+    lots = lots if outer > 1 else [order]
+
     pieces, names = [], []
-    for lot in lots:
-        spread = {0: jnp.stack([found[r] for r in lot])}
+    for lot_index, lot in enumerate(lots):
+        own = weight_blocks.reshape(1, most, LANES)
+        spread = {0: jnp.stack([found[r][head:] for r in lot]) if lot_index else own}
         bit = inner // 2
         while bit:
             for r in list(spread):
@@ -215,10 +273,7 @@
         r, s = names[index]
         return relative_index(outer, i, r) * inner + (j ^ s)
 
-    hfloat = hidden_in.astype(jnp.float32)
-    square = jnp.sum(hfloat * hfloat, axis=1)
-    squares = [t[None, :] for t in axis_terms(square, "gz", halves)]
-    gain = norm_gain[None, :]
+    squares = axis_terms(square, "gz", halves)
 
     starts = [i * group_blocks // parts for i in range(outer)]
     rows = max(
@@ -232,10 +287,20 @@
     windows = call(
         functools.partial(norm_kernel, target, model_width, starts, rows),
         (window,) * outer,
-        [place],
-        [*squares, hidden_in, gain],
-    )
-    keys = gather_relatives(key_grad, "gx", outer)
+        [meta],
+        [*squares, hidden, gain],
+    )
+
+    sources, key_pieces = [], []
+    for r in order[1:]:
+        member = functools.partial(relative_index, halves, r=0) if split else (lambda i: 0)
+        sources.append((member, [r], share))
+        key_pieces.append(found[r][None])
+    for lot in [order[1:-1], order[-1:]] if split and outer > 1 else []:
+        stack = jnp.stack([found[r][:head] for r in lot])
+        for s in range(1, halves):
+            sources.append((functools.partial(relative_index, halves, r=s), lot, share))
+            key_pieces.append(lax.ppermute(stack, "gz", relative(halves, s)))
     norms = [windows[0]]
     for r in range(1, outer):
         norms.append(lax.ppermute(windows[r], "gx", relative(outer, r)))
@@ -246,28 +311,32 @@
             jax.ShapeDtypeStruct((tokens, features), jnp.float32),
             jax.ShapeDtypeStruct((1, tokens), jnp.float32),
         ),
-        [counts, place],
-        [key_grad, normed_grad, hidden_in, gain, *pieces],
+        [meta],
+        [key_grad, normed_grad, hidden, gain, *pieces],
         [
             pltpu.VMEM((ceil_to(blocks + most, 8), LANES), jnp.float32),
             pltpu.SMEM((owners,), jnp.int32),
         ],
+        megabytes=8,
     )
     projs = axis_terms(proj, "gz", halves)
     hidden_grad = call(
         functools.partial(finish_kernel, model_width),
         jax.ShapeDtypeStruct((tokens, features), jnp.bfloat16),
         [],
-        [*squares, *projs, scaled, hidden_in],
+        [*squares, *projs, scaled, hidden],
     )
 
     half = jax.ShapeDtypeStruct((inner // 2, most, LANES), jnp.float32)
     sent, kept = call(
-        functools.partial(weight_grad_kernel, inner, group_blocks, most),
+        functools.partial(weight_grad_kernel, sources, inner, group_blocks, most),
         (half, half),
-        [counts, place],
-        [*norms, *[keys[r] for r in range(outer)]],
-        [pltpu.VMEM((ceil_to(rows * parts + most, 8), LANES), jnp.float32)],
+        [meta],
+        [key_grad, *key_pieces, *norms],
+        [
+            pltpu.VMEM((ceil_to(rows * parts + most, 8), LANES), jnp.float32),
+            pltpu.VMEM((outer * tokens, width), jnp.bfloat16),
+        ],
     )
     bit = 1
     while True:
@@ -277,9 +346,6 @@
             break
         sent, kept = kept[1::2] + got[1::2], kept[0::2] + got[0::2]
     owned = (kept + got)[0]
-    count = lax.dynamic_index_in_dim(counts, gx * inner + gy, 0, keepdims=False)
-    slots = lax.broadcasted_iota(jnp.int32, (most, LANES), 0)
-    owned = jnp.where(slots < count, owned, jnp.float32(0.0))
     return (hidden_grad, owned.reshape(1, 1, most, LANES))
 
 

time: 61.3 us -> 59.8 us (0.976)
  other arithmetic: 4.54 us -> 0.9 us
  Pallas kernels: 6.28 us -> 7.88 us
  waiting for transfers between devices: 24.6 us -> 26.1 us
  local copies, waits for them, and re-layouts: 2.07 us -> 0.75 us
    ppermute x3, waiting for transfers between devices: 7.73 us -> 0.01 us  [shards(): norms.append(lax.ppermute(windows[r], 'gx', relative(outer, r)))]
    ppermute x6 -> x9, waiting for transfers between devices: 6.16 us -> 11 us  [shards(): spread[r ^ bit] = lax.ppermute(spread[r], 'gy', relative(inner, bit))]
    ppermute x6 -> x3, starting transfers between devices: 10 us -> 6.19 us  [gather_relatives(): known[r ^ basis] = lax.ppermute(known[r], axis, relative(n, basis))]
    ppermute x6 -> x3, waiting for transfers between devices: 7.3 us -> 10.6 us  [gather_relatives(): known[r ^ basis] = lax.ppermute(known[r], axis, relative(n, basis))]
    ppermute x0 -> x2, starting transfers between devices: none -> 3.17 us  [shards(): key_pieces.append(lax.ppermute(stack, 'gz', relative(halves, s)))]
    pallas_call x0 -> x1, Pallas kernels: none -> 2.03 us  [shards(): pl.pallas_call(functools.partial(load_kernel, share), name='load', out_sh...]
    ppermute x6 -> x9, starting transfers between devices: 3.63 us -> 5.55 us  [shards(): spread[r ^ bit] = lax.ppermute(spread[r], 'gy', relative(inner, bit))]
    select_n x1 -> x0, other arithmetic: 1.81 us -> none  [shards(): owned = jnp.where(slots < count, owned, jnp.float32(0.0))]
  transfers between devices with their start and end apart: 19 -> 21, of which waited for: 8 -> 8; matrix products, arithmetic and copies ran while one was open for 5% -> 0% of each run, Pallas kernels for 10% -> 10%
where the time goes in v3:
time: 59.8 us; the launch traced here: 59.7 us
  waiting for transfers between devices  26.1 us (44%)
  starting transfers between devices  23.2 us (39%)
  Pallas kernels  7.88 us (13%)
  other arithmetic  0.9 us (2%)
  between operations  0.79 us (1%)
  local copies, waits for them, and re-layouts  0.75 us (1%)
    ppermute x9, waiting for transfers between devices, shards(): spread[r ^ bit] = lax.ppermute(spread[r], 'gy', relative(inner, bit))  11 us
    ppermute x3, waiting for transfers between devices, gather_relatives(): known[r ^ basis] = lax.ppermute(known[r], axis, relative(n, basis))  10.6 us
    ppermute x3, starting transfers between devices, gather_relatives(): known[r ^ basis] = lax.ppermute(known[r], axis, relative(n, basis))  6.19 us
    pallas_call x4, Pallas kernels, call(): pl.pallas_call(kernel, out_shape=out_shape, in_specs=[smem] * len(scalars...  5.86 us
    ppermute x9, starting transfers between devices, shards(): spread[r ^ bit] = lax.ppermute(spread[r], 'gy', relative(inner, bit))  5.55 us
    ppermute x3, starting transfers between devices, shards(): norms.append(lax.ppermute(windows[r], 'gx', relative(outer, r)))  4.53 us
    ppermute x2, waiting for transfers between devices, axis_terms(): lax.ppermute(x, axis, relative(n, bit))  3.37 us
    ppermute x2, starting transfers between devices, shards(): key_pieces.append(lax.ppermute(stack, 'gz', relative(halves, s)))  3.17 us
  transfers between devices with their start and end apart: 21, of which 8 were waited for; matrix products, arithmetic and copies ran while one was open for 0% of the time, Pallas kernels for 10%

profile of v3, /device:TPU:0, one launch (start us, length us, event | category | flops | bytes accessed | tf_op | source)
XLA Modules:
  0.0 59.7 jit_solution(10315985473145780690)
XLA Ops:
  0.6 2.0 %load.1 = (bf16[776,128]{1,0:T(8,128)(2,1)}, f32[1,128]{1,0:T(1,128)}) custom-call(bf16[520,128]{1,0:T(8,128)(2,1)} %bitcast.27, bf16[128,512]{1,0:T(8,128)(2,1)} %own.1, bf16[128,2048]{1,0:T(8,128)(2,1)} %hidden.7), custom_call_target="tpu_custom_call" | custom-call | tf_op jit(solution)/shard_map/load/pallas_call | solution.py:239
  2.7 5.1 %collective-permute-start.4 = (bf16[776,128]{1,0:T(8,128)(2,1)}, bf16[776,128]{1,0:T(8,128)(2,1)S(1)}, u32[]{:S(2)}, u32[]{:S(2)}) collective-permute-start(bf16[776,128]{1,0:T(8,128)(2,1)} %get-tuple-element.13), channel_id=1, source_target_pairs={{0,24},{8,16},{16,8},{24,0},{1,25},{9,17},{17,9},{25,1},{2,26},{10... | collective-permute-start | bytes 595976 | tf_op jit(solution)/shard_map/ppermute | solution.py:41
  7.8 1.5 %collective-permute-start = (f32[1,128]{1,0:T(1,128)S(1)}, f32[1,128]{1,0:T(1,128)S(1)}, u32[]{:S(2)}, u32[]{:S(2)}) collective-permute-start(f32[1,128]{1,0:T(1,128)S(1)} %copy-done.5), channel_id=1, source_target_pairs={{0,1},{1,0},{2,3},{3,2},{4,5},{5,4},{6,7},{7,6},{8,9},{9,8},{10,11... | collective-permute-start | bytes 1544 | tf_op jit(solution)/shard_map/ppermute | solution.py:54
  10.1 1.3 %collective-permute-done.other = f32[1,128]{1,0:T(1,128)S(1)} collective-permute-done((f32[1,128]{1,0:T(1,128)S(1)}, f32[1,128]{1,0:T(1,128)S(1)}, u32[]{:S(2)}, u32[]{:S(2)}) %collective-permute-start) | collective-permute-done | bytes 544 | tf_op jit(solution)/shard_map/ppermute | solution.py:54
  11.4 0.8 %shard_map.79 = (bf16[128,512]{1,0:T(8,128)(2,1)S(1)}, bf16[128,512]{1,0:T(8,128)(2,1)S(1)}, bf16[128,512]{1,0:T(8,128)(2,1)S(1)}, bf16[128,512]{1,0:T(8,128)(2,1)S(1)}) custom-call(s32[19]{0:T(128)S(1)} %pad_add_fusion.meta, f32[1,128]{1,0:T(1,128)S(1)} %copy-done.5, f32[1,128]{1,0:T(1,128)S(1)} %collective-permute-done.other, ...), custom_call_target="tpu_custom_call" | custom-call | tf_op jit(solution)/shard_map/pallas_call | solution.py:225
  12.2 2.1 %collective-permute-start.16 = (bf16[128,512]{1,0:T(8,128)(2,1)S(1)}, bf16[128,512]{1,0:T(8,128)(2,1)S(1)}, u32[]{:S(2)}, u32[]{:S(2)}) collective-permute-start(bf16[128,512]{1,0:T(8,128)(2,1)S(1)} %get-tuple-element.17), channel_id=1, source_target_pairs={{0,8},{8,0},{16,24},{24,16},{1,9},{9,1},{17,25},{25,17},{2,10},{10... | collective-permute-start | bytes 393224 | tf_op jit(solution)/shard_map/ppermute | solution.py:306
  14.3 2.4 %collective-permute-start.18 = (bf16[128,512]{1,0:T(8,128)(2,1)S(1)}, bf16[128,512]{1,0:T(8,128)(2,1)S(1)}, u32[]{:S(2)}, u32[]{:S(2)}) collective-permute-start(bf16[128,512]{1,0:T(8,128)(2,1)S(1)} %get-tuple-element.19), channel_id=1, source_target_pairs={{0,24},{8,16},{16,8},{24,0},{1,25},{9,17},{17,9},{25,1},{2,26},{10... | collective-permute-start | bytes 393224 | tf_op jit(solution)/shard_map/ppermute | solution.py:306
  16.7 1.0 %collective-permute-start.9 = (bf16[776,128]{1,0:T(8,128)(2,1)S(1)}, bf16[776,128]{1,0:T(8,128)(2,1)S(1)}, u32[]{:S(2)}, u32[]{:S(2)}) collective-permute-start(bf16[776,128]{1,0:T(8,128)(2,1)S(1)} %collective-permute-done.4), channel_id=1, source_target_pairs={{0,8},{8,0},{16,24},{24,16},{1,9},{9,1},{17,25},{25,17},{2,10},{10... | collective-permute-start | bytes 595976 | tf_op jit(solution)/shard_map/ppermute | solution.py:41
  17.8 1.1 %collective-permute-done.5 = bf16[776,128]{1,0:T(8,128)(2,1)S(1)} collective-permute-done((bf16[776,128]{1,0:T(8,128)(2,1)}, bf16[776,128]{1,0:T(8,128)(2,1)S(1)}, u32[]{:S(2)}, u32[]{:S(2)}) %collective-permute-start.5) | collective-permute-done | bytes 198688 | tf_op jit(solution)/shard_map/ppermute | solution.py:41
  18.9 1.6 %collective-permute-start.14 = (bf16[2,256,128]{2,1,0:T(8,128)(2,1)S(1)}, bf16[2,256,128]{2,1,0:T(8,128)(2,1)S(1)}, u32[]{:S(2)}, u32[]{:S(2)}) collective-permute-start(bf16[2,256,128]{2,1,0:T(8,128)(2,1)S(1)} %pad_maximum_fusion.1), channel_id=1, source_target_pairs={{0,1},{1,0},{2,3},{3,2},{4,5},{5,4},{6,7},{7,6},{8,9},{9,8},{10,11... | collective-permute-start | bytes 393224 | tf_op jit(solution)/shard_map/ppermute | solution.py:303
  20.5 9.5 %collective-permute-done.9 = bf16[776,128]{1,0:T(8,128)(2,1)S(1)} collective-permute-done((bf16[776,128]{1,0:T(8,128)(2,1)S(1)}, bf16[776,128]{1,0:T(8,128)(2,1)S(1)}, u32[]{:S(2)}, u32[]{:S(2)}) %collective-permute-start.9) | collective-permute-done | bytes 198688 | tf_op jit(solution)/shard_map/ppermute | solution.py:41
  30.0 1.6 %collective-permute-start.15 = (bf16[1,256,128]{2,1,0:T(8,128)(2,1)S(1)}, bf16[1,256,128]{2,1,0:T(8,128)(2,1)S(1)}, u32[]{:S(2)}, u32[]{:S(2)}) collective-permute-start(bf16[1,256,128]{2,1,0:T(8,128)(2,1)S(1)} %slice_bitcast_fusion.3), channel_id=1, source_target_pairs={{0,1},{1,0},{2,3},{3,2},{4,5},{5,4},{6,7},{7,6},{8,9},{9,8},{10,11... | collective-permute-start | bytes 196616 | tf_op jit(solution)/shard_map/ppermute | solution.py:303
  31.7 1.6 %collective-permute-start.1 = (bf16[1,520,128]{2,1,0:T(8,128)(2,1)S(1)}, bf16[1,520,128]{2,1,0:T(8,128)(2,1)S(1)}, u32[]{:S(2)}, u32[]{:S(2)}) collective-permute-start(bf16[1,520,128]{2,1,0:T(8,128)(2,1)S(1)} %bitcast.28), channel_id=1, source_target_pairs={{0,4},{2,6},{4,0},{6,2},{1,5},{3,7},{5,1},{7,3},{8,12},{10,14},{12... | collective-permute-start | bytes 399368 | tf_op jit(solution)/shard_map/ppermute | solution.py:267
  33.2 1.1 %collective-permute-done.15.refs_4_ = bf16[1,256,128]{2,1,0:T(8,128)(2,1)S(1)} collective-permute-done((bf16[1,256,128]{2,1,0:T(8,128)(2,1)S(1)}, bf16[1,256,128]{2,1,0:T(8,128)(2,1)S(1)}, u32[]{:S(2)}, u32[]{:S(2)}) %collective-permute-start.15) | collective-permute-done | bytes 65568 | tf_op jit(solution)/shard_map/ppermute | solution.py:303
  34.4 1.5 %shard_map.80 = (f32[2,520,128]{2,1,0:T(8,128)S(1)}, f32[2,520,128]{2,1,0:T(8,128)S(1)}) custom-call(s32[19]{0:T(128)S(1)} %pad_add_fusion.meta, bf16[128,512]{1,0:T(8,128)(2,1)S(1)} %copy-done.1, bf16[1,776,128]{2,1,0:T(8,128)(2,1)S(1)} %bitcast.25, bf16[1,776,128]{2,1,0:T(8,128)(2,1)S(1)} %bitcast.24, bf16[1,776,128]{2,1,0:T(8,128)(2,1)S(1)} %bitcast.26, ...), custom_call_target="tpu_custom_call" | custom-call | tf_op jit(solution)/shard_map/pallas_call | solution.py:225
  36.0 1.6 %collective-permute-start.6 = (bf16[2,520,128]{2,1,0:T(8,128)(2,1)S(1)}, bf16[2,520,128]{2,1,0:T(8,128)(2,1)S(1)}, u32[]{:S(2)}, u32[]{:S(2)}) collective-permute-start(bf16[2,520,128]{2,1,0:T(8,128)(2,1)S(1)} %pad_maximum_fusion.refs_4_), channel_id=1, source_target_pairs={{0,4},{2,6},{4,0},{6,2},{1,5},{3,7},{5,1},{7,3},{8,12},{10,14},{12... | collective-permute-start | bytes 798728 | tf_op jit(solution)/shard_map/ppermute | solution.py:267
  38.3 6.6 %collective-permute-done.6.refs_5_ = bf16[2,520,128]{2,1,0:T(8,128)(2,1)S(1)} collective-permute-done((bf16[2,520,128]{2,1,0:T(8,128)(2,1)S(1)}, bf16[2,520,128]{2,1,0:T(8,128)(2,1)S(1)}, u32[]{:S(2)}, u32[]{:S(2)}) %collective-permute-start.6) | collective-permute-done | bytes 266272 | tf_op jit(solution)/shard_map/ppermute | solution.py:267
  44.9 1.5 %collective-permute-start.10 = (bf16[1,520,128]{2,1,0:T(8,128)(2,1)S(1)}, bf16[1,520,128]{2,1,0:T(8,128)(2,1)S(1)}, u32[]{:S(2)}, u32[]{:S(2)}) collective-permute-start(bf16[1,520,128]{2,1,0:T(8,128)(2,1)S(1)} %slice_bitcast_fusion.refs_8_), channel_id=1, source_target_pairs={{0,4},{2,6},{4,0},{6,2},{1,5},{3,7},{5,1},{7,3},{8,12},{10,14},{12... | collective-permute-start | bytes 399368 | tf_op jit(solution)/shard_map/ppermute | solution.py:267
  47.3 3.1 %collective-permute-done.10.refs_9_ = bf16[1,520,128]{2,1,0:T(8,128)(2,1)S(1)} collective-permute-done((bf16[1,520,128]{2,1,0:T(8,128)(2,1)S(1)}, bf16[1,520,128]{2,1,0:T(8,128)(2,1)S(1)}, u32[]{:S(2)}, u32[]{:S(2)}) %collective-permute-start.10) | collective-permute-done | bytes 133152 | tf_op jit(solution)/shard_map/ppermute | solution.py:267
  50.4 1.3 %collective-permute-done.12.refs_11_ = bf16[1,520,128]{2,1,0:T(8,128)(2,1)S(1)} collective-permute-done((bf16[1,520,128]{2,1,0:T(8,128)(2,1)S(1)}, bf16[1,520,128]{2,1,0:T(8,128)(2,1)S(1)}, u32[]{:S(2)}, u32[]{:S(2)}) %collective-permute-start.12) | collective-permute-done | bytes 133152 | tf_op jit(solution)/shard_map/ppermute | solution.py:267
  51.7 2.5 %shard_map.77 = (f32[128,2048]{1,0:T(8,128)S(1)}, f32[1,128]{1,0:T(1,128)S(1)}) custom-call(s32[19]{0:T(128)S(1)} %pad_add_fusion.meta, bf16[128,512]{1,0:T(8,128)(2,1)S(1)} %copy-done.1, bf16[128,2048]{1,0:T(8,128)(2,1)S(1)} %copy-done.3, bf16[128,2048]{1,0:T(8,128)(2,1)S(1)} %copy-done, f32[1,2048]{1,0:T(1,128)S(1)} %bitcast.32, ...), custom_call_target="tpu_custom_call" | custom-call | tf_op jit(solution)/shard_map/pallas_call | solution.py:225
  54.2 1.6 %collective-permute-start.13 = (f32[1,128]{1,0:T(1,128)S(1)}, f32[1,128]{1,0:T(1,128)S(1)}, u32[]{:S(2)}, u32[]{:S(2)}) collective-permute-start(f32[1,128]{1,0:T(1,128)S(1)} %get-tuple-element.14.proj), channel_id=1, source_target_pairs={{0,1},{1,0},{2,3},{3,2},{4,5},{5,4},{6,7},{7,6},{8,9},{9,8},{10,11... | collective-permute-start | bytes 1544 | tf_op jit(solution)/shard_map/ppermute | solution.py:54
  55.8 2.1 %collective-permute-done.13.proj_other = f32[1,128]{1,0:T(1,128)S(1)} collective-permute-done((f32[1,128]{1,0:T(1,128)S(1)}, f32[1,128]{1,0:T(1,128)S(1)}, u32[]{:S(2)}, u32[]{:S(2)}) %collective-permute-start.13) | collective-permute-done | bytes 544 | tf_op jit(solution)/shard_map/ppermute | solution.py:54
  57.8 1.1 %shard_map.78 = bf16[128,2048]{1,0:T(8,128)(2,1)} custom-call(f32[1,128]{1,0:T(1,128)S(1)} %copy-done.5, f32[1,128]{1,0:T(1,128)S(1)} %collective-permute-done.other, f32[1,128]{1,0:T(1,128)S(1)} %get-tuple-element.14.proj, f32[1,128]{1,0:T(1,128)S(1)} %collective-permute-done.13.proj_other, f32[128,2048]{1,0:T(8,128)S(1)} %get-tuple-element.15.scaled, ...), custom_call_target="tpu_custom_call" | custom-call | tf_op jit(solution)/shard_map/pallas_call | solution.py:225
  (48 shorter events, 3.3 us)
Async XLA Ops:
  0.6 10.8 %copy-start = (bf16[128,2048]{1,0:T(8,128)(2,1)S(1)}, bf16[128,2048]{1,0:T(8,128)(2,1)}, u32[]{:S(2)}) copy-start(bf16[128,2048]{1,0:T(8,128)(2,1)} %hidden.7) | copy-start | bytes 1572868
  2.7 5.2 %copy-start.5 = (f32[1,128]{1,0:T(1,128)S(1)}, f32[1,128]{1,0:T(1,128)}, u32[]{:S(2)}) copy-start(f32[1,128]{1,0:T(1,128)} %get-tuple-element.12.square) | copy-start | bytes 1540
  2.7 14.1 %collective-permute-start.4 = (bf16[776,128]{1,0:T(8,128)(2,1)}, bf16[776,128]{1,0:T(8,128)(2,1)S(1)}, u32[]{:S(2)}, u32[]{:S(2)}) collective-permute-start(bf16[776,128]{1,0:T(8,128)(2,1)} %get-tuple-element.13), channel_id=1, source_target_pairs={{0,24},{8,16},{16,8},{24,0},{1,25},{9,17},{17,9},{25,1},{2,26},{10... | collective-permute-start | bytes 595976 | tf_op jit(solution)/shard_map/ppermute | solution.py:41
  7.8 11.1 %collective-permute-start.5 = (bf16[776,128]{1,0:T(8,128)(2,1)}, bf16[776,128]{1,0:T(8,128)(2,1)S(1)}, u32[]{:S(2)}, u32[]{:S(2)}) collective-permute-start(bf16[776,128]{1,0:T(8,128)(2,1)} %get-tuple-element.13), channel_id=1, source_target_pairs={{0,8},{8,0},{16,24},{24,16},{1,9},{9,1},{17,25},{25,17},{2,10},{10... | collective-permute-start | bytes 595976 | tf_op jit(solution)/shard_map/ppermute | solution.py:41
  7.8 3.6 %collective-permute-start = (f32[1,128]{1,0:T(1,128)S(1)}, f32[1,128]{1,0:T(1,128)S(1)}, u32[]{:S(2)}, u32[]{:S(2)}) collective-permute-start(f32[1,128]{1,0:T(1,128)S(1)} %copy-done.5), channel_id=1, source_target_pairs={{0,1},{1,0},{2,3},{3,2},{4,5},{5,4},{6,7},{7,6},{8,9},{9,8},{10,11... | collective-permute-start | bytes 1544 | tf_op jit(solution)/shard_map/ppermute | solution.py:54
  12.2 19.4 %collective-permute-start.16 = (bf16[128,512]{1,0:T(8,128)(2,1)S(1)}, bf16[128,512]{1,0:T(8,128)(2,1)S(1)}, u32[]{:S(2)}, u32[]{:S(2)}) collective-permute-start(bf16[128,512]{1,0:T(8,128)(2,1)S(1)} %get-tuple-element.17), channel_id=1, source_target_pairs={{0,8},{8,0},{16,24},{24,16},{1,9},{9,1},{17,25},{25,17},{2,10},{10... | collective-permute-start | bytes 393224 | tf_op jit(solution)/shard_map/ppermute | solution.py:306
  14.3 18.9 %collective-permute-start.17 = (bf16[128,512]{1,0:T(8,128)(2,1)S(1)}, bf16[128,512]{1,0:T(8,128)(2,1)S(1)}, u32[]{:S(2)}, u32[]{:S(2)}) collective-permute-start(bf16[128,512]{1,0:T(8,128)(2,1)S(1)} %get-tuple-element.18), channel_id=1, source_target_pairs={{0,16},{8,24},{16,0},{24,8},{1,17},{9,25},{17,1},{25,9},{2,18},{10... | collective-permute-start | bytes 393224 | tf_op jit(solution)/shard_map/ppermute | solution.py:306
  14.3 18.9 %collective-permute-start.18 = (bf16[128,512]{1,0:T(8,128)(2,1)S(1)}, bf16[128,512]{1,0:T(8,128)(2,1)S(1)}, u32[]{:S(2)}, u32[]{:S(2)}) collective-permute-start(bf16[128,512]{1,0:T(8,128)(2,1)S(1)} %get-tuple-element.19), channel_id=1, source_target_pairs={{0,24},{8,16},{16,8},{24,0},{1,25},{9,17},{17,9},{25,1},{2,26},{10... | collective-permute-start | bytes 393224 | tf_op jit(solution)/shard_map/ppermute | solution.py:306
  16.7 13.3 %collective-permute-start.9 = (bf16[776,128]{1,0:T(8,128)(2,1)S(1)}, bf16[776,128]{1,0:T(8,128)(2,1)S(1)}, u32[]{:S(2)}, u32[]{:S(2)}) collective-permute-start(bf16[776,128]{1,0:T(8,128)(2,1)S(1)} %collective-permute-done.4), channel_id=1, source_target_pairs={{0,8},{8,0},{16,24},{24,16},{1,9},{9,1},{17,25},{25,17},{2,10},{10... | collective-permute-start | bytes 595976 | tf_op jit(solution)/shard_map/ppermute | solution.py:41
  18.9 14.3 %collective-permute-start.14 = (bf16[2,256,128]{2,1,0:T(8,128)(2,1)S(1)}, bf16[2,256,128]{2,1,0:T(8,128)(2,1)S(1)}, u32[]{:S(2)}, u32[]{:S(2)}) collective-permute-start(bf16[2,256,128]{2,1,0:T(8,128)(2,1)S(1)} %pad_maximum_fusion.1), channel_id=1, source_target_pairs={{0,1},{1,0},{2,3},{3,2},{4,5},{5,4},{6,7},{7,6},{8,9},{9,8},{10,11... | collective-permute-start | bytes 393224 | tf_op jit(solution)/shard_map/ppermute | solution.py:303
  30.0 4.3 %collective-permute-start.15 = (bf16[1,256,128]{2,1,0:T(8,128)(2,1)S(1)}, bf16[1,256,128]{2,1,0:T(8,128)(2,1)S(1)}, u32[]{:S(2)}, u32[]{:S(2)}) collective-permute-start(bf16[1,256,128]{2,1,0:T(8,128)(2,1)S(1)} %slice_bitcast_fusion.3), channel_id=1, source_target_pairs={{0,1},{1,0},{2,3},{3,2},{4,5},{5,4},{6,7},{7,6},{8,9},{9,8},{10,11... | collective-permute-start | bytes 196616 | tf_op jit(solution)/shard_map/ppermute | solution.py:303
  31.7 6.1 %collective-permute-start.1 = (bf16[1,520,128]{2,1,0:T(8,128)(2,1)S(1)}, bf16[1,520,128]{2,1,0:T(8,128)(2,1)S(1)}, u32[]{:S(2)}, u32[]{:S(2)}) collective-permute-start(bf16[1,520,128]{2,1,0:T(8,128)(2,1)S(1)} %bitcast.28), channel_id=1, source_target_pairs={{0,4},{2,6},{4,0},{6,2},{1,5},{3,7},{5,1},{7,3},{8,12},{10,14},{12... | collective-permute-start | bytes 399368 | tf_op jit(solution)/shard_map/ppermute | solution.py:267
  35.9 10.5 %collective-permute-start.19 = (f32[2,520,128]{2,1,0:T(8,128)S(1)}, f32[2,520,128]{2,1,0:T(8,128)S(1)}, u32[]{:S(2)}, u32[]{:S(2)}) collective-permute-start(f32[2,520,128]{2,1,0:T(8,128)S(1)} %get-tuple-element.21), channel_id=1, source_target_pairs={{0,2},{2,0},{4,6},{6,4},{1,3},{3,1},{5,7},{7,5},{8,10},{10,8},{12,... | collective-permute-start | bytes 1597448 | tf_op jit(solution)/shard_map/ppermute | solution.py:343
  36.0 15.7 %copy-start.3 = (bf16[128,2048]{1,0:T(8,128)(2,1)S(1)}, bf16[128,2048]{1,0:T(8,128)(2,1)}, u32[]{:S(2)}) copy-start(bf16[128,2048]{1,0:T(8,128)(2,1)} %grad.1) | copy-start | bytes 1572868
  36.0 8.9 %collective-permute-start.6 = (bf16[2,520,128]{2,1,0:T(8,128)(2,1)S(1)}, bf16[2,520,128]{2,1,0:T(8,128)(2,1)S(1)}, u32[]{:S(2)}, u32[]{:S(2)}) collective-permute-start(bf16[2,520,128]{2,1,0:T(8,128)(2,1)S(1)} %pad_maximum_fusion.refs_4_), channel_id=1, source_target_pairs={{0,4},{2,6},{4,0},{6,2},{1,5},{3,7},{5,1},{7,3},{8,12},{10,14},{12... | collective-permute-start | bytes 798728 | tf_op jit(solution)/shard_map/ppermute | solution.py:267
  37.6 8.8 %collective-permute-start.2 = (bf16[1,520,128]{2,1,0:T(8,128)(2,1)S(1)}, bf16[1,520,128]{2,1,0:T(8,128)(2,1)S(1)}, u32[]{:S(2)}, u32[]{:S(2)}) collective-permute-start(bf16[1,520,128]{2,1,0:T(8,128)(2,1)S(1)} %bitcast.29), channel_id=1, source_target_pairs={{0,2},{2,0},{4,6},{6,4},{1,3},{3,1},{5,7},{7,5},{8,10},{10,8},{12,... | collective-permute-start | bytes 399368 | tf_op jit(solution)/shard_map/ppermute | solution.py:267
  37.8 9.2 %collective-permute-start.3 = (bf16[1,520,128]{2,1,0:T(8,128)(2,1)S(1)}, bf16[1,520,128]{2,1,0:T(8,128)(2,1)S(1)}, u32[]{:S(2)}, u32[]{:S(2)}) collective-permute-start(bf16[1,520,128]{2,1,0:T(8,128)(2,1)S(1)} %collective-permute-done.1.refs_1_), channel_id=1, source_target_pairs={{0,2},{2,0},{4,6},{6,4},{1,3},{3,1},{5,7},{7,5},{8,10},{10,8},{12,... | collective-permute-start | bytes 399368 | tf_op jit(solution)/shard_map/ppermute | solution.py:267
  38.1 12.2 %collective-permute-start.7 = (bf16[2,520,128]{2,1,0:T(8,128)(2,1)S(1)}, bf16[2,520,128]{2,1,0:T(8,128)(2,1)S(1)}, u32[]{:S(2)}, u32[]{:S(2)}) collective-permute-start(bf16[2,520,128]{2,1,0:T(8,128)(2,1)S(1)} %pad_maximum_fusion.refs_4_), channel_id=1, source_target_pairs={{0,2},{2,0},{4,6},{6,4},{1,3},{3,1},{5,7},{7,5},{8,10},{10,8},{12,... | collective-permute-start | bytes 798728 | tf_op jit(solution)/shard_map/ppermute | solution.py:267
  44.9 5.5 %collective-permute-start.10 = (bf16[1,520,128]{2,1,0:T(8,128)(2,1)S(1)}, bf16[1,520,128]{2,1,0:T(8,128)(2,1)S(1)}, u32[]{:S(2)}, u32[]{:S(2)}) collective-permute-start(bf16[1,520,128]{2,1,0:T(8,128)(2,1)S(1)} %slice_bitcast_fusion.refs_8_), channel_id=1, source_target_pairs={{0,4},{2,6},{4,0},{6,2},{1,5},{3,7},{5,1},{7,3},{8,12},{10,14},{12... | collective-permute-start | bytes 399368 | tf_op jit(solution)/shard_map/ppermute | solution.py:267
  46.4 5.3 %collective-permute-start.8 = (bf16[2,520,128]{2,1,0:T(8,128)(2,1)S(1)}, bf16[2,520,128]{2,1,0:T(8,128)(2,1)S(1)}, u32[]{:S(2)}, u32[]{:S(2)}) collective-permute-start(bf16[2,520,128]{2,1,0:T(8,128)(2,1)S(1)} %collective-permute-done.6.refs_5_), channel_id=1, source_target_pairs={{0,2},{2,0},{4,6},{6,4},{1,3},{3,1},{5,7},{7,5},{8,10},{10,8},{12,... | collective-permute-start | bytes 798728 | tf_op jit(solution)/shard_map/ppermute | solution.py:267
  46.4 12.5 %collective-permute-start.20 = (f32[1,520,128]{2,1,0:T(8,128)S(1)}, f32[1,520,128]{2,1,0:T(8,128)S(1)}, u32[]{:S(2)}, u32[]{:S(2)}) collective-permute-start(f32[1,520,128]{2,1,0:T(8,128)S(1)} %slice_add_fusion), channel_id=1, source_target_pairs={{0,4},{2,6},{4,0},{6,2},{1,5},{3,7},{5,1},{7,3},{8,12},{10,14},{12... | collective-permute-start | bytes 798728 | tf_op jit(solution)/shard_map/ppermute | solution.py:343
  47.0 3.3 %collective-permute-start.11 = (bf16[1,520,128]{2,1,0:T(8,128)(2,1)S(1)}, bf16[1,520,128]{2,1,0:T(8,128)(2,1)S(1)}, u32[]{:S(2)}, u32[]{:S(2)}) collective-permute-start(bf16[1,520,128]{2,1,0:T(8,128)(2,1)S(1)} %slice_bitcast_fusion.refs_8_), channel_id=1, source_target_pairs={{0,2},{2,0},{4,6},{6,4},{1,3},{3,1},{5,7},{7,5},{8,10},{10,8},{12,... | collective-permute-start | bytes 399368 | tf_op jit(solution)/shard_map/ppermute | solution.py:267
  50.3 1.4 %collective-permute-start.12 = (bf16[1,520,128]{2,1,0:T(8,128)(2,1)S(1)}, bf16[1,520,128]{2,1,0:T(8,128)(2,1)S(1)}, u32[]{:S(2)}, u32[]{:S(2)}) collective-permute-start(bf16[1,520,128]{2,1,0:T(8,128)(2,1)S(1)} %collective-permute-done.10.refs_9_), channel_id=1, source_target_pairs={{0,2},{2,0},{4,6},{6,4},{1,3},{3,1},{5,7},{7,5},{8,10},{10,8},{12,... | collective-permute-start | bytes 399368 | tf_op jit(solution)/shard_map/ppermute | solution.py:267
  54.2 3.6 %collective-permute-start.13 = (f32[1,128]{1,0:T(1,128)S(1)}, f32[1,128]{1,0:T(1,128)S(1)}, u32[]{:S(2)}, u32[]{:S(2)}) collective-permute-start(f32[1,128]{1,0:T(1,128)S(1)} %get-tuple-element.14.proj), channel_id=1, source_target_pairs={{0,1},{1,0},{2,3},{3,2},{4,5},{5,4},{6,7},{7,6},{8,9},{9,8},{10,11... | collective-permute-start | bytes 1544 | tf_op jit(solution)/shard_map/ppermute | solution.py:54
  (4 other events, 8.7 us)

commit v4 on v3

--- a/solution.py
+++ b/solution.py
@@ -32,18 +32,28 @@
     return lax.rem(me + (n - r), n)
 
 
-def gather_relatives(x, axis, n):
-    known = {0: x}
-    if power_of_two(n):
-        basis = n - 1
-        while basis:
-            for r in list(known):
-                known[r ^ basis] = lax.ppermute(known[r], axis, relative(n, basis))
-            basis //= 2
-    else:
+def gather_relatives(blocks, part, parcel, axis, n):
+    head = part.shape[0]
+    found, parts = {0: blocks}, {0: part}
+
+    def both(r):
+        parts[r] = lax.ppermute(parcel, axis, relative(n, r))
+        found[r] = parts[r][head:]
+
+    if not power_of_two(n):
         for r in range(1, n):
-            known[r] = lax.ppermute(x, axis, relative(n, r))
-    return known
+            both(r)
+        return found, parts
+    basis = n - 1
+    while basis:
+        for r in list(found):
+            if basis == 1 and r == 0:
+                both(1)
+                continue
+            found[r ^ basis] = lax.ppermute(found[r], axis, relative(n, basis))
+            parts[r ^ basis] = lax.ppermute(parts[r], axis, relative(n, basis))
+        basis //= 2
+    return found, parts
 
 
 def axis_terms(x, axis, n):
@@ -62,7 +72,7 @@
     return jnp.transpose(jnp.broadcast_to(row, (lanes, row.shape[1])))
 
 
-def load_kernel(share, blocks, key, hidden, parcel, square, loaded, sems):
+def load_kernel(share, blocks, key, hidden, parcel, own, square, loaded, sems):
     parts = key.shape[1] // LANES
     at = 0
     if share < key.shape[0]:
@@ -71,6 +81,7 @@
     for c in range(parts):
         part = key.at[pl.ds(at, share), c * LANES : (c + 1) * LANES]
         pairs.append((part, parcel.at[c * share : (c + 1) * share, :]))
+        pairs.append((part, own.at[c * share : (c + 1) * share, :]))
     copies = [pltpu.make_async_copy(a, b, sems.at[i]) for i, (a, b) in enumerate(pairs)]
     for copy in copies:
         copy.start()
@@ -236,31 +247,32 @@
     share = share if split else tokens
     head = share * parts
     hbm = pl.BlockSpec(memory_space=pltpu.HBM)
-    parcel, square = pl.pallas_call(
+    parcel, part, square = pl.pallas_call(
         functools.partial(load_kernel, share),
         name="load",
         out_shape=(
             jax.ShapeDtypeStruct((head + most, LANES), jnp.bfloat16),
+            jax.ShapeDtypeStruct((head, LANES), jnp.bfloat16),
             jax.ShapeDtypeStruct((1, tokens), jnp.float32),
         ),
         in_specs=[hbm] * 3,
-        out_specs=(vmem, vmem),
+        out_specs=(vmem, vmem, vmem),
         scratch_shapes=[
             pltpu.VMEM((tokens, features), jnp.bfloat16),
-            pltpu.SemaphoreType.DMA((parts + 2,)),
+            pltpu.SemaphoreType.DMA((2 * parts + 2,)),
         ],
         compiler_params=pltpu.CompilerParams(vmem_limit_bytes=60 << 20),
     )(weight_blocks.reshape(most, LANES), key_grad, hidden_in)
     hidden, gain = hidden_in, norm_gain[None, :]
-    found = gather_relatives(parcel, "gx", outer)
+    own_blocks = weight_blocks.reshape(most, LANES)
+    found, key_parts = gather_relatives(own_blocks, part, parcel, "gx", outer)
     order = list(found)
     lots = [lot for lot in (order[:1], order[1:-1], order[-1:]) if lot]
     lots = lots if outer > 1 else [order]
 
     pieces, names = [], []
-    for lot_index, lot in enumerate(lots):
-        own = weight_blocks.reshape(1, most, LANES)
-        spread = {0: jnp.stack([found[r][head:] for r in lot]) if lot_index else own}
+    for lot in lots:
+        spread = {0: jnp.stack([found[r] for r in lot])}
         bit = inner // 2
         while bit:
             for r in list(spread):
@@ -295,9 +307,9 @@
     for r in order[1:]:
         member = functools.partial(relative_index, halves, r=0) if split else (lambda i: 0)
         sources.append((member, [r], share))
-        key_pieces.append(found[r][None])
+        key_pieces.append(key_parts[r][None])
     for lot in [order[1:-1], order[-1:]] if split and outer > 1 else []:
-        stack = jnp.stack([found[r][:head] for r in lot])
+        stack = jnp.stack([key_parts[r][:head] for r in lot])
         for s in range(1, halves):
             sources.append((functools.partial(relative_index, halves, r=s), lot, share))
             key_pieces.append(lax.ppermute(stack, "gz", relative(halves, s)))

time: 59.8 us -> 56.7 us (0.948)
  waiting for transfers between devices: 26.1 us -> 20.2 us
  starting transfers between devices: 23.2 us -> 25.9 us
    ppermute x3 -> x5, starting transfers between devices: 6.19 us -> 12.3 us  [the longest x2 6.51 us: gather_relatives(): found[r ^ basis] = lax.ppermute(found[r], axis, relative(n, basis))]
    ppermute x3 -> x5, waiting for transfers between devices: 10.6 us -> 6.24 us  [the longest x2 4.81 us: gather_relatives(): parts[r ^ basis] = lax.ppermute(parts[r], axis, relative(n, basis))]
    ppermute x9, starting transfers between devices: 5.55 us -> 4.33 us  [shards(): spread[r ^ bit] = lax.ppermute(spread[r], 'gy', relative(inner, bit))]
    ppermute x2, waiting for transfers between devices: 1.15 us -> 0.01 us  [shards(): key_pieces.append(lax.ppermute(stack, 'gz', relative(halves, s)))]
    ppermute x2, starting transfers between devices: 3.09 us -> 2 us  [axis_terms(): lax.ppermute(x, axis, relative(n, bit))]
    ppermute x2, starting transfers between devices: 3.17 us -> 2.17 us  [shards(): key_pieces.append(lax.ppermute(stack, 'gz', relative(halves, s)))]
  transfers between devices with their start and end apart: 21 -> 23, of which waited for: 8 -> 6; matrix products, arithmetic and copies ran while one was open for 0% -> 0% of each run, Pallas kernels for 10% -> 10%
where the time goes in v4:
time: 56.7 us; the launch traced here: 56.4 us
  starting transfers between devices  25.9 us (46%)
  waiting for transfers between devices  20.2 us (36%)
  Pallas kernels  7.95 us (14%)
  other arithmetic  0.91 us (2%)
  between operations  0.79 us (1%)
  local copies, waits for them, and re-layouts  0.72 us (1%)
    ppermute x9, waiting for transfers between devices, shards(): spread[r ^ bit] = lax.ppermute(spread[r], 'gy', relative(inner, bit))  10.8 us
    ppermute x2, starting transfers between devices, gather_relatives(): found[r ^ basis] = lax.ppermute(found[r], axis, relative(n, basis))  6.51 us
    pallas_call x4, Pallas kernels, call(): pl.pallas_call(kernel, out_shape=out_shape, in_specs=[smem] * len(scalars...  5.86 us
    ppermute x2, waiting for transfers between devices, gather_relatives(): parts[r ^ basis] = lax.ppermute(parts[r], axis, relative(n, basis))  4.81 us
    ppermute x3, starting transfers between devices, shards(): norms.append(lax.ppermute(windows[r], 'gx', relative(outer, r)))  4.45 us
    ppermute x9, starting transfers between devices, shards(): spread[r ^ bit] = lax.ppermute(spread[r], 'gy', relative(inner, bit))  4.33 us
    ppermute x2, waiting for transfers between devices, axis_terms(): lax.ppermute(x, axis, relative(n, bit))  3.16 us
    ppermute x1, starting transfers between devices, both(): parts[r] = lax.ppermute(parcel, axis, relative(n, r))  3.12 us
  transfers between devices with their start and end apart: 23, of which 6 were waited for; matrix products, arithmetic and copies ran while one was open for 0% of the time, Pallas kernels for 10%

profile of v4, /device:TPU:0, one launch (start us, length us, event | category | flops | bytes accessed | tf_op | source)
XLA Modules:
  0.0 56.4 jit_solution(1282319413532674521)
XLA Ops:
  0.6 2.1 %load.1 = (bf16[776,128]{1,0:T(8,128)(2,1)}, bf16[256,128]{1,0:T(8,128)(2,1)}, f32[1,128]{1,0:T(1,128)}) custom-call(bf16[520,128]{1,0:T(8,128)(2,1)} %bitcast.19, bf16[128,512]{1,0:T(8,128)(2,1)} %own.1, bf16[128,2048]{1,0:T(8,128)(2,1)} %hidden.7), custom_call_target="tpu_custom_call" | custom-call | tf_op jit(solution)/shard_map/load/pallas_call | solution.py:250
  2.7 3.1 %collective-permute-start.5 = (bf16[776,128]{1,0:T(8,128)(2,1)}, bf16[776,128]{1,0:T(8,128)(2,1)S(1)}, u32[]{:S(2)}, u32[]{:S(2)}) collective-permute-start(bf16[776,128]{1,0:T(8,128)(2,1)} %get-tuple-element.14), channel_id=1, source_target_pairs={{0,8},{8,0},{16,24},{24,16},{1,9},{9,1},{17,25},{25,17},{2,10},{10... | collective-permute-start | bytes 595976 | tf_op jit(solution)/shard_map/ppermute | solution.py:40
  5.9 1.5 %collective-permute-start = (f32[1,128]{1,0:T(1,128)S(1)}, f32[1,128]{1,0:T(1,128)S(1)}, u32[]{:S(2)}, u32[]{:S(2)}) collective-permute-start(f32[1,128]{1,0:T(1,128)S(1)} %copy-done.5), channel_id=1, source_target_pairs={{0,1},{1,0},{2,3},{3,2},{4,5},{5,4},{6,7},{7,6},{8,9},{9,8},{10,11... | collective-permute-start | bytes 1544 | tf_op jit(solution)/shard_map/ppermute | solution.py:64
  7.4 2.6 %collective-permute-start.14 = (bf16[256,128]{1,0:T(8,128)(2,1)}, bf16[256,128]{1,0:T(8,128)(2,1)S(1)}, u32[]{:S(2)}, u32[]{:S(2)}) collective-permute-start(bf16[256,128]{1,0:T(8,128)(2,1)} %get-tuple-element.17), channel_id=1, source_target_pairs={{0,24},{8,16},{16,8},{24,0},{1,25},{9,17},{17,9},{25,1},{2,26},{10... | collective-permute-start | bytes 196616 | tf_op jit(solution)/shard_map/ppermute | solution.py:54
  10.0 0.7 %copy-done.6 = s32[1,16]{1,0:T(1,128)S(1)} copy-done((s32[1,16]{1,0:T(1,128)S(1)}, s32[1,16]{1,0:T(1,128)}, u32[]{:S(2)}) %copy-start.6) | copy-done | bytes 88
  10.8 0.8 %shard_map.79 = (bf16[128,512]{1,0:T(8,128)(2,1)S(1)}, bf16[128,512]{1,0:T(8,128)(2,1)S(1)}, bf16[128,512]{1,0:T(8,128)(2,1)S(1)}, bf16[128,512]{1,0:T(8,128)(2,1)S(1)}) custom-call(s32[19]{0:T(128)S(1)} %pad_add_fusion.meta, f32[1,128]{1,0:T(1,128)S(1)} %copy-done.5, f32[1,128]{1,0:T(1,128)S(1)} %collective-permute-done.other, ...), custom_call_target="tpu_custom_call" | custom-call | tf_op jit(solution)/shard_map/pallas_call | solution.py:236
  12.2 1.3 %collective-permute-start.19 = (bf16[128,512]{1,0:T(8,128)(2,1)S(1)}, bf16[128,512]{1,0:T(8,128)(2,1)S(1)}, u32[]{:S(2)}, u32[]{:S(2)}) collective-permute-start(bf16[128,512]{1,0:T(8,128)(2,1)S(1)} %get-tuple-element.20), channel_id=1, source_target_pairs={{0,16},{8,24},{16,0},{24,8},{1,17},{9,25},{17,1},{25,9},{2,18},{10... | collective-permute-start | bytes 393224 | tf_op jit(solution)/shard_map/ppermute | solution.py:318
  13.5 2.5 %collective-permute-start.20 = (bf16[128,512]{1,0:T(8,128)(2,1)S(1)}, bf16[128,512]{1,0:T(8,128)(2,1)S(1)}, u32[]{:S(2)}, u32[]{:S(2)}) collective-permute-start(bf16[128,512]{1,0:T(8,128)(2,1)S(1)} %get-tuple-element.21), channel_id=1, source_target_pairs={{0,24},{8,16},{16,8},{24,0},{1,25},{9,17},{17,9},{25,1},{2,26},{10... | collective-permute-start | bytes 393224 | tf_op jit(solution)/shard_map/ppermute | solution.py:318
  16.1 1.3 %collective-permute-start.16 = (bf16[2,256,128]{2,1,0:T(8,128)(2,1)S(1)}, bf16[2,256,128]{2,1,0:T(8,128)(2,1)S(1)}, u32[]{:S(2)}, u32[]{:S(2)}) collective-permute-start(bf16[2,256,128]{2,1,0:T(8,128)(2,1)S(1)} %pad_maximum_fusion.1), channel_id=1, source_target_pairs={{0,1},{1,0},{2,3},{3,2},{4,5},{5,4},{6,7},{7,6},{8,9},{9,8},{10,11... | collective-permute-start | bytes 393224 | tf_op jit(solution)/shard_map/ppermute | solution.py:315
  17.4 4.8 %collective-permute-done.15 = bf16[256,128]{1,0:T(8,128)(2,1)S(1)} collective-permute-done((bf16[256,128]{1,0:T(8,128)(2,1)S(1)}, bf16[256,128]{1,0:T(8,128)(2,1)S(1)}, u32[]{:S(2)}, u32[]{:S(2)}) %collective-permute-start.15) | collective-permute-done | bytes 65568 | tf_op jit(solution)/shard_map/ppermute | solution.py:54
  22.2 0.9 %collective-permute-start.17 = (bf16[1,256,128]{2,1,0:T(8,128)(2,1)S(1)}, bf16[1,256,128]{2,1,0:T(8,128)(2,1)S(1)}, u32[]{:S(2)}, u32[]{:S(2)}) collective-permute-start(bf16[1,256,128]{2,1,0:T(8,128)(2,1)S(1)} %bitcast.29), channel_id=1, source_target_pairs={{0,1},{1,0},{2,3},{3,2},{4,5},{5,4},{6,7},{7,6},{8,9},{9,8},{10,11... | collective-permute-start | bytes 196616 | tf_op jit(solution)/shard_map/ppermute | solution.py:315
  23.1 3.8 %collective-permute-start.4 = (bf16[520,128]{1,0:T(8,128)(2,1)S(1)}, bf16[520,128]{1,0:T(8,128)(2,1)S(1)}, u32[]{:S(2)}, u32[]{:S(2)}) collective-permute-start(bf16[520,128]{1,0:T(8,128)(2,1)S(1)} %bitcast.20), channel_id=1, source_target_pairs={{0,24},{8,16},{16,8},{24,0},{1,25},{9,17},{17,9},{25,1},{2,26},{10... | collective-permute-start | bytes 399368 | tf_op jit(solution)/shard_map/ppermute | solution.py:53
  26.9 1.5 %shard_map.80 = (f32[2,520,128]{2,1,0:T(8,128)S(1)}, f32[2,520,128]{2,1,0:T(8,128)S(1)}) custom-call(s32[19]{0:T(128)S(1)} %pad_add_fusion.meta, bf16[128,512]{1,0:T(8,128)(2,1)S(1)} %copy-done.1, bf16[1,256,128]{2,1,0:T(8,128)(2,1)S(1)} %bitcast.25, bf16[1,776,128]{2,1,0:T(8,128)(2,1)S(1)} %bitcast.18, bf16[1,256,128]{2,1,0:T(8,128)(2,1)S(1)} %bitcast.30, ...), custom_call_target="tpu_custom_call" | custom-call | tf_op jit(solution)/shard_map/pallas_call | solution.py:236
  28.5 1.4 %collective-permute-done.4 = bf16[520,128]{1,0:T(8,128)(2,1)S(1)} collective-permute-done((bf16[520,128]{1,0:T(8,128)(2,1)S(1)}, bf16[520,128]{1,0:T(8,128)(2,1)S(1)}, u32[]{:S(2)}, u32[]{:S(2)}) %collective-permute-start.4) | collective-permute-done | bytes 133152 | tf_op jit(solution)/shard_map/ppermute | solution.py:53
  30.0 1.6 %collective-permute-start.6 = (bf16[2,520,128]{2,1,0:T(8,128)(2,1)S(1)}, bf16[2,520,128]{2,1,0:T(8,128)(2,1)S(1)}, u32[]{:S(2)}, u32[]{:S(2)}) collective-permute-start(bf16[2,520,128]{2,1,0:T(8,128)(2,1)S(1)} %pad_maximum_fusion.refs_4_), channel_id=1, source_target_pairs={{0,4},{2,6},{4,0},{6,2},{1,5},{3,7},{5,1},{7,3},{8,12},{10,14},{12... | collective-permute-start | bytes 798728 | tf_op jit(solution)/shard_map/ppermute | solution.py:279
  32.1 2.7 %collective-permute-start.9 = (bf16[520,128]{1,0:T(8,128)(2,1)S(1)}, bf16[520,128]{1,0:T(8,128)(2,1)S(1)}, u32[]{:S(2)}, u32[]{:S(2)}) collective-permute-start(bf16[520,128]{1,0:T(8,128)(2,1)S(1)} %collective-permute-done.4), channel_id=1, source_target_pairs={{0,8},{8,0},{16,24},{24,16},{1,9},{9,1},{17,25},{25,17},{2,10},{10... | collective-permute-start | bytes 399368 | tf_op jit(solution)/shard_map/ppermute | solution.py:53
  34.8 5.5 %collective-permute-done.1.refs_1_ = bf16[1,520,128]{2,1,0:T(8,128)(2,1)S(1)} collective-permute-done((bf16[1,520,128]{2,1,0:T(8,128)(2,1)S(1)}, bf16[1,520,128]{2,1,0:T(8,128)(2,1)S(1)}, u32[]{:S(2)}, u32[]{:S(2)}) %collective-permute-start.1) | collective-permute-done | bytes 133152 | tf_op jit(solution)/shard_map/ppermute | solution.py:279
  40.8 1.5 %collective-permute-start.10 = (bf16[1,520,128]{2,1,0:T(8,128)(2,1)S(1)}, bf16[1,520,128]{2,1,0:T(8,128)(2,1)S(1)}, u32[]{:S(2)}, u32[]{:S(2)}) collective-permute-start(bf16[1,520,128]{2,1,0:T(8,128)(2,1)S(1)} %bitcast.26), channel_id=1, source_target_pairs={{0,4},{2,6},{4,0},{6,2},{1,5},{3,7},{5,1},{7,3},{8,12},{10,14},{12... | collective-permute-start | bytes 399368 | tf_op jit(solution)/shard_map/ppermute | solution.py:279
  43.2 3.9 %collective-permute-done.10.refs_9_ = bf16[1,520,128]{2,1,0:T(8,128)(2,1)S(1)} collective-permute-done((bf16[1,520,128]{2,1,0:T(8,128)(2,1)S(1)}, bf16[1,520,128]{2,1,0:T(8,128)(2,1)S(1)}, u32[]{:S(2)}, u32[]{:S(2)}) %collective-permute-start.10) | collective-permute-done | bytes 133152 | tf_op jit(solution)/shard_map/ppermute | solution.py:279
  47.2 1.3 %collective-permute-done.12.refs_11_ = bf16[1,520,128]{2,1,0:T(8,128)(2,1)S(1)} collective-permute-done((bf16[1,520,128]{2,1,0:T(8,128)(2,1)S(1)}, bf16[1,520,128]{2,1,0:T(8,128)(2,1)S(1)}, u32[]{:S(2)}, u32[]{:S(2)}) %collective-permute-start.12) | collective-permute-done | bytes 133152 | tf_op jit(solution)/shard_map/ppermute | solution.py:279
  48.5 2.5 %shard_map.77 = (f32[128,2048]{1,0:T(8,128)S(1)}, f32[1,128]{1,0:T(1,128)S(1)}) custom-call(s32[19]{0:T(128)S(1)} %pad_add_fusion.meta, bf16[128,512]{1,0:T(8,128)(2,1)S(1)} %copy-done.1, bf16[128,2048]{1,0:T(8,128)(2,1)S(1)} %copy-done.3, bf16[128,2048]{1,0:T(8,128)(2,1)S(1)} %copy-done, f32[1,2048]{1,0:T(1,128)S(1)} %bitcast.32, ...), custom_call_target="tpu_custom_call" | custom-call | tf_op jit(solution)/shard_map/pallas_call | solution.py:236
  51.5 3.2 %collective-permute-done.13.proj_other = f32[1,128]{1,0:T(1,128)S(1)} collective-permute-done((f32[1,128]{1,0:T(1,128)S(1)}, f32[1,128]{1,0:T(1,128)S(1)}, u32[]{:S(2)}, u32[]{:S(2)}) %collective-permute-start.13) | collective-permute-done | bytes 544 | tf_op jit(solution)/shard_map/ppermute | solution.py:64
  54.6 1.1 %shard_map.78 = bf16[128,2048]{1,0:T(8,128)(2,1)} custom-call(f32[1,128]{1,0:T(1,128)S(1)} %copy-done.5, f32[1,128]{1,0:T(1,128)S(1)} %collective-permute-done.other, f32[1,128]{1,0:T(1,128)S(1)} %get-tuple-element.15.proj, f32[1,128]{1,0:T(1,128)S(1)} %collective-permute-done.13.proj_other, f32[128,2048]{1,0:T(8,128)S(1)} %get-tuple-element.16.scaled, ...), custom_call_target="tpu_custom_call" | custom-call | tf_op jit(solution)/shard_map/pallas_call | solution.py:236
  55.7 0.8 %fusion.1 = f32[1,1,520,128]{3,2,1,0:T(8,128)} fusion(f32[1,520,128]{2,1,0:T(8,128)S(1)} %collective-permute-done.22, f32[2,520,128]{2,1,0:T(8,128)S(1)} %collective-permute-done.21, f32[2,520,128]{2,1,0:T(8,128)S(1)} %get-tuple-element.22), kind=kLoop, calls=%fused_computation.3 | loop fusion | flops 133120 | bytes 1064960 | tf_op jit(solution)/shard_map/reshape;squeeze | solution.py:361
  (48 shorter events, 3.3 us)
Async XLA Ops:
  2.7 13.3 %collective-permute-start.5 = (bf16[776,128]{1,0:T(8,128)(2,1)}, bf16[776,128]{1,0:T(8,128)(2,1)S(1)}, u32[]{:S(2)}, u32[]{:S(2)}) collective-permute-start(bf16[776,128]{1,0:T(8,128)(2,1)} %get-tuple-element.14), channel_id=1, source_target_pairs={{0,8},{8,0},{16,24},{24,16},{1,9},{9,1},{17,25},{25,17},{2,10},{10... | collective-permute-start | bytes 595976 | tf_op jit(solution)/shard_map/ppermute | solution.py:40
  5.9 4.9 %collective-permute-start = (f32[1,128]{1,0:T(1,128)S(1)}, f32[1,128]{1,0:T(1,128)S(1)}, u32[]{:S(2)}, u32[]{:S(2)}) collective-permute-start(f32[1,128]{1,0:T(1,128)S(1)} %copy-done.5), channel_id=1, source_target_pairs={{0,1},{1,0},{2,3},{3,2},{4,5},{5,4},{6,7},{7,6},{8,9},{9,8},{10,11... | collective-permute-start | bytes 1544 | tf_op jit(solution)/shard_map/ppermute | solution.py:64
  7.4 8.6 %collective-permute-start.14 = (bf16[256,128]{1,0:T(8,128)(2,1)}, bf16[256,128]{1,0:T(8,128)(2,1)S(1)}, u32[]{:S(2)}, u32[]{:S(2)}) collective-permute-start(bf16[256,128]{1,0:T(8,128)(2,1)} %get-tuple-element.17), channel_id=1, source_target_pairs={{0,24},{8,16},{16,8},{24,0},{1,25},{9,17},{17,9},{25,1},{2,26},{10... | collective-permute-start | bytes 196616 | tf_op jit(solution)/shard_map/ppermute | solution.py:54
  11.6 11.5 %collective-permute-start.18 = (bf16[128,512]{1,0:T(8,128)(2,1)S(1)}, bf16[128,512]{1,0:T(8,128)(2,1)S(1)}, u32[]{:S(2)}, u32[]{:S(2)}) collective-permute-start(bf16[128,512]{1,0:T(8,128)(2,1)S(1)} %get-tuple-element.19), channel_id=1, source_target_pairs={{0,8},{8,0},{16,24},{24,16},{1,9},{9,1},{17,25},{25,17},{2,10},{10... | collective-permute-start | bytes 393224 | tf_op jit(solution)/shard_map/ppermute | solution.py:318
  12.2 14.7 %collective-permute-start.19 = (bf16[128,512]{1,0:T(8,128)(2,1)S(1)}, bf16[128,512]{1,0:T(8,128)(2,1)S(1)}, u32[]{:S(2)}, u32[]{:S(2)}) collective-permute-start(bf16[128,512]{1,0:T(8,128)(2,1)S(1)} %get-tuple-element.20), channel_id=1, source_target_pairs={{0,16},{8,24},{16,0},{24,8},{1,17},{9,25},{17,1},{25,9},{2,18},{10... | collective-permute-start | bytes 393224 | tf_op jit(solution)/shard_map/ppermute | solution.py:318
  13.5 13.4 %collective-permute-start.20 = (bf16[128,512]{1,0:T(8,128)(2,1)S(1)}, bf16[128,512]{1,0:T(8,128)(2,1)S(1)}, u32[]{:S(2)}, u32[]{:S(2)}) collective-permute-start(bf16[128,512]{1,0:T(8,128)(2,1)S(1)} %get-tuple-element.21), channel_id=1, source_target_pairs={{0,24},{8,16},{16,8},{24,0},{1,25},{9,17},{17,9},{25,1},{2,26},{10... | collective-permute-start | bytes 393224 | tf_op jit(solution)/shard_map/ppermute | solution.py:318
  16.0 6.2 %collective-permute-start.15 = (bf16[256,128]{1,0:T(8,128)(2,1)S(1)}, bf16[256,128]{1,0:T(8,128)(2,1)S(1)}, u32[]{:S(2)}, u32[]{:S(2)}) collective-permute-start(bf16[256,128]{1,0:T(8,128)(2,1)S(1)} %collective-permute-done.14), channel_id=1, source_target_pairs={{0,8},{8,0},{16,24},{24,16},{1,9},{9,1},{17,25},{25,17},{2,10},{10... | collective-permute-start | bytes 196616 | tf_op jit(solution)/shard_map/ppermute | solution.py:54
  16.1 10.8 %collective-permute-start.16 = (bf16[2,256,128]{2,1,0:T(8,128)(2,1)S(1)}, bf16[2,256,128]{2,1,0:T(8,128)(2,1)S(1)}, u32[]{:S(2)}, u32[]{:S(2)}) collective-permute-start(bf16[2,256,128]{2,1,0:T(8,128)(2,1)S(1)} %pad_maximum_fusion.1), channel_id=1, source_target_pairs={{0,1},{1,0},{2,3},{3,2},{4,5},{5,4},{6,7},{7,6},{8,9},{9,8},{10,11... | collective-permute-start | bytes 393224 | tf_op jit(solution)/shard_map/ppermute | solution.py:315
  22.2 4.7 %collective-permute-start.17 = (bf16[1,256,128]{2,1,0:T(8,128)(2,1)S(1)}, bf16[1,256,128]{2,1,0:T(8,128)(2,1)S(1)}, u32[]{:S(2)}, u32[]{:S(2)}) collective-permute-start(bf16[1,256,128]{2,1,0:T(8,128)(2,1)S(1)} %bitcast.29), channel_id=1, source_target_pairs={{0,1},{1,0},{2,3},{3,2},{4,5},{5,4},{6,7},{7,6},{8,9},{9,8},{10,11... | collective-permute-start | bytes 196616 | tf_op jit(solution)/shard_map/ppermute | solution.py:315
  23.1 6.9 %collective-permute-start.4 = (bf16[520,128]{1,0:T(8,128)(2,1)S(1)}, bf16[520,128]{1,0:T(8,128)(2,1)S(1)}, u32[]{:S(2)}, u32[]{:S(2)}) collective-permute-start(bf16[520,128]{1,0:T(8,128)(2,1)S(1)} %bitcast.20), channel_id=1, source_target_pairs={{0,24},{8,16},{16,8},{24,0},{1,25},{9,17},{17,9},{25,1},{2,26},{10... | collective-permute-start | bytes 399368 | tf_op jit(solution)/shard_map/ppermute | solution.py:53
  28.4 13.9 %collective-permute-start.21 = (f32[2,520,128]{2,1,0:T(8,128)S(1)}, f32[2,520,128]{2,1,0:T(8,128)S(1)}, u32[]{:S(2)}, u32[]{:S(2)}) collective-permute-start(f32[2,520,128]{2,1,0:T(8,128)S(1)} %get-tuple-element.23), channel_id=1, source_target_pairs={{0,2},{2,0},{4,6},{6,4},{1,3},{3,1},{5,7},{7,5},{8,10},{10,8},{12,... | collective-permute-start | bytes 1597448 | tf_op jit(solution)/shard_map/ppermute | solution.py:355
  30.0 18.5 %copy-start.3 = (bf16[128,2048]{1,0:T(8,128)(2,1)S(1)}, bf16[128,2048]{1,0:T(8,128)(2,1)}, u32[]{:S(2)}) copy-start(bf16[128,2048]{1,0:T(8,128)(2,1)} %grad.1) | copy-start | bytes 1572868
  30.0 10.8 %collective-permute-start.6 = (bf16[2,520,128]{2,1,0:T(8,128)(2,1)S(1)}, bf16[2,520,128]{2,1,0:T(8,128)(2,1)S(1)}, u32[]{:S(2)}, u32[]{:S(2)}) collective-permute-start(bf16[2,520,128]{2,1,0:T(8,128)(2,1)S(1)} %pad_maximum_fusion.refs_4_), channel_id=1, source_target_pairs={{0,4},{2,6},{4,0},{6,2},{1,5},{3,7},{5,1},{7,3},{8,12},{10,14},{12... | collective-permute-start | bytes 798728 | tf_op jit(solution)/shard_map/ppermute | solution.py:279
  31.6 8.7 %collective-permute-start.1 = (bf16[1,520,128]{2,1,0:T(8,128)(2,1)S(1)}, bf16[1,520,128]{2,1,0:T(8,128)(2,1)S(1)}, u32[]{:S(2)}, u32[]{:S(2)}) collective-permute-start(bf16[1,520,128]{2,1,0:T(8,128)(2,1)S(1)} %bitcast.21), channel_id=1, source_target_pairs={{0,4},{2,6},{4,0},{6,2},{1,5},{3,7},{5,1},{7,3},{8,12},{10,14},{12... | collective-permute-start | bytes 399368 | tf_op jit(solution)/shard_map/ppermute | solution.py:279
  32.1 8.2 %collective-permute-start.9 = (bf16[520,128]{1,0:T(8,128)(2,1)S(1)}, bf16[520,128]{1,0:T(8,128)(2,1)S(1)}, u32[]{:S(2)}, u32[]{:S(2)}) collective-permute-start(bf16[520,128]{1,0:T(8,128)(2,1)S(1)} %collective-permute-done.4), channel_id=1, source_target_pairs={{0,8},{8,0},{16,24},{24,16},{1,9},{9,1},{17,25},{25,17},{2,10},{10... | collective-permute-start | bytes 399368 | tf_op jit(solution)/shard_map/ppermute | solution.py:53
  34.8 7.6 %collective-permute-start.2 = (bf16[1,520,128]{2,1,0:T(8,128)(2,1)S(1)}, bf16[1,520,128]{2,1,0:T(8,128)(2,1)S(1)}, u32[]{:S(2)}, u32[]{:S(2)}) collective-permute-start(bf16[1,520,128]{2,1,0:T(8,128)(2,1)S(1)} %bitcast.22), channel_id=1, source_target_pairs={{0,2},{2,0},{4,6},{6,4},{1,3},{3,1},{5,7},{7,5},{8,10},{10,8},{12,... | collective-permute-start | bytes 399368 | tf_op jit(solution)/shard_map/ppermute | solution.py:279
  40.3 2.7 %collective-permute-start.3 = (bf16[1,520,128]{2,1,0:T(8,128)(2,1)S(1)}, bf16[1,520,128]{2,1,0:T(8,128)(2,1)S(1)}, u32[]{:S(2)}, u32[]{:S(2)}) collective-permute-start(bf16[1,520,128]{2,1,0:T(8,128)(2,1)S(1)} %collective-permute-done.1.refs_1_), channel_id=1, source_target_pairs={{0,2},{2,0},{4,6},{6,4},{1,3},{3,1},{5,7},{7,5},{8,10},{10,8},{12,... | collective-permute-start | bytes 399368 | tf_op jit(solution)/shard_map/ppermute | solution.py:279
  40.3 6.8 %collective-permute-start.7 = (bf16[2,520,128]{2,1,0:T(8,128)(2,1)S(1)}, bf16[2,520,128]{2,1,0:T(8,128)(2,1)S(1)}, u32[]{:S(2)}, u32[]{:S(2)}) collective-permute-start(bf16[2,520,128]{2,1,0:T(8,128)(2,1)S(1)} %pad_maximum_fusion.refs_4_), channel_id=1, source_target_pairs={{0,2},{2,0},{4,6},{6,4},{1,3},{3,1},{5,7},{7,5},{8,10},{10,8},{12,... | collective-permute-start | bytes 798728 | tf_op jit(solution)/shard_map/ppermute | solution.py:279
  40.8 6.3 %collective-permute-start.10 = (bf16[1,520,128]{2,1,0:T(8,128)(2,1)S(1)}, bf16[1,520,128]{2,1,0:T(8,128)(2,1)S(1)}, u32[]{:S(2)}, u32[]{:S(2)}) collective-permute-start(bf16[1,520,128]{2,1,0:T(8,128)(2,1)S(1)} %bitcast.26), channel_id=1, source_target_pairs={{0,4},{2,6},{4,0},{6,2},{1,5},{3,7},{5,1},{7,3},{8,12},{10,14},{12... | collective-permute-start | bytes 399368 | tf_op jit(solution)/shard_map/ppermute | solution.py:279
  42.3 6.2 %collective-permute-start.8 = (bf16[2,520,128]{2,1,0:T(8,128)(2,1)S(1)}, bf16[2,520,128]{2,1,0:T(8,128)(2,1)S(1)}, u32[]{:S(2)}, u32[]{:S(2)}) collective-permute-start(bf16[2,520,128]{2,1,0:T(8,128)(2,1)S(1)} %collective-permute-done.6.refs_5_), channel_id=1, source_target_pairs={{0,2},{2,0},{4,6},{6,4},{1,3},{3,1},{5,7},{7,5},{8,10},{10,8},{12,... | collective-permute-start | bytes 798728 | tf_op jit(solution)/shard_map/ppermute | solution.py:279
  42.4 13.3 %collective-permute-start.22 = (f32[1,520,128]{2,1,0:T(8,128)S(1)}, f32[1,520,128]{2,1,0:T(8,128)S(1)}, u32[]{:S(2)}, u32[]{:S(2)}) collective-permute-start(f32[1,520,128]{2,1,0:T(8,128)S(1)} %slice_add_fusion), channel_id=1, source_target_pairs={{0,4},{2,6},{4,0},{6,2},{1,5},{3,7},{5,1},{7,3},{8,12},{10,14},{12... | collective-permute-start | bytes 798728 | tf_op jit(solution)/shard_map/ppermute | solution.py:355
  43.0 4.2 %collective-permute-start.11 = (bf16[1,520,128]{2,1,0:T(8,128)(2,1)S(1)}, bf16[1,520,128]{2,1,0:T(8,128)(2,1)S(1)}, u32[]{:S(2)}, u32[]{:S(2)}) collective-permute-start(bf16[1,520,128]{2,1,0:T(8,128)(2,1)S(1)} %bitcast.27), channel_id=1, source_target_pairs={{0,2},{2,0},{4,6},{6,4},{1,3},{3,1},{5,7},{7,5},{8,10},{10,8},{12,... | collective-permute-start | bytes 399368 | tf_op jit(solution)/shard_map/ppermute | solution.py:279
  47.1 1.4 %collective-permute-start.12 = (bf16[1,520,128]{2,1,0:T(8,128)(2,1)S(1)}, bf16[1,520,128]{2,1,0:T(8,128)(2,1)S(1)}, u32[]{:S(2)}, u32[]{:S(2)}) collective-permute-start(bf16[1,520,128]{2,1,0:T(8,128)(2,1)S(1)} %collective-permute-done.10.refs_9_), channel_id=1, source_target_pairs={{0,2},{2,0},{4,6},{6,4},{1,3},{3,1},{5,7},{7,5},{8,10},{10,8},{12,... | collective-permute-start | bytes 399368 | tf_op jit(solution)/shard_map/ppermute | solution.py:279
  51.0 3.6 %collective-permute-start.13 = (f32[1,128]{1,0:T(1,128)S(1)}, f32[1,128]{1,0:T(1,128)S(1)}, u32[]{:S(2)}, u32[]{:S(2)}) collective-permute-start(f32[1,128]{1,0:T(1,128)S(1)} %get-tuple-element.15.proj), channel_id=1, source_target_pairs={{0,1},{1,0},{2,3},{3,2},{4,5},{5,4},{6,7},{7,6},{8,9},{9,8},{10,11... | collective-permute-start | bytes 1544 | tf_op jit(solution)/shard_map/ppermute | solution.py:64
  (6 other events, 32.6 us)

commit v5 on v3

--- a/solution.py
+++ b/solution.py
@@ -62,28 +62,6 @@
     return jnp.transpose(jnp.broadcast_to(row, (lanes, row.shape[1])))
 
 
-def load_kernel(share, blocks, key, hidden, parcel, square, loaded, sems):
-    parts = key.shape[1] // LANES
-    at = 0
-    if share < key.shape[0]:
-        at = pl.multiple_of(lax.axis_index("gz") * share, share)
-    pairs = [(hidden, loaded), (blocks, parcel.at[pl.ds(parts * share, blocks.shape[0]), :])]
-    for c in range(parts):
-        part = key.at[pl.ds(at, share), c * LANES : (c + 1) * LANES]
-        pairs.append((part, parcel.at[c * share : (c + 1) * share, :]))
-    copies = [pltpu.make_async_copy(a, b, sems.at[i]) for i, (a, b) in enumerate(pairs)]
-    for copy in copies:
-        copy.start()
-    copies[0].wait()
-    total = jnp.zeros((hidden.shape[0], LANES), jnp.float32)
-    for c in range(0, hidden.shape[1], LANES):
-        value = loaded[:, c : c + LANES].astype(jnp.float32)
-        total = total + value * value
-    square[...] = jnp.sum(jnp.transpose(total), axis=0, keepdims=True)
-    for copy in copies[1:]:
-        copy.wait()
-
-
 def norm_kernel(members, model_width, starts, rows, meta, square, other, hidden, gain, *outs):
     tokens, features = hidden.shape
     total = square[...] + other[...]
@@ -113,19 +91,33 @@
                     out[...] = part.astype(jnp.bfloat16)
 
 
-def finish_kernel(model_width, square, other, proj, proj_other, scaled, hidden, out):
+def finish_kernel(calls, outer, model_width, meta, square, other, proj, proj_other, hidden, *refs):
     rstd = lax.rsqrt((square[...] + other[...]) / model_width + EPS)
     shift = rstd**3 * (proj[...] + proj_other[...]) / model_width
     rstd, shift = column(rstd, LANES), column(shift, LANES)
-    for at in range(0, hidden.shape[1], LANES):
-        cols = slice(at, at + LANES)
-        grad = scaled[:, cols] * rstd - hidden[:, cols].astype(jnp.float32) * shift
-        out[:, cols] = grad.astype(jnp.bfloat16)
-
-
-def input_grad_kernel(owner_of, most, meta, key, grad, hidden, gain, *refs):
-    pieces, (scaled, proj, dense, starts) = refs[:-4], refs[-4:]
+    out = refs[-1]
+    for relatives, scaled in zip(calls, refs):
+        columns = scaled.shape[2]
+        for i in range(scaled.shape[0]):
+            for at in range(0, columns, LANES):
+                cols = pl.ds(at, LANES)
+                if relatives is not None:
+                    base = relative_index(outer, meta[0], relatives[i]) * columns
+                    cols = pl.ds(pl.multiple_of(base + at, LANES), LANES)
+                value = hidden[:, cols].astype(jnp.float32)
+                grad = scaled[i, :, at : at + LANES] * rstd - value * shift
+                out[:, cols] = grad.astype(jnp.bfloat16)
+
+
+def input_grad_kernel(names, relatives, outer, inner, most, meta, key, grad, hidden, gain, *refs):
+    scaled, proj, dense, starts = refs[-4:]
+    pieces = [ref for ref in refs[:-4] if ref.dtype == jnp.bfloat16]
+    before = [ref for ref in refs[:-4] if ref.dtype == jnp.float32]
     owners = meta.shape[0] - PLACE
+    tokens = hidden.shape[0]
+    parts = key.shape[1] // LANES
+    columns = scaled.shape[2]
+    span = columns * parts
 
     def mark(o, at):
         starts[o] = at
@@ -136,29 +128,39 @@
     index = 0
     for piece in pieces:
         for i in range(piece.shape[0]):
-            owner = owner_of(meta[0], meta[1], index)
-            rows = pl.ds(starts[owner], most)
+            r, s = names[index]
+            member = relative_index(outer, meta[0], r)
+            owner = member * inner + (meta[1] ^ s)
+            start = starts[owner]
+            if relatives is not None:
+                start = start + (relatives.index(r) - member) * span
+            rows = pl.ds(start, most)
             new = piece[i].astype(jnp.float32)
             dense[rows, :] = jnp.where(slot < meta[PLACE + owner], new, dense[rows, :])
             index += 1
-    tokens, features = hidden.shape
-    parts = key.shape[1] // LANES
-    step = 256 if features % 256 == 0 else features
+    step = 256 if columns % 256 == 0 else columns
     total = jnp.zeros((tokens, LANES), jnp.float32)
-    for at in range(0, features, step):
-        weight = jnp.concatenate(
-            [dense[pl.ds(at * parts + c, step, stride=parts), :] for c in range(parts)], axis=1
-        ).astype(jnp.bfloat16)
-        cols = slice(at, at + step)
-        product = lax.dot_general(
-            key[...], weight, (((1,), (1,)), ((), ())), preferred_element_type=jnp.float32
-        )
-        gained = gain[:, cols] * (grad[:, cols].astype(jnp.float32) + product)
-        scaled[:, cols] = gained
-        terms = gained * hidden[:, cols].astype(jnp.float32)
-        for c in range(0, step, LANES):
-            total = total + terms[:, c : c + LANES]
+    for i in range(scaled.shape[0]):
+        base = 0
+        if relatives is not None:
+            base = relative_index(outer, meta[0], relatives[i]) * columns
+        for at in range(0, columns, step):
+            first = (i * columns + at) * parts
+            weight = jnp.concatenate(
+                [dense[pl.ds(first + c, step, stride=parts), :] for c in range(parts)], axis=1
+            ).astype(jnp.bfloat16)
+            cols = pl.ds(at if relatives is None else pl.multiple_of(base + at, LANES), step)
+            product = lax.dot_general(
+                key[...], weight, (((1,), (1,)), ((), ())), preferred_element_type=jnp.float32
+            )
+            gained = gain[:, cols] * (grad[:, cols].astype(jnp.float32) + product)
+            scaled[i, :, at : at + step] = gained
+            terms = gained * hidden[:, cols].astype(jnp.float32)
+            for c in range(0, step, LANES):
+                total = total + terms[:, c : c + LANES]
     proj[...] = jnp.sum(jnp.transpose(total), axis=0, keepdims=True)
+    for ref in before:
+        proj[...] += ref[...]
 
 
 def weight_grad_kernel(sources, inner, group_blocks, most, meta, own, *refs):
@@ -168,12 +170,9 @@
     rows = norms[0].shape[1]
     parts = width // LANES
     whole[:tokens, :] = own[...]
-    for (member, lot, share), piece in zip(sources, pieces):
-        offset = member(meta[2]) * share
-        for i, r in enumerate(lot):
-            for c in range(parts):
-                target = pl.ds(pl.multiple_of(r * tokens + offset, share), share)
-                whole[target, c * LANES : (c + 1) * LANES] = piece[i, c * share : (c + 1) * share, :]
+    for place, piece in zip(sources, pieces):
+        first = pl.multiple_of(place(meta[2]) * tokens, tokens)
+        whole[pl.ds(first, tokens), :] = piece[...]
     step = 256 if rows % 256 == 0 else rows
     for at in range(0, rows, step):
         total = None
@@ -231,36 +230,18 @@
             compiler_params=pltpu.CompilerParams(vmem_limit_bytes=megabytes << 20),
         )(*scalars, *arrays)
 
-    share = tokens // halves
-    split = halves > 1 and tokens % halves == 0 and share % 16 == 0
-    share = share if split else tokens
-    head = share * parts
-    hbm = pl.BlockSpec(memory_space=pltpu.HBM)
-    parcel, square = pl.pallas_call(
-        functools.partial(load_kernel, share),
-        name="load",
-        out_shape=(
-            jax.ShapeDtypeStruct((head + most, LANES), jnp.bfloat16),
-            jax.ShapeDtypeStruct((1, tokens), jnp.float32),
-        ),
-        in_specs=[hbm] * 3,
-        out_specs=(vmem, vmem),
-        scratch_shapes=[
-            pltpu.VMEM((tokens, features), jnp.bfloat16),
-            pltpu.SemaphoreType.DMA((parts + 2,)),
-        ],
-        compiler_params=pltpu.CompilerParams(vmem_limit_bytes=60 << 20),
-    )(weight_blocks.reshape(most, LANES), key_grad, hidden_in)
+    own_blocks = weight_blocks.reshape(most, LANES)
     hidden, gain = hidden_in, norm_gain[None, :]
-    found = gather_relatives(parcel, "gx", outer)
+    hfloat = hidden_in.astype(jnp.float32)
+    square = jnp.sum(hfloat * hfloat, axis=1)[None, :]
+    found = gather_relatives(own_blocks, "gx", outer)
     order = list(found)
     lots = [lot for lot in (order[:1], order[1:-1], order[-1:]) if lot]
     lots = lots if outer > 1 else [order]
 
     pieces, names = [], []
-    for lot_index, lot in enumerate(lots):
-        own = weight_blocks.reshape(1, most, LANES)
-        spread = {0: jnp.stack([found[r][head:] for r in lot]) if lot_index else own}
+    for lot in lots:
+        spread = {0: jnp.stack([found[r] for r in lot])}
         bit = inner // 2
         while bit:
             for r in list(spread):
@@ -269,10 +250,6 @@
         pieces += list(spread.values())
         names += [(r, s) for s in spread for r in lot]
 
-    def owner_of(i, j, index):
-        r, s = names[index]
-        return relative_index(outer, i, r) * inner + (j ^ s)
-
     squares = axis_terms(square, "gz", halves)
 
     starts = [i * group_blocks // parts for i in range(outer)]
@@ -292,39 +269,59 @@
     )
 
     sources, key_pieces = [], []
-    for r in order[1:]:
-        member = functools.partial(relative_index, halves, r=0) if split else (lambda i: 0)
-        sources.append((member, [r], share))
-        key_pieces.append(found[r][None])
-    for lot in [order[1:-1], order[-1:]] if split and outer > 1 else []:
-        stack = jnp.stack([found[r][:head] for r in lot])
+
+    def bring(place, x, axis, pairs):
+        sources.append(place)
+        key_pieces.append(lax.ppermute(x, axis, pairs))
+        return key_pieces[-1]
+
+    far = range(2, outer)
+    shared = power_of_two(outer) and power_of_two(halves) and len(far) == halves
+    for r in range(1, 2 if shared else outer):
+        bring(lambda g, r=r: r, key_grad, "gx", relative(outer, r))
+    if shared:
+        pairs = [
+            (i * halves + g, (i ^ far[g]) * halves + g) for i in range(outer) for g in range(halves)
+        ]
+        mine = bring(lambda g: 2 + g, key_grad, ("gx", "gz"), pairs)
         for s in range(1, halves):
-            sources.append((functools.partial(relative_index, halves, r=s), lot, share))
-            key_pieces.append(lax.ppermute(stack, "gz", relative(halves, s)))
+            bring(lambda g, s=s: 2 + (g ^ s), mine, "gz", relative(halves, s))
     norms = [windows[0]]
     for r in range(1, outer):
         norms.append(lax.ppermute(windows[r], "gx", relative(outer, r)))
 
-    scaled, proj = call(
-        functools.partial(input_grad_kernel, owner_of, most),
-        (
-            jax.ShapeDtypeStruct((tokens, features), jnp.float32),
-            jax.ShapeDtypeStruct((1, tokens), jnp.float32),
-        ),
-        [meta],
-        [key_grad, normed_grad, hidden, gain, *pieces],
-        [
-            pltpu.VMEM((ceil_to(blocks + most, 8), LANES), jnp.float32),
-            pltpu.SMEM((owners,), jnp.int32),
-        ],
-        megabytes=8,
-    )
+    if group_blocks % parts == 0 and rows * outer == features and rows % LANES == 0 and len(lots) > 2:
+        count = sum(r != order[-1] for r, _ in names)
+        calls = [order[:-1], order[-1:]]
+        parts_of = [(names[:count], pieces[:-inner]), (names[count:], pieces[-inner:])]
+    else:
+        calls, parts_of = [None], [(names, pieces)]
+    scaled, before = [], []
+    for relatives, (own_names, own_pieces) in zip(calls, parts_of):
+        shape = (1, tokens, features) if relatives is None else (len(relatives), tokens, rows)
+        span = shape[0] * shape[2] * parts
+        result, proj = call(
+            functools.partial(input_grad_kernel, own_names, relatives, outer, inner, most),
+            (
+                jax.ShapeDtypeStruct(shape, jnp.float32),
+                jax.ShapeDtypeStruct((1, tokens), jnp.float32),
+            ),
+            [meta],
+            [key_grad, normed_grad, hidden, gain, *before, *own_pieces],
+            [
+                pltpu.VMEM((ceil_to(span + most, 8), LANES), jnp.float32),
+                pltpu.SMEM((owners,), jnp.int32),
+            ],
+            megabytes=8,
+        )
+        scaled.append(result)
+        before = [proj]
     projs = axis_terms(proj, "gz", halves)
     hidden_grad = call(
-        functools.partial(finish_kernel, model_width),
+        functools.partial(finish_kernel, calls, outer, model_width),
         jax.ShapeDtypeStruct((tokens, features), jnp.bfloat16),
-        [],
-        [*squares, *projs, scaled, hidden],
+        [meta],
+        [*squares, *projs, hidden, *scaled],
     )
 
     half = jax.ShapeDtypeStruct((inner // 2, most, LANES), jnp.float32)

time: 59.8 us -> 63 us (1.054)
  waiting for transfers between devices: 26.1 us -> 28.9 us
  other arithmetic: 0.9 us -> 2.12 us
    ppermute x3, waiting for transfers between devices: 0.01 us -> 6.07 us  [shards(): norms.append(lax.ppermute(windows[r], 'gx', relative(outer, r)))]
    ppermute x2 -> x3, starting transfers between devices: 3.17 us -> 7.11 us  [bring(): key_pieces.append(lax.ppermute(x, axis, pairs))]
    ppermute x3, waiting for transfers between devices: 10.6 us -> 6.78 us  [gather_relatives(): known[r ^ basis] = lax.ppermute(known[r], axis, relative(n, basis))]
    ppermute x3, starting transfers between devices: 6.19 us -> 3.41 us  [gather_relatives(): known[r ^ basis] = lax.ppermute(known[r], axis, relative(n, basis))]
    pallas_call x1 -> x0, Pallas kernels: 2.03 us -> none  [shards(): pl.pallas_call(functools.partial(load_kernel, share), name='load', out_sh...]
    ppermute x9, waiting for transfers between devices: 11 us -> 12.6 us  [shards(): spread[r ^ bit] = lax.ppermute(spread[r], 'gy', relative(inner, bit))]
    pallas_call x4 -> x5, Pallas kernels: 5.86 us -> 7.32 us  [call(): pl.pallas_call(kernel, out_shape=out_shape, in_specs=[smem] * len(scalars...]
    ppermute x9, starting transfers between devices: 5.55 us -> 4.32 us  [shards(): spread[r ^ bit] = lax.ppermute(spread[r], 'gy', relative(inner, bit))]
  transfers between devices with their start and end apart: 21 -> 22, of which waited for: 8 -> 7; matrix products, arithmetic and copies ran while one was open for 0% -> 2% of each run, Pallas kernels for 10% -> 9%
where the time goes in v5:
time: 63 us; the launch traced here: 62.8 us
  waiting for transfers between devices  28.9 us (46%)
  starting transfers between devices  23.1 us (37%)
  Pallas kernels  7.32 us (12%)
  other arithmetic  2.12 us (3%)
  between operations  0.76 us (1%)
  local copies, waits for them, and re-layouts  0.69 us (1%)
    ppermute x9, waiting for transfers between devices, shards(): spread[r ^ bit] = lax.ppermute(spread[r], 'gy', relative(inner, bit))  12.6 us
    pallas_call x5, Pallas kernels, call(): pl.pallas_call(kernel, out_shape=out_shape, in_specs=[smem] * len(scalars...  7.32 us
    ppermute x3, starting transfers between devices, bring(): key_pieces.append(lax.ppermute(x, axis, pairs))  7.11 us
    ppermute x3, waiting for transfers between devices, gather_relatives(): known[r ^ basis] = lax.ppermute(known[r], axis, relative(n, basis))  6.78 us
    ppermute x3, waiting for transfers between devices, shards(): norms.append(lax.ppermute(windows[r], 'gx', relative(outer, r)))  6.07 us
    ppermute x3, starting transfers between devices, shards(): norms.append(lax.ppermute(windows[r], 'gx', relative(outer, r)))  4.45 us
    ppermute x9, starting transfers between devices, shards(): spread[r ^ bit] = lax.ppermute(spread[r], 'gy', relative(inner, bit))  4.32 us
    ppermute x2, waiting for transfers between devices, axis_terms(): lax.ppermute(x, axis, relative(n, bit))  3.43 us
  transfers between devices with their start and end apart: 22, of which 7 were waited for; matrix products, arithmetic and copies ran while one was open for 2% of the time, Pallas kernels for 9%

profile of v5, /device:TPU:0, one launch (start us, length us, event | category | flops | bytes accessed | tf_op | source)
XLA Modules:
  0.0 62.8 jit_solution(8319602519116330871)
XLA Ops:
  0.6 3.1 %collective-permute-start.14 = (bf16[128,512]{1,0:T(8,128)(2,1)}, bf16[128,512]{1,0:T(8,128)(2,1)S(1)}, u32[]{:S(2)}, u32[]{:S(2)}) collective-permute-start(bf16[128,512]{1,0:T(8,128)(2,1)} %own.1), channel_id=1, source_target_pairs={{0,8},{8,0},{16,24},{24,16},{1,9},{9,1},{17,25},{25,17},{2,10},{10... | collective-permute-start | bytes 393224 | tf_op jit(solution)/shard_map/ppermute | solution.py:275
  3.8 2.6 %collective-permute-start.15 = (bf16[128,512]{1,0:T(8,128)(2,1)}, bf16[128,512]{1,0:T(8,128)(2,1)S(1)}, u32[]{:S(2)}, u32[]{:S(2)}) collective-permute-start(bf16[128,512]{1,0:T(8,128)(2,1)} %own.1), channel_id=1, source_target_pairs={{0,16},{1,25},{8,24},{9,17},{16,0},{17,9},{24,8},{25,1},{2,18},{3,... | collective-permute-start | bytes 393224 | tf_op jit(solution)/shard_map/ppermute | solution.py:275
  6.3 1.2 %multiply_reduce_fusion = f32[128]{0:T(128)S(1)} fusion(bf16[128,2048]{1,0:T(8,128)(2,1)} %hidden.7), kind=kLoop, calls=%fused_computation | loop fusion | flops 786304 | bytes 524800 | tf_op jit(solution)/shard_map/reduce_sum | solution.py:236
  7.6 1.5 %collective-permute-start = (f32[1,128]{1,0:T(1,128)S(1)}, f32[1,128]{1,0:T(1,128)S(1)}, u32[]{:S(2)}, u32[]{:S(2)}) collective-permute-start(f32[1,128]{1,0:T(1,128)S(1)} %bitcast.24), channel_id=1, source_target_pairs={{0,1},{1,0},{2,3},{3,2},{4,5},{5,4},{6,7},{7,6},{8,9},{9,8},{10,11... | collective-permute-start | bytes 1544 | tf_op jit(solution)/shard_map/ppermute | solution.py:54
  9.8 1.4 %collective-permute-done.other = f32[1,128]{1,0:T(1,128)S(1)} collective-permute-done((f32[1,128]{1,0:T(1,128)S(1)}, f32[1,128]{1,0:T(1,128)S(1)}, u32[]{:S(2)}, u32[]{:S(2)}) %collective-permute-start) | collective-permute-done | bytes 544 | tf_op jit(solution)/shard_map/ppermute | solution.py:54
  11.2 0.8 %shard_map.80 = (bf16[128,512]{1,0:T(8,128)(2,1)S(1)}, bf16[128,512]{1,0:T(8,128)(2,1)S(1)}, bf16[128,512]{1,0:T(8,128)(2,1)S(1)}, bf16[128,512]{1,0:T(8,128)(2,1)S(1)}) custom-call(s32[19]{0:T(128)S(1)} %pad_add_fusion.meta, f32[1,128]{1,0:T(1,128)S(1)} %bitcast.25, f32[1,128]{1,0:T(1,128)S(1)} %collective-permute-done.other, ...), custom_call_target="tpu_custom_call" | custom-call | tf_op jit(solution)/shard_map/pallas_call | solution.py:224
  12.5 0.8 %collective-permute-start.18 = (bf16[128,512]{1,0:T(8,128)(2,1)S(1)}, bf16[128,512]{1,0:T(8,128)(2,1)S(1)}, u32[]{:S(2)}, u32[]{:S(2)}) collective-permute-start(bf16[128,512]{1,0:T(8,128)(2,1)S(1)} %get-tuple-element.18), channel_id=1, source_target_pairs={{0,16},{8,24},{16,0},{24,8},{1,17},{9,25},{17,1},{25,9},{2,18},{10... | collective-permute-start | bytes 393224 | tf_op jit(solution)/shard_map/ppermute | solution.py:291
  13.4 3.1 %collective-permute-start.19 = (bf16[128,512]{1,0:T(8,128)(2,1)S(1)}, bf16[128,512]{1,0:T(8,128)(2,1)S(1)}, u32[]{:S(2)}, u32[]{:S(2)}) collective-permute-start(bf16[128,512]{1,0:T(8,128)(2,1)S(1)} %get-tuple-element.19), channel_id=1, source_target_pairs={{0,24},{8,16},{16,8},{24,0},{1,25},{9,17},{17,9},{25,1},{2,26},{10... | collective-permute-start | bytes 393224 | tf_op jit(solution)/shard_map/ppermute | solution.py:291
  16.5 1.4 %collective-permute-start.16 = (bf16[128,512]{1,0:T(8,128)(2,1)S(1)}, bf16[128,512]{1,0:T(8,128)(2,1)S(1)}, u32[]{:S(2)}, u32[]{:S(2)}) collective-permute-start(bf16[128,512]{1,0:T(8,128)(2,1)S(1)} %collective-permute-done.15.refs_1_), channel_id=1, source_target_pairs={{0,1},{1,0},{2,3},{3,2},{4,5},{5,4},{6,7},{7,6},{8,9},{9,8},{10,11... | collective-permute-start | bytes 393224 | tf_op jit(solution)/shard_map/ppermute | solution.py:275
  17.9 6.1 %collective-permute-done.18.refs_5_ = bf16[128,512]{1,0:T(8,128)(2,1)S(1)} collective-permute-done((bf16[128,512]{1,0:T(8,128)(2,1)S(1)}, bf16[128,512]{1,0:T(8,128)(2,1)S(1)}, u32[]{:S(2)}, u32[]{:S(2)}) %collective-permute-start.18) | collective-permute-done | bytes 131104 | tf_op jit(solution)/shard_map/ppermute | solution.py:291
  24.0 1.5 %shard_map.81 = (f32[2,520,128]{2,1,0:T(8,128)S(1)}, f32[2,520,128]{2,1,0:T(8,128)S(1)}) custom-call(s32[19]{0:T(128)S(1)} %pad_add_fusion.meta, bf16[128,512]{1,0:T(8,128)(2,1)S(1)} %copy-done.2, bf16[128,512]{1,0:T(8,128)(2,1)S(1)} %collective-permute-done.14.refs_0_, bf16[128,512]{1,0:T(8,128)(2,1)S(1)} %collective-permute-done.15.refs_1_, ...), custom_call_target="tpu_custom_call" | custom-call | tf_op jit(solution)/shard_map/pallas_call | solution.py:224
  25.5 2.0 %collective-permute-start.5 = (bf16[520,128]{1,0:T(8,128)(2,1)S(1)}, bf16[520,128]{1,0:T(8,128)(2,1)S(1)}, u32[]{:S(2)}, u32[]{:S(2)}) collective-permute-start(bf16[520,128]{1,0:T(8,128)(2,1)S(1)} %bitcast.13), channel_id=1, source_target_pairs={{0,8},{8,0},{16,24},{24,16},{1,9},{9,1},{17,25},{25,17},{2,10},{10... | collective-permute-start | bytes 399368 | tf_op jit(solution)/shard_map/ppermute | solution.py:41
  27.6 1.4 %collective-permute-start.4 = (bf16[520,128]{1,0:T(8,128)(2,1)S(1)}, bf16[520,128]{1,0:T(8,128)(2,1)S(1)}, u32[]{:S(2)}, u32[]{:S(2)}) collective-permute-start(bf16[520,128]{1,0:T(8,128)(2,1)S(1)} %bitcast.14), channel_id=1, source_target_pairs={{0,24},{8,16},{16,8},{24,0},{1,25},{9,17},{17,9},{25,1},{2,26},{10... | collective-permute-start | bytes 399368 | tf_op jit(solution)/shard_map/ppermute | solution.py:41
  28.9 2.7 %collective-permute-done.5 = bf16[520,128]{1,0:T(8,128)(2,1)S(1)} collective-permute-done((bf16[520,128]{1,0:T(8,128)(2,1)S(1)}, bf16[520,128]{1,0:T(8,128)(2,1)S(1)}, u32[]{:S(2)}, u32[]{:S(2)}) %collective-permute-start.5) | collective-permute-done | bytes 133152 | tf_op jit(solution)/shard_map/ppermute | solution.py:41
  31.7 4.0 %collective-permute-done.4 = bf16[520,128]{1,0:T(8,128)(2,1)S(1)} collective-permute-done((bf16[520,128]{1,0:T(8,128)(2,1)S(1)}, bf16[520,128]{1,0:T(8,128)(2,1)S(1)}, u32[]{:S(2)}, u32[]{:S(2)}) %collective-permute-start.4) | collective-permute-done | bytes 133152 | tf_op jit(solution)/shard_map/ppermute | solution.py:41
  35.8 1.5 %collective-permute-start.6 = (bf16[2,520,128]{2,1,0:T(8,128)(2,1)S(1)}, bf16[2,520,128]{2,1,0:T(8,128)(2,1)S(1)}, u32[]{:S(2)}, u32[]{:S(2)}) collective-permute-start(bf16[2,520,128]{2,1,0:T(8,128)(2,1)S(1)} %pad_maximum_fusion.refs_4_), channel_id=1, source_target_pairs={{0,4},{2,6},{4,0},{6,2},{1,5},{3,7},{5,1},{7,3},{8,12},{10,14},{12... | collective-permute-start | bytes 798728 | tf_op jit(solution)/shard_map/ppermute | solution.py:248
  37.9 8.6 %collective-permute-done.1.refs_1_ = bf16[1,520,128]{2,1,0:T(8,128)(2,1)S(1)} collective-permute-done((bf16[1,520,128]{2,1,0:T(8,128)(2,1)S(1)}, bf16[1,520,128]{2,1,0:T(8,128)(2,1)S(1)}, u32[]{:S(2)}, u32[]{:S(2)}) %collective-permute-start.1) | collective-permute-done | bytes 133152 | tf_op jit(solution)/shard_map/ppermute | solution.py:248
  47.0 1.5 %collective-permute-start.10 = (bf16[1,520,128]{2,1,0:T(8,128)(2,1)S(1)}, bf16[1,520,128]{2,1,0:T(8,128)(2,1)S(1)}, u32[]{:S(2)}, u32[]{:S(2)}) collective-permute-start(bf16[1,520,128]{2,1,0:T(8,128)(2,1)S(1)} %bitcast.18), channel_id=1, source_target_pairs={{0,4},{2,6},{4,0},{6,2},{1,5},{3,7},{5,1},{7,3},{8,12},{10,14},{12... | collective-permute-start | bytes 399368 | tf_op jit(solution)/shard_map/ppermute | solution.py:248
  49.4 3.9 %collective-permute-done.10.refs_2_ = bf16[1,520,128]{2,1,0:T(8,128)(2,1)S(1)} collective-permute-done((bf16[1,520,128]{2,1,0:T(8,128)(2,1)S(1)}, bf16[1,520,128]{2,1,0:T(8,128)(2,1)S(1)}, u32[]{:S(2)}, u32[]{:S(2)}) %collective-permute-start.10) | collective-permute-done | bytes 133152 | tf_op jit(solution)/shard_map/ppermute | solution.py:248
  53.4 2.1 %shard_map.77 = (f32[3,128,512]{2,1,0:T(8,128)S(1)}, f32[1,128]{1,0:T(1,128)S(1)}) custom-call(s32[19]{0:T(128)S(1)} %pad_add_fusion.meta, bf16[128,512]{1,0:T(8,128)(2,1)S(1)} %copy-done.2, bf16[128,2048]{1,0:T(8,128)(2,1)S(1)} %copy-done.1, bf16[128,2048]{1,0:T(8,128)(2,1)S(1)} %copy-done, f32[1,2048]{1,0:T(1,128)S(1)} %bitcast.22, ...), custom_call_target="tpu_custom_call" | custom-call | tf_op jit(solution)/shard_map/pallas_call | solution.py:224
  55.5 1.3 %shard_map.78 = (f32[1,128,512]{2,1,0:T(8,128)S(1)}, f32[1,128]{1,0:T(1,128)S(1)}) custom-call(s32[19]{0:T(128)S(1)} %pad_add_fusion.meta, bf16[128,512]{1,0:T(8,128)(2,1)S(1)} %copy-done.2, bf16[128,2048]{1,0:T(8,128)(2,1)S(1)} %copy-done.1, bf16[128,2048]{1,0:T(8,128)(2,1)S(1)} %copy-done, f32[1,2048]{1,0:T(1,128)S(1)} %bitcast.23, ...), custom_call_target="tpu_custom_call" | custom-call | tf_op jit(solution)/shard_map/pallas_call | solution.py:224
  56.8 1.6 %collective-permute-start.13 = (f32[1,128]{1,0:T(1,128)S(1)}, f32[1,128]{1,0:T(1,128)S(1)}, u32[]{:S(2)}, u32[]{:S(2)}) collective-permute-start(f32[1,128]{1,0:T(1,128)S(1)} %get-tuple-element.13.proj), channel_id=1, source_target_pairs={{0,1},{1,0},{2,3},{3,2},{4,5},{5,4},{6,7},{7,6},{8,9},{9,8},{10,11... | collective-permute-start | bytes 1544 | tf_op jit(solution)/shard_map/ppermute | solution.py:54
  58.4 2.0 %collective-permute-done.13.proj_other = f32[1,128]{1,0:T(1,128)S(1)} collective-permute-done((f32[1,128]{1,0:T(1,128)S(1)}, f32[1,128]{1,0:T(1,128)S(1)}, u32[]{:S(2)}, u32[]{:S(2)}) %collective-permute-start.13) | collective-permute-done | bytes 544 | tf_op jit(solution)/shard_map/ppermute | solution.py:54
  60.4 1.7 %shard_map.79 = bf16[128,2048]{1,0:T(8,128)(2,1)} custom-call(s32[19]{0:T(128)S(1)} %pad_add_fusion.meta, f32[1,128]{1,0:T(1,128)S(1)} %bitcast.26, f32[1,128]{1,0:T(1,128)S(1)} %collective-permute-done.other, f32[1,128]{1,0:T(1,128)S(1)} %get-tuple-element.13.proj, f32[1,128]{1,0:T(1,128)S(1)} %collective-permute-done.13.proj_other, ...), custom_call_target="tpu_custom_call" | custom-call | tf_op jit(solution)/shard_map/pallas_call | solution.py:224
  (42 shorter events, 4.1 us)
Async XLA Ops:
  0.6 17.2 %collective-permute-start.14 = (bf16[128,512]{1,0:T(8,128)(2,1)}, bf16[128,512]{1,0:T(8,128)(2,1)S(1)}, u32[]{:S(2)}, u32[]{:S(2)}) collective-permute-start(bf16[128,512]{1,0:T(8,128)(2,1)} %own.1), channel_id=1, source_target_pairs={{0,8},{8,0},{16,24},{24,16},{1,9},{9,1},{17,25},{25,17},{2,10},{10... | collective-permute-start | bytes 393224 | tf_op jit(solution)/shard_map/ppermute | solution.py:275
  3.8 12.7 %collective-permute-start.15 = (bf16[128,512]{1,0:T(8,128)(2,1)}, bf16[128,512]{1,0:T(8,128)(2,1)S(1)}, u32[]{:S(2)}, u32[]{:S(2)}) collective-permute-start(bf16[128,512]{1,0:T(8,128)(2,1)} %own.1), channel_id=1, source_target_pairs={{0,16},{1,25},{8,24},{9,17},{16,0},{17,9},{24,8},{25,1},{2,18},{3,... | collective-permute-start | bytes 393224 | tf_op jit(solution)/shard_map/ppermute | solution.py:275
  7.6 3.6 %collective-permute-start = (f32[1,128]{1,0:T(1,128)S(1)}, f32[1,128]{1,0:T(1,128)S(1)}, u32[]{:S(2)}, u32[]{:S(2)}) collective-permute-start(f32[1,128]{1,0:T(1,128)S(1)} %bitcast.24), channel_id=1, source_target_pairs={{0,1},{1,0},{2,3},{3,2},{4,5},{5,4},{6,7},{7,6},{8,9},{9,8},{10,11... | collective-permute-start | bytes 1544 | tf_op jit(solution)/shard_map/ppermute | solution.py:54
  11.2 12.8 %copy-start.2 = (bf16[128,512]{1,0:T(8,128)(2,1)S(1)}, bf16[128,512]{1,0:T(8,128)(2,1)}, u32[]{:S(2)}) copy-start(bf16[128,512]{1,0:T(8,128)(2,1)} %own.1) | copy-start | bytes 393220
  12.0 5.9 %collective-permute-start.17 = (bf16[128,512]{1,0:T(8,128)(2,1)S(1)}, bf16[128,512]{1,0:T(8,128)(2,1)S(1)}, u32[]{:S(2)}, u32[]{:S(2)}) collective-permute-start(bf16[128,512]{1,0:T(8,128)(2,1)S(1)} %get-tuple-element.17), channel_id=1, source_target_pairs={{0,8},{8,0},{16,24},{24,16},{1,9},{9,1},{17,25},{25,17},{2,10},{10... | collective-permute-start | bytes 393224 | tf_op jit(solution)/shard_map/ppermute | solution.py:291
  12.5 11.4 %collective-permute-start.18 = (bf16[128,512]{1,0:T(8,128)(2,1)S(1)}, bf16[128,512]{1,0:T(8,128)(2,1)S(1)}, u32[]{:S(2)}, u32[]{:S(2)}) collective-permute-start(bf16[128,512]{1,0:T(8,128)(2,1)S(1)} %get-tuple-element.18), channel_id=1, source_target_pairs={{0,16},{8,24},{16,0},{24,8},{1,17},{9,25},{17,1},{25,9},{2,18},{10... | collective-permute-start | bytes 393224 | tf_op jit(solution)/shard_map/ppermute | solution.py:291
  13.4 10.6 %collective-permute-start.19 = (bf16[128,512]{1,0:T(8,128)(2,1)S(1)}, bf16[128,512]{1,0:T(8,128)(2,1)S(1)}, u32[]{:S(2)}, u32[]{:S(2)}) collective-permute-start(bf16[128,512]{1,0:T(8,128)(2,1)S(1)} %get-tuple-element.19), channel_id=1, source_target_pairs={{0,24},{8,16},{16,8},{24,0},{1,25},{9,17},{17,9},{25,1},{2,26},{10... | collective-permute-start | bytes 393224 | tf_op jit(solution)/shard_map/ppermute | solution.py:291
  16.5 7.5 %collective-permute-start.16 = (bf16[128,512]{1,0:T(8,128)(2,1)S(1)}, bf16[128,512]{1,0:T(8,128)(2,1)S(1)}, u32[]{:S(2)}, u32[]{:S(2)}) collective-permute-start(bf16[128,512]{1,0:T(8,128)(2,1)S(1)} %collective-permute-done.15.refs_1_), channel_id=1, source_target_pairs={{0,1},{1,0},{2,3},{3,2},{4,5},{5,4},{6,7},{7,6},{8,9},{9,8},{10,11... | collective-permute-start | bytes 393224 | tf_op jit(solution)/shard_map/ppermute | solution.py:275
  25.4 23.1 %collective-permute-start.20 = (f32[2,520,128]{2,1,0:T(8,128)S(1)}, f32[2,520,128]{2,1,0:T(8,128)S(1)}, u32[]{:S(2)}, u32[]{:S(2)}) collective-permute-start(f32[2,520,128]{2,1,0:T(8,128)S(1)} %get-tuple-element.21), channel_id=1, source_target_pairs={{0,2},{2,0},{4,6},{6,4},{1,3},{3,1},{5,7},{7,5},{8,10},{10,8},{12,... | collective-permute-start | bytes 1597448 | tf_op jit(solution)/shard_map/ppermute | solution.py:340
  25.5 6.2 %collective-permute-start.5 = (bf16[520,128]{1,0:T(8,128)(2,1)S(1)}, bf16[520,128]{1,0:T(8,128)(2,1)S(1)}, u32[]{:S(2)}, u32[]{:S(2)}) collective-permute-start(bf16[520,128]{1,0:T(8,128)(2,1)S(1)} %bitcast.13), channel_id=1, source_target_pairs={{0,8},{8,0},{16,24},{24,16},{1,9},{9,1},{17,25},{25,17},{2,10},{10... | collective-permute-start | bytes 399368 | tf_op jit(solution)/shard_map/ppermute | solution.py:41
  27.6 8.2 %collective-permute-start.4 = (bf16[520,128]{1,0:T(8,128)(2,1)S(1)}, bf16[520,128]{1,0:T(8,128)(2,1)S(1)}, u32[]{:S(2)}, u32[]{:S(2)}) collective-permute-start(bf16[520,128]{1,0:T(8,128)(2,1)S(1)} %bitcast.14), channel_id=1, source_target_pairs={{0,24},{8,16},{16,8},{24,0},{1,25},{9,17},{17,9},{25,1},{2,26},{10... | collective-permute-start | bytes 399368 | tf_op jit(solution)/shard_map/ppermute | solution.py:41
  35.7 17.6 %copy-start.1 = (bf16[128,2048]{1,0:T(8,128)(2,1)S(1)}, bf16[128,2048]{1,0:T(8,128)(2,1)}, u32[]{:S(2)}) copy-start(bf16[128,2048]{1,0:T(8,128)(2,1)} %grad.3) | copy-start | bytes 1572868
  35.8 11.2 %collective-permute-start.6 = (bf16[2,520,128]{2,1,0:T(8,128)(2,1)S(1)}, bf16[2,520,128]{2,1,0:T(8,128)(2,1)S(1)}, u32[]{:S(2)}, u32[]{:S(2)}) collective-permute-start(bf16[2,520,128]{2,1,0:T(8,128)(2,1)S(1)} %pad_maximum_fusion.refs_4_), channel_id=1, source_target_pairs={{0,4},{2,6},{4,0},{6,2},{1,5},{3,7},{5,1},{7,3},{8,12},{10,14},{12... | collective-permute-start | bytes 798728 | tf_op jit(solution)/shard_map/ppermute | solution.py:248
  37.3 9.2 %collective-permute-start.1 = (bf16[1,520,128]{2,1,0:T(8,128)(2,1)S(1)}, bf16[1,520,128]{2,1,0:T(8,128)(2,1)S(1)}, u32[]{:S(2)}, u32[]{:S(2)}) collective-permute-start(bf16[1,520,128]{2,1,0:T(8,128)(2,1)S(1)} %bitcast.15), channel_id=1, source_target_pairs={{0,4},{2,6},{4,0},{6,2},{1,5},{3,7},{5,1},{7,3},{8,12},{10,14},{12... | collective-permute-start | bytes 399368 | tf_op jit(solution)/shard_map/ppermute | solution.py:248
  37.9 8.6 %collective-permute-start.9 = (bf16[520,128]{1,0:T(8,128)(2,1)S(1)}, bf16[520,128]{1,0:T(8,128)(2,1)S(1)}, u32[]{:S(2)}, u32[]{:S(2)}) collective-permute-start(bf16[520,128]{1,0:T(8,128)(2,1)S(1)} %collective-permute-done.4), channel_id=1, source_target_pairs={{0,8},{8,0},{16,24},{24,16},{1,9},{9,1},{17,25},{25,17},{2,10},{10... | collective-permute-start | bytes 399368 | tf_op jit(solution)/shard_map/ppermute | solution.py:41
  37.9 10.7 %collective-permute-start.2 = (bf16[1,520,128]{2,1,0:T(8,128)(2,1)S(1)}, bf16[1,520,128]{2,1,0:T(8,128)(2,1)S(1)}, u32[]{:S(2)}, u32[]{:S(2)}) collective-permute-start(bf16[1,520,128]{2,1,0:T(8,128)(2,1)S(1)} %bitcast.16), channel_id=1, source_target_pairs={{0,2},{2,0},{4,6},{6,4},{1,3},{3,1},{5,7},{7,5},{8,10},{10,8},{12,... | collective-permute-start | bytes 399368 | tf_op jit(solution)/shard_map/ppermute | solution.py:248
  46.5 6.8 %collective-permute-start.7 = (bf16[2,520,128]{2,1,0:T(8,128)(2,1)S(1)}, bf16[2,520,128]{2,1,0:T(8,128)(2,1)S(1)}, u32[]{:S(2)}, u32[]{:S(2)}) collective-permute-start(bf16[2,520,128]{2,1,0:T(8,128)(2,1)S(1)} %pad_maximum_fusion.refs_4_), channel_id=1, source_target_pairs={{0,2},{2,0},{4,6},{6,4},{1,3},{3,1},{5,7},{7,5},{8,10},{10,8},{12,... | collective-permute-start | bytes 798728 | tf_op jit(solution)/shard_map/ppermute | solution.py:248
  46.5 2.7 %collective-permute-start.3 = (bf16[1,520,128]{2,1,0:T(8,128)(2,1)S(1)}, bf16[1,520,128]{2,1,0:T(8,128)(2,1)S(1)}, u32[]{:S(2)}, u32[]{:S(2)}) collective-permute-start(bf16[1,520,128]{2,1,0:T(8,128)(2,1)S(1)} %collective-permute-done.1.refs_1_), channel_id=1, source_target_pairs={{0,2},{2,0},{4,6},{6,4},{1,3},{3,1},{5,7},{7,5},{8,10},{10,8},{12,... | collective-permute-start | bytes 399368 | tf_op jit(solution)/shard_map/ppermute | solution.py:248
  47.0 6.3 %collective-permute-start.10 = (bf16[1,520,128]{2,1,0:T(8,128)(2,1)S(1)}, bf16[1,520,128]{2,1,0:T(8,128)(2,1)S(1)}, u32[]{:S(2)}, u32[]{:S(2)}) collective-permute-start(bf16[1,520,128]{2,1,0:T(8,128)(2,1)S(1)} %bitcast.18), channel_id=1, source_target_pairs={{0,4},{2,6},{4,0},{6,2},{1,5},{3,7},{5,1},{7,3},{8,12},{10,14},{12... | collective-permute-start | bytes 399368 | tf_op jit(solution)/shard_map/ppermute | solution.py:248
  48.5 4.8 %collective-permute-start.8 = (bf16[2,520,128]{2,1,0:T(8,128)(2,1)S(1)}, bf16[2,520,128]{2,1,0:T(8,128)(2,1)S(1)}, u32[]{:S(2)}, u32[]{:S(2)}) collective-permute-start(bf16[2,520,128]{2,1,0:T(8,128)(2,1)S(1)} %collective-permute-done.6.refs_5_), channel_id=1, source_target_pairs={{0,2},{2,0},{4,6},{6,4},{1,3},{3,1},{5,7},{7,5},{8,10},{10,8},{12,... | collective-permute-start | bytes 798728 | tf_op jit(solution)/shard_map/ppermute | solution.py:248
  48.5 13.5 %collective-permute-start.21 = (f32[1,520,128]{2,1,0:T(8,128)S(1)}, f32[1,520,128]{2,1,0:T(8,128)S(1)}, u32[]{:S(2)}, u32[]{:S(2)}) collective-permute-start(f32[1,520,128]{2,1,0:T(8,128)S(1)} %slice_add_fusion), channel_id=1, source_target_pairs={{0,4},{2,6},{4,0},{6,2},{1,5},{3,7},{5,1},{7,3},{8,12},{10,14},{12... | collective-permute-start | bytes 798728 | tf_op jit(solution)/shard_map/ppermute | solution.py:340
  49.2 6.3 %collective-permute-start.11 = (bf16[1,520,128]{2,1,0:T(8,128)(2,1)S(1)}, bf16[1,520,128]{2,1,0:T(8,128)(2,1)S(1)}, u32[]{:S(2)}, u32[]{:S(2)}) collective-permute-start(bf16[1,520,128]{2,1,0:T(8,128)(2,1)S(1)} %bitcast.19), channel_id=1, source_target_pairs={{0,2},{2,0},{4,6},{6,4},{1,3},{3,1},{5,7},{7,5},{8,10},{10,8},{12,... | collective-permute-start | bytes 399368 | tf_op jit(solution)/shard_map/ppermute | solution.py:248
  53.3 2.1 %collective-permute-start.12 = (bf16[1,520,128]{2,1,0:T(8,128)(2,1)S(1)}, bf16[1,520,128]{2,1,0:T(8,128)(2,1)S(1)}, u32[]{:S(2)}, u32[]{:S(2)}) collective-permute-start(bf16[1,520,128]{2,1,0:T(8,128)(2,1)S(1)} %collective-permute-done.10.refs_2_), channel_id=1, source_target_pairs={{0,2},{2,0},{4,6},{6,4},{1,3},{3,1},{5,7},{7,5},{8,10},{10,8},{12,... | collective-permute-start | bytes 399368 | tf_op jit(solution)/shard_map/ppermute | solution.py:248
  56.8 3.6 %collective-permute-start.13 = (f32[1,128]{1,0:T(1,128)S(1)}, f32[1,128]{1,0:T(1,128)S(1)}, u32[]{:S(2)}, u32[]{:S(2)}) collective-permute-start(f32[1,128]{1,0:T(1,128)S(1)} %get-tuple-element.13.proj), channel_id=1, source_target_pairs={{0,1},{1,0},{2,3},{3,2},{4,5},{5,4},{6,7},{7,6},{8,9},{9,8},{10,11... | collective-permute-start | bytes 1544 | tf_op jit(solution)/shard_map/ppermute | solution.py:54
  (4 other events, 15.0 us)
